TPU v7x, 32 devices: a whole 2x2x4 slice. The times are simulated.
32 devices in a mesh: clip: 4 (over x, core), seq: 2 (over y), head: 4 (over z).
Axes of the slice: x: 2, y: 2, z: 4, core: 2. Of those that a mesh axis runs over, the one named last changes fastest.
Arguments:
- inputs: bfloat16 [4, 1500, 768], P('clip', 'seq'), may hold values from -6 to 6
- gain_one: bfloat16 [768], P(('clip', 'seq')), may hold values from 0.25 to 1.75
- shift_one: bfloat16 [768], P(('clip', 'seq')), may hold values from -1.75 to 1.75
- w_query: bfloat16 [768, 768], P(('clip', 'seq'), 'head'), may hold values from -0.21875 to 0.21875
- b_query: bfloat16 [768], P('head'), may hold values from -3 to 3
- w_key: bfloat16 [768, 768], P(('clip', 'seq'), 'head'), may hold values from -0.21875 to 0.21875
- w_value: bfloat16 [768, 768], P(('clip', 'seq'), 'head'), may hold values from -0.21875 to 0.21875
- b_value: bfloat16 [768], P('head'), may hold values from -0.3125 to 0.3125
- w_out: bfloat16 [768, 768], P('head', ('clip', 'seq')), may hold values from -3.5 to 3.5
- b_out: bfloat16 [768], P(('clip', 'seq')), may hold values from -3 to 3
- gain_two: bfloat16 [768], P(('clip', 'seq')), may hold values from 0.25 to 1.75
- shift_two: bfloat16 [768], P(('clip', 'seq')), may hold values from -1.75 to 1.75
- w_fc_one: bfloat16 [768, 3072], P(('clip', 'seq'), 'head'), may hold values from -0.21875 to 0.21875
- b_fc_one: bfloat16 [3072], P('head'), may hold values from -3 to 3
- w_fc_two: bfloat16 [3072, 768], P('head', ('clip', 'seq')), may hold values from -0.3125 to 0.3125
- b_fc_two: bfloat16 [768], P(('clip', 'seq')), may hold values from -3 to 3
- cotangent: bfloat16 [4, 1500, 768], P('clip', 'seq'), may hold values from -6 to 6
Outputs:
- outputs: bfloat16 [4, 1500, 768], P('clip', 'seq')
- input_gradient: float32 [4, 1500, 768], P('clip', 'seq')
- first_gain_gradient: float32 [768], P(('clip', 'seq'))
- grad_shift_one: float32 [768], P(('clip', 'seq'))
- grad_w_query: float32 [768, 768], P(('clip', 'seq'), 'head')
- grad_b_query: float32 [768], P('head')
- grad_w_key: float32 [768, 768], P(('clip', 'seq'), 'head')
- grad_w_value: float32 [768, 768], P(('clip', 'seq'), 'head')
- grad_b_value: float32 [768], P('head')
- grad_w_out: float32 [768, 768], P('head', ('clip', 'seq'))
- grad_b_out: float32 [768], P(('clip', 'seq'))
- second_gain_gradient: float32 [768], P(('clip', 'seq'))
- grad_shift_two: float32 [768], P(('clip', 'seq'))
- grad_w_fc_one: float32 [768, 3072], P(('clip', 'seq'), 'head')
- grad_b_fc_one: float32 [3072], P('head')
- grad_w_fc_two: float32 [3072, 768], P('head', ('clip', 'seq'))
- grad_b_fc_two: float32 [768], P(('clip', 'seq'))
All inputs are finite; a program needn't handle non-finite values.
Results may differ from a plain program's by a relative error of at most 0.012.
Values may be sent and summed in bfloat16 or wider, within the bound.
A program may use at most 128 MiB of HBM per device.

v0:
```python
from functools import partial

import jax
import jax.numpy as jnp
from jax import lax
from jax.sharding import PartitionSpec as P

HEAD_DIM = 64


eps = 1e-05


def layer_norm_forward(values, norm_gain, norm_shift):
    row_mean = jnp.mean(values, axis=-1, keepdims=True)
    centered_values = values - row_mean
    spread = jnp.mean(centered_values * centered_values, axis=-1, keepdims=True)
    inverse_deviation = lax.rsqrt(spread + eps)
    standardized = centered_values * inverse_deviation
    return (standardized * norm_gain + norm_shift, standardized, inverse_deviation)


def layer_norm_backward(output_gradient, standardized, inverse_deviation, norm_gain):
    scaled_rows = output_gradient * norm_gain
    first_row_mean = jnp.mean(scaled_rows, axis=-1, keepdims=True)
    second_row_mean = jnp.mean(scaled_rows * standardized, axis=-1, keepdims=True)
    return inverse_deviation * (scaled_rows - first_row_mean - standardized * second_row_mean)


def fetch_weights(
    gain_one,
    shift_one,
    w_query,
    w_key,
    w_value,
    b_out,
    gain_two,
    shift_two,
    w_fc_one,
    b_fc_two,
    w_out,
    w_fc_two,
):
    rows = (
        lax.all_gather(gain_one, ("clip", "seq"), axis=0, tiled=True),
        lax.all_gather(shift_one, ("clip", "seq"), axis=0, tiled=True),
        lax.all_gather(w_query, ("clip", "seq"), axis=0, tiled=True),
        lax.all_gather(w_key, ("clip", "seq"), axis=0, tiled=True),
        lax.all_gather(w_value, ("clip", "seq"), axis=0, tiled=True),
        lax.all_gather(b_out, ("clip", "seq"), axis=0, tiled=True),
        lax.all_gather(gain_two, ("clip", "seq"), axis=0, tiled=True),
        lax.all_gather(shift_two, ("clip", "seq"), axis=0, tiled=True),
        lax.all_gather(w_fc_one, ("clip", "seq"), axis=0, tiled=True),
        lax.all_gather(b_fc_two, ("clip", "seq"), axis=0, tiled=True),
    )
    columns = (
        lax.all_gather(w_out, ("clip", "seq"), axis=1, tiled=True),
        lax.all_gather(w_fc_two, ("clip", "seq"), axis=1, tiled=True),
    )
    return (rows, columns)


def head_total(partial_sum):
    return lax.psum(partial_sum, "head")


def on_device(
    inputs,
    gain_one,
    shift_one,
    w_query,
    b_query,
    w_key,
    w_value,
    b_value,
    w_out,
    b_out,
    gain_two,
    shift_two,
    w_fc_one,
    b_fc_one,
    w_fc_two,
    b_fc_two,
    cotangent,
):
    clips, frames, width = inputs.shape
    local = w_query.shape[1]
    heads = local // HEAD_DIM
    scale = HEAD_DIM ** (-0.5)
    gathered_rows = jnp.float32
    count = clips * frames
    rows, columns = fetch_weights(
        gain_one,
        shift_one,
        w_query,
        w_key,
        w_value,
        b_out,
        gain_two,
        shift_two,
        w_fc_one,
        b_fc_two,
        w_out,
        w_fc_two,
    )
    (
        full_gain_one,
        gathered_first_shift,
        full_query,
        full_key,
        full_value,
        full_b_out,
        full_gain_two,
        gathered_second_shift,
        full_fc_one,
        full_b_fc_two,
    ) = rows
    full_out, full_fc_two = columns
    token_rows = inputs.astype(gathered_rows).reshape(count, width)
    first_norm_gain = full_gain_one.astype(gathered_rows)
    second_norm_gain = full_gain_two.astype(gathered_rows)
    normalized_gathered, first_standardized, first_inverse_deviation = layer_norm_forward(
        token_rows, first_norm_gain, gathered_first_shift.astype(gathered_rows)
    )
    normed_one = normalized_gathered.astype(jnp.bfloat16)
    query = (
        jnp.dot(normed_one, full_query, preferred_element_type=gathered_rows)
        + b_query.astype(gathered_rows)
    ).astype(jnp.bfloat16)
    key = jnp.dot(normed_one, full_key, preferred_element_type=gathered_rows).astype(jnp.bfloat16)
    value = (
        jnp.dot(normed_one, full_value, preferred_element_type=gathered_rows)
        + b_value.astype(gathered_rows)
    ).astype(jnp.bfloat16)
    query_clips = query.reshape(clips, frames, local)
    key_all, value_all = (
        lax.all_gather(key.reshape(clips, frames, local), "seq", axis=1, tiled=True),
        lax.all_gather(value.reshape(clips, frames, local), "seq", axis=1, tiled=True),
    )

    def attend(block):
        query_block, key_block, value_block = block
        query_heads = query_block.reshape(frames, heads, HEAD_DIM)
        key_heads = key_block.reshape(-1, heads, HEAD_DIM)
        value_heads = value_block.reshape(-1, heads, HEAD_DIM)
        scores = (
            jnp.einsum("qhd,khd->hqk", query_heads, key_heads, preferred_element_type=gathered_rows)
            * scale
        )
        top = jnp.max(scores, axis=-1, keepdims=True)
        expo = jnp.exp(scores - top)
        total = jnp.sum(expo, axis=-1, keepdims=True)
        probs = (expo / total).astype(jnp.bfloat16)
        result = jnp.einsum(
            "hqk,khd->qhd", probs, value_heads, preferred_element_type=gathered_rows
        )
        return (result.reshape(frames, local).astype(jnp.bfloat16), (top + jnp.log(total))[..., 0])

    attended_clips, log_totals = lax.map(attend, (query_clips, key_all, value_all))
    attended = attended_clips.reshape(count, local)
    attn_terms = jnp.dot(attended, full_out, preferred_element_type=gathered_rows)
    middle_state = token_rows + head_total(attn_terms) + full_b_out.astype(gathered_rows)
    normalized_middle, second_standardized, second_inverse_deviation = layer_norm_forward(
        middle_state, second_norm_gain, gathered_second_shift.astype(gathered_rows)
    )
    normed_two = normalized_middle.astype(jnp.bfloat16)
    pre = jnp.dot(normed_two, full_fc_one, preferred_element_type=gathered_rows) + b_fc_one.astype(
        gathered_rows
    )
    act = jax.nn.gelu(pre, approximate=False).astype(jnp.bfloat16)
    ffn_terms = jnp.dot(act, full_fc_two, preferred_element_type=gathered_rows)
    outputs = (middle_state + head_total(ffn_terms) + full_b_fc_two.astype(gathered_rows)).astype(
        jnp.bfloat16
    )
    rows, columns = fetch_weights(
        gain_one,
        shift_one,
        w_query,
        w_key,
        w_value,
        b_out,
        gain_two,
        shift_two,
        w_fc_one,
        b_fc_two,
        w_out,
        w_fc_two,
    )
    (
        full_gain_one,
        gathered_first_shift,
        full_query,
        full_key,
        full_value,
        full_b_out,
        full_gain_two,
        gathered_second_shift,
        full_fc_one,
        full_b_fc_two,
    ) = rows
    full_out, full_fc_two = columns
    first_norm_gain = full_gain_one.astype(gathered_rows)
    second_norm_gain = full_gain_two.astype(gathered_rows)
    upstream_gradient = cotangent.astype(gathered_rows).reshape(count, width)
    grad_b_fc_two = jnp.sum(upstream_gradient, axis=0)
    grad_top_low = upstream_gradient.astype(jnp.bfloat16)
    grad_w_fc_two = jnp.einsum("tf,td->fd", act, grad_top_low, preferred_element_type=gathered_rows)
    grad_act = jnp.einsum(
        "td,fd->tf", grad_top_low, full_fc_two, preferred_element_type=gathered_rows
    )
    unused, gelu_back = jax.vjp(partial(jax.nn.gelu, approximate=False), pre)
    grad_pre = gelu_back(grad_act)[0].astype(jnp.bfloat16)
    grad_b_fc_one = jnp.sum(grad_pre.astype(gathered_rows), axis=0)
    grad_w_fc_one = jnp.einsum(
        "td,tf->df", normed_two, grad_pre, preferred_element_type=gathered_rows
    )
    normed_two_terms = jnp.einsum(
        "tf,df->td", grad_pre, full_fc_one, preferred_element_type=gathered_rows
    )
    second_normalized_gradient = head_total(normed_two_terms)
    middle_gradient = upstream_gradient + layer_norm_backward(
        second_normalized_gradient, second_standardized, second_inverse_deviation, second_norm_gain
    )
    grad_mid_low = middle_gradient.astype(jnp.bfloat16)
    second_gain_gradient = jnp.sum(second_normalized_gradient * second_standardized, axis=0)
    grad_shift_two = jnp.sum(second_normalized_gradient, axis=0)
    grad_b_out = jnp.sum(middle_gradient, axis=0)
    grad_w_out = jnp.einsum(
        "tj,td->jd", attended, grad_mid_low, preferred_element_type=gathered_rows
    )
    grad_attended = jnp.einsum(
        "td,jd->tj", grad_mid_low, full_out, preferred_element_type=gathered_rows
    ).astype(jnp.bfloat16)

    def attend_back(block):
        query_block, key_block, value_block, grad_block, log_block = block
        query_heads = query_block.reshape(frames, heads, HEAD_DIM)
        key_heads = key_block.reshape(-1, heads, HEAD_DIM)
        value_heads = value_block.reshape(-1, heads, HEAD_DIM)
        grad_heads = grad_block.reshape(frames, heads, HEAD_DIM)
        scores = (
            jnp.einsum("qhd,khd->hqk", query_heads, key_heads, preferred_element_type=gathered_rows)
            * scale
        )
        probs = jnp.exp(scores - log_block[..., None])
        grad_values = jnp.einsum(
            "hqk,qhd->khd",
            probs.astype(jnp.bfloat16),
            grad_heads,
            preferred_element_type=gathered_rows,
        )
        grad_probs = jnp.einsum(
            "qhd,khd->hqk", grad_heads, value_heads, preferred_element_type=gathered_rows
        )
        inner = jnp.sum(probs * grad_probs, axis=-1, keepdims=True)
        grad_scores = (probs * (grad_probs - inner)).astype(jnp.bfloat16)
        grad_queries = (
            jnp.einsum("hqk,khd->qhd", grad_scores, key_heads, preferred_element_type=gathered_rows)
            * scale
        )
        grad_keys = (
            jnp.einsum(
                "hqk,qhd->khd", grad_scores, query_heads, preferred_element_type=gathered_rows
            )
            * scale
        )
        return (
            grad_queries.reshape(frames, local).astype(jnp.bfloat16),
            grad_keys.reshape(-1, local),
            grad_values.reshape(-1, local),
        )

    grad_query_clips, grad_key_all, grad_value_all = lax.map(
        attend_back,
        (query_clips, key_all, value_all, grad_attended.reshape(clips, frames, local), log_totals),
    )
    grad_key_own, grad_value_own = (
        lax.psum_scatter(grad_key_all, "seq", scatter_dimension=1, tiled=True),
        lax.psum_scatter(grad_value_all, "seq", scatter_dimension=1, tiled=True),
    )
    grad_query = grad_query_clips.reshape(count, local)
    grad_key = grad_key_own.reshape(count, local).astype(jnp.bfloat16)
    grad_value = grad_value_own.reshape(count, local).astype(jnp.bfloat16)
    grad_b_query = jnp.sum(grad_query.astype(gathered_rows), axis=0)
    grad_b_value = jnp.sum(grad_value.astype(gathered_rows), axis=0)
    grad_w_query = jnp.einsum(
        "td,tj->dj", normed_one, grad_query, preferred_element_type=gathered_rows
    )
    grad_w_key = jnp.einsum("td,tj->dj", normed_one, grad_key, preferred_element_type=gathered_rows)
    grad_w_value = jnp.einsum(
        "td,tj->dj", normed_one, grad_value, preferred_element_type=gathered_rows
    )
    grad_normed_part = jnp.einsum(
        "tj,dj->td", grad_query, full_query, preferred_element_type=gathered_rows
    )
    grad_normed_part = grad_normed_part + jnp.einsum(
        "tj,dj->td", grad_key, full_key, preferred_element_type=gathered_rows
    )
    grad_normed_part = grad_normed_part + jnp.einsum(
        "tj,dj->td", grad_value, full_value, preferred_element_type=gathered_rows
    )
    first_normalized_gradient = head_total(grad_normed_part)
    first_gain_gradient = jnp.sum(first_normalized_gradient * first_standardized, axis=0)
    grad_shift_one = jnp.sum(first_normalized_gradient, axis=0)
    input_gradient = middle_gradient + layer_norm_backward(
        first_normalized_gradient, first_standardized, first_inverse_deviation, first_norm_gain
    )
    owned_rows = (
        lax.psum_scatter(first_gain_gradient, ("clip", "seq"), scatter_dimension=0, tiled=True),
        lax.psum_scatter(grad_shift_one, ("clip", "seq"), scatter_dimension=0, tiled=True),
        lax.psum_scatter(grad_w_query, ("clip", "seq"), scatter_dimension=0, tiled=True),
        lax.psum_scatter(grad_w_key, ("clip", "seq"), scatter_dimension=0, tiled=True),
        lax.psum_scatter(grad_w_value, ("clip", "seq"), scatter_dimension=0, tiled=True),
        lax.psum_scatter(grad_b_out, ("clip", "seq"), scatter_dimension=0, tiled=True),
        lax.psum_scatter(second_gain_gradient, ("clip", "seq"), scatter_dimension=0, tiled=True),
        lax.psum_scatter(grad_shift_two, ("clip", "seq"), scatter_dimension=0, tiled=True),
        lax.psum_scatter(grad_w_fc_one, ("clip", "seq"), scatter_dimension=0, tiled=True),
        lax.psum_scatter(grad_b_fc_two, ("clip", "seq"), scatter_dimension=0, tiled=True),
    )
    owned_columns = (
        lax.psum_scatter(grad_w_out, ("clip", "seq"), scatter_dimension=1, tiled=True),
        lax.psum_scatter(grad_w_fc_two, ("clip", "seq"), scatter_dimension=1, tiled=True),
    )
    bias_totals = lax.psum((grad_b_query, grad_b_value, grad_b_fc_one), ("clip", "seq"))
    return (
        outputs.reshape(clips, frames, width),
        input_gradient.reshape(clips, frames, width),
        owned_rows[0],
        owned_rows[1],
        owned_rows[2],
        bias_totals[0],
        owned_rows[3],
        owned_rows[4],
        bias_totals[1],
        owned_columns[0],
        owned_rows[5],
        owned_rows[6],
        owned_rows[7],
        owned_rows[8],
        bias_totals[2],
        owned_columns[1],
        owned_rows[9],
    )


def solution(mesh):
    return jax.shard_map(
        on_device,
        mesh=mesh,
        in_specs=(
            P("clip", "seq", None),
            P(("clip", "seq")),
            P(("clip", "seq")),
            P(("clip", "seq"), "head"),
            P("head"),
            P(("clip", "seq"), "head"),
            P(("clip", "seq"), "head"),
            P("head"),
            P("head", ("clip", "seq")),
            P(("clip", "seq")),
            P(("clip", "seq")),
            P(("clip", "seq")),
            P(("clip", "seq"), "head"),
            P("head"),
            P("head", ("clip", "seq")),
            P(("clip", "seq")),
            P("clip", "seq", None),
        ),
        out_specs=(
            P("clip", "seq", None),
            P("clip", "seq", None),
            P(("clip", "seq")),
            P(("clip", "seq")),
            P(("clip", "seq"), "head"),
            P("head"),
            P(("clip", "seq"), "head"),
            P(("clip", "seq"), "head"),
            P("head"),
            P("head", ("clip", "seq")),
            P(("clip", "seq")),
            P(("clip", "seq")),
            P(("clip", "seq")),
            P(("clip", "seq"), "head"),
            P("head"),
            P("head", ("clip", "seq")),
            P(("clip", "seq")),
        ),
        check_vma=False,
    )
```

profile of v0, /device:TPU:0, one launch (start us, length us, event | category | flops | bytes accessed | tf_op | source)
XLA Modules:
  0.0 687.4 jit_solution(10025798544051608802)
XLA Ops:
  15.1 25.7 %all-reduce.17 = (bf16[768]{0:T(1024)(128)(2,1)S(1)}, bf16[768]{0:T(1024)(128)(2,1)S(1)}, bf16[768]{0:T(1024)(128)(2,1)S(1)}, bf16[768]{0:T(1024)(128)(2,1)S(1)}...) all-reduce(bf16[768]{0:T(1024)(128)(2,1)S(1)} %dynamic-update-slice, ...), channel_id=1, replica_groups=mesh['clip'=4,'seq'=2,'head'=4] {'clip','seq'}, use_global_device_ids=true, to_apply=%add.1 | all-reduce | flops 4608 | bytes 18432
  44.1 15.9 %all_gather.55 = bf16[768,192]{1,0:T(8,128)(2,1)S(1)} all-gather(bf16[96,192]{1,0:T(8,128)(2,1)S(1)} %copy-done.26), channel_id=1, replica_groups=mesh['clip'=4,'seq'=2,'head'=4] {'clip','seq'}, dimensions={0}, use_global_device_ids=true | all-gather | bytes 331776 | tf_op jit(solution)/shard_map/all_gather | solution.py:48
  61.1 10.5 %all-gather.3 = bf16[2,750,192]{1,2,0:T(8,128)(2,1)S(1)} all-gather(bf16[1,750,192]{1,2,0:T(8,128)(2,1)S(1)} %fusion.39), channel_id=3, replica_groups=mesh['clip'=4,'seq'=2,'head'=4] {'seq'}, dimensions={0}, use_global_device_ids=true | all-gather | bytes 864000 | tf_op jit(solution)/shard_map/all_gather | solution.py:137
  75.3 15.6 %all_gather.54 = bf16[768,192]{1,0:T(8,128)(2,1)S(1)} all-gather(bf16[96,192]{1,0:T(8,128)(2,1)S(1)} %copy-done.27), channel_id=1, replica_groups=mesh['clip'=4,'seq'=2,'head'=4] {'clip','seq'}, dimensions={0}, use_global_device_ids=true | all-gather | bytes 331776 | tf_op jit(solution)/shard_map/all_gather | solution.py:47
  91.0 16.6 %all_gather.52 = bf16[768,192]{1,0:T(8,128)(2,1)S(1)} all-gather(bf16[96,192]{1,0:T(8,128)(2,1)S(1)} %copy-done.28), channel_id=1, replica_groups=mesh['clip'=4,'seq'=2,'head'=4] {'clip','seq'}, dimensions={0}, use_global_device_ids=true | all-gather | bytes 331776 | tf_op jit(solution)/shard_map/all_gather | solution.py:49
  108.9 9.9 %all-gather.2 = bf16[2,750,192]{1,2,0:T(8,128)(2,1)S(1)} all-gather(bf16[1,750,192]{1,2,0:T(8,128)(2,1)S(1)} %fusion.40), channel_id=2, replica_groups=mesh['clip'=4,'seq'=2,'head'=4] {'seq'}, dimensions={0}, use_global_device_ids=true | all-gather | bytes 864000 | tf_op jit(solution)/shard_map/all_gather | solution.py:138
  123.2 16.3 %all_gather.57 = bf16[192,768]{0,1:T(8,128)(2,1)S(1)} all-gather(bf16[192,96]{0,1:T(8,128)(2,1)S(1)} %copy.40), channel_id=1, replica_groups=mesh['clip'=4,'seq'=2,'head'=4] {'clip','seq'}, dimensions={1}, use_global_device_ids=true | all-gather | bytes 331776 | tf_op jit(solution)/shard_map/all_gather | solution.py:57
  140.1 7.0 %multiply_reduce_fusion.1 = (f32[3,750]{1,0:T(4,128)S(1)}, f32[3,750,1500]{2,1,0:T(8,128)}) fusion(bf16[750,3,64]{0,2,1:T(8,128)(2,1)S(1)} %bitcast.146, bf16[1500,3,64]{0,2,1:T(8,128)(2,1)S(1)} %reshape.253), kind=kOutput, calls=%fused_computation.6 | convolution fusion | flops 438747744 | bytes 14373000 | tf_op jit(solution)/shard_map/while/body/eval_jaxpr/qhd,khd->hqk/dot_general | solution.py:147
  147.1 7.4 %fusion = f32[3,750]{1,0:T(4,128)S(1)} fusion(f32[3,750,1500]{2,1,0:T(8,128)} %get-tuple-element.151, f32[3,750]{1,0:T(4,128)S(1)} %get-tuple-element.150), kind=kLoop, calls=%fused_computation.5 | loop fusion | flops 10122750 | bytes 13518000 | tf_op jit(solution)/shard_map/while/body/eval_jaxpr/reduce_sum | solution.py:152
  154.5 6.6 fusion.38
  164.4 94.1 %all-reduce.23.cloned.1.call-done = f32[750,768]{1,0:T(8,128)} async-done(((f32[750,768]{1,0:T(8,128)}), f32[750,768]{1,0:T(8,128)}) %all-reduce.23.cloned.1.call-update) | async-done | bytes 2304016 | tf_op jit(solution)/shard_map/psum | solution.py:64
  261.0 8.9 %multiply_convert_fusion.1 = (bf16[750,768]{1,0:T(8,128)(2,1)}, f32[750,768]{1,0:T(8,128)}, f32[750,768]{1,0:T(8,128)}) fusion(f32[768]{0:T(1024)S(1)} %convert_element_type.151, bf16[768,768]{1,0:T(8,128)(2,1)} %all-gather.7.cloned.1.call-done, f32[750,768]{1,0:T(8,128)S(1)} %get-tuple-element.147, f32[768]{0:T(1024)S(1)} %convert_element_type.149, ...), kind=kOutput, calls=%fused_computation.48 | convolution fusion | flops 925632000 | bytes 9258864 | tf_op jit(solution)/shard_map/dot_general | solution.py:167
  269.8 4.8 convert_reduce_fusion.2
  280.0 4.1 fusion.71
  284.2 86.5 %all-reduce.25.cloned.1.call-done = f32[750,768]{1,0:T(8,128)} async-done(((f32[750,768]{1,0:T(8,128)}), f32[750,768]{1,0:T(8,128)}) %all-reduce.25.cloned.1.call-update) | async-done | bytes 2304016 | tf_op jit(solution)/shard_map/psum | solution.py:64
  376.6 7.7 %fusion.2 = f32[3,64,1500]{2,1,0:T(8,128)} fusion(bf16[750,3,64]{0,2,1:T(8,128)(2,1)S(1)} %bitcast.144, f32[3,750,1500]{2,1,0:T(8,128)} %get-tuple-element.151, f32[3,750]{1,0:T(4,128)S(1)} %log_add_fusion), kind=kOutput, calls=%fused_computation.8 | convolution fusion | flops 442124992 | bytes 14949000 | tf_op jit(solution)/shard_map/while/body/eval_jaxpr/hqk,qhd->khd/dot_general | solution.py:246
  384.4 7.0 %multiply_reduce_fusion = (f32[3,750]{1,0:T(4,128)S(1)}, f32[3,750,1500]{2,1,0:T(8,128)}) fusion(f32[3,750,1500]{2,1,0:T(8,128)S(1)} %bitcast.141, f32[3,750]{1,0:T(4,128)S(1)} %log_add_fusion, bf16[750,3,64]{0,2,1:T(8,128)(2,1)S(1)} %bitcast.145, bf16[1500,3,64]{0,2,1:T(8,128)(2,1)S(1)} %copy-done.18), kind=kOutput, calls=%fused_computation.1 | convolution fusion | flops 445497760 | bytes 27882000 | tf_op jit(solution)/shard_map/while/body/eval_jaxpr/qhd,khd->hqk/dot_general | solution.py:252
  391.4 6.9 multiply_convert_fusion
  405.0 62.3 %all-reduce.28 = (bf16[1,1500,192]{1,2,0:T(8,128)(2,1)}, bf16[1,1500,192]{1,2,0:T(8,128)(2,1)}) all-reduce(f32[1,1500,192]{1,2,0:T(8,128)} %bitcast.142, f32[1,1500,192]{1,2,0:T(8,128)} %bitcast.143), channel_id=4, replica_groups=mesh['clip'=4,'seq'=2,'head'=4] {'seq'}, use_global_device_ids=true, to_apply=%region_12.13.clone | all-reduce | flops 576000 | bytes 3456000
  481.7 4.2 fusion.61
  485.9 4.2 fusion.43
  494.0 145.6 %all-reduce.27.cloned.1.call-done = (f32[750,768]{1,0:T(8,128)}, f32[750,768]{1,0:T(8,128)}) async-done(((f32[750,768]{1,0:T(8,128)}, f32[750,768]{1,0:T(8,128)}), (f32[750,768]{1,0:T(8,128)}, f32[750,768]{1,0:T(8,128)})) %all-reduce.27.cloned.1.call-update) | async-done | bytes 4608016 | tf_op jit(solution)/shard_map/psum | solution.py:64
  642.3 25.1 %all-reduce.14 = (f32[768]{0:T(1024)S(1)}, f32[768]{0:T(1024)S(1)}, f32[192]{0:T(256)}, f32[192]{0:T(256)}, f32[768]{0:T(1024)S(1)}, /*index=5*/f32[768]{0:T(102...) all-reduce(f32[768]{0:T(1024)S(1)} %get-tuple-element.115, ...), channel_id=6, replica_groups=mesh['clip'=4,'seq'=2,'head'=4] {'clip','seq'}, use_global_device_ids=true, to_apply=%region_18.19.clone | all-reduce | flops 5760 | bytes 46080
  673.7 3.8 copy.41
  (183 shorter events, 72.4 us)
Async XLA Ops:
  8.0 52.0 %copy-start = (bf16[1,750,768]{2,1,0:T(8,128)(2,1)S(1)}, bf16[1,750,768]{2,1,0:T(8,128)(2,1)}, u32[]{:S(2)}) copy-start(bf16[1,750,768]{2,1,0:T(8,128)(2,1)} %param.17) | copy-start | bytes 3456004
  8.0 36.0 %copy-start.26 = (bf16[96,192]{1,0:T(8,128)(2,1)S(1)}, bf16[96,192]{1,0:T(8,128)(2,1)}, u32[]{:S(2)}) copy-start(bf16[96,192]{1,0:T(8,128)(2,1)} %param.22) | copy-start | bytes 110596
  8.0 250.4 %all-reduce.23.cloned.1.call-start = ((), (), s32[]{:S(2)}) async-start(), calls=%async_computation.6 | async-start | bytes 4620288 | tf_op jit(solution)/shard_map/psum | solution.py:64
  60.0 11.6 %copy-start.8 = (bf16[768,192]{1,0:T(8,128)(2,1)}, bf16[768,192]{1,0:T(8,128)(2,1)S(1)}, u32[]{:S(2)}) copy-start(bf16[768,192]{1,0:T(8,128)(2,1)S(1)} %all_gather.55) | copy-start | bytes 884740
  60.5 14.8 %copy-start.27 = (bf16[96,192]{1,0:T(8,128)(2,1)S(1)}, bf16[96,192]{1,0:T(8,128)(2,1)}, u32[]{:S(2)}) copy-start(bf16[96,192]{1,0:T(8,128)(2,1)} %param.20) | copy-start | bytes 110596
  60.5 30.5 %copy-start.32 = (bf16[192]{0:T(256)(128)(2,1)S(1)}, bf16[192]{0:T(256)(128)(2,1)}, u32[]{:S(2)}) copy-start(bf16[192]{0:T(256)(128)(2,1)} %param.21) | copy-start | bytes 1156
  60.5 30.5 %copy-start.28 = (bf16[96,192]{1,0:T(8,128)(2,1)S(1)}, bf16[96,192]{1,0:T(8,128)(2,1)}, u32[]{:S(2)}) copy-start(bf16[96,192]{1,0:T(8,128)(2,1)} %param.23) | copy-start | bytes 110596
  61.1 46.5 %copy-start.33 = (bf16[192]{0:T(256)(128)(2,1)S(1)}, bf16[192]{0:T(256)(128)(2,1)}, u32[]{:S(2)}) copy-start(bf16[192]{0:T(256)(128)(2,1)} %param.24) | copy-start | bytes 1156
  75.3 64.8 %copy-start.5 = (bf16[1500,3,64]{0,2,1:T(8,128)(2,1)}, bf16[1500,3,64]{0,2,1:T(8,128)(2,1)S(1)}, u32[]{:S(2)}) copy-start(bf16[1500,3,64]{0,2,1:T(8,128)(2,1)S(1)} %reshape.253) | copy-start | bytes 1728004
  91.0 48.5 %copy-start.9 = (bf16[768,192]{1,0:T(8,128)(2,1)}, bf16[768,192]{1,0:T(8,128)(2,1)S(1)}, u32[]{:S(2)}) copy-start(bf16[768,192]{1,0:T(8,128)(2,1)S(1)} %all_gather.54) | copy-start | bytes 884740
  108.4 14.7 %copy-start.29 = (bf16[192,96]{1,0:T(8,128)(2,1)S(1)}, bf16[192,96]{1,0:T(8,128)(2,1)}, u32[]{:S(2)}) copy-start(bf16[192,96]{1,0:T(8,128)(2,1)} %param.25) | copy-start | bytes 110596
  139.5 21.6 %copy-start.11 = (bf16[192,768]{0,1:T(8,128)(2,1)}, bf16[192,768]{0,1:T(8,128)(2,1)S(1)}, u32[]{:S(2)}) copy-start(bf16[192,768]{0,1:T(8,128)(2,1)S(1)} %all_gather.57) | copy-start | bytes 884740
  163.1 97.9 %all-gather.7.cloned.1.call-start = ((), (), s32[]{:S(2)}) async-start(), calls=%async_computation.7 | async-start | bytes 1327104 | tf_op jit(solution)/shard_map/all_gather | solution.py:53
  163.7 106.2 %all-gather.9.cloned.1.call-start = ((), (), s32[]{:S(2)}) async-start(), calls=%async_computation.8 | async-start | bytes 1327104 | tf_op jit(solution)/shard_map/all_gather | solution.py:58
  164.3 206.4 %all-reduce.25.cloned.1.call-start = ((), (), s32[]{:S(2)}) async-start(), calls=%async_computation.9 | async-start | bytes 4620288 | tf_op jit(solution)/shard_map/psum | solution.py:64
  278.1 214.2 %reduce-scatter.21.cloned.1.call-start = ((), (), s32[]{:S(2)}) async-start(), calls=%async_computation.15 | async-start | bytes 884736
  373.6 10.8 %slice-start = ((s8[13860864]{0:T(1024)(128)(4,1)}), s8[4194304]{0:T(1024)(128)(4,1)S(1)}, s32[]{:S(2)}) async-start(s8[13860864]{0:T(1024)(128)(4,1)} %bitcast.140), calls=%async_computation.17 | async-start | bytes 8388608
  373.6 10.8 %slice-start.1 = ((s8[13860864]{0:T(1024)(128)(4,1)}), s8[4194304]{0:T(1024)(128)(4,1)S(1)}, s32[]{:S(2)}) async-start(s8[13860864]{0:T(1024)(128)(4,1)} %bitcast.140), calls=%async_computation.18 | async-start | bytes 8388608
  404.9 234.7 %all-reduce.27.cloned.1.call-start = ((), (), s32[]{:S(2)}) async-start(), calls=%async_computation.16 | async-start | bytes 9240576 | tf_op jit(solution)/shard_map/psum | solution.py:64
  472.2 206.7 %reduce-scatter.15.cloned.1.call-start = ((), (), s32[]{:S(2)}) async-start(), calls=%async_computation.12 | async-start | bytes 884736 | tf_op jit(solution)/shard_map/reduce_scatter | solution.py:313
  475.4 203.4 %reduce-scatter.13.cloned.1.call-start = ((), (), s32[]{:S(2)}) async-start(), calls=%async_computation.11 | async-start | bytes 884736 | tf_op jit(solution)/shard_map/reduce_scatter | solution.py:312
  478.8 200.0 %reduce-scatter.11.cloned.1.call-start = ((), (), s32[]{:S(2)}) async-start(), calls=%async_computation.10 | async-start | bytes 884736 | tf_op jit(solution)/shard_map/reduce_scatter | solution.py:311
  481.6 197.2 %reduce-scatter.17.cloned.1.call-start = ((), (), s32[]{:S(2)}) async-start(), calls=%async_computation.13 | async-start | bytes 2654208 | tf_op jit(solution)/shard_map/reduce_scatter | solution.py:317
  485.9 193.9 %reduce-scatter.19.cloned.1.call-start = ((), (), s32[]{:S(2)}) async-start(), calls=%async_computation.14 | async-start | bytes 2654208 | tf_op jit(solution)/shard_map/reduce_scatter | solution.py:322
  (27 other events, 92.8 us)
Sparse Core Ops, SparseCore 0:
  163.2 95.2 all-reduce.22
  278.3 92.3 all-reduce.24
  472.3 167.2 all-reduce.26
Sparse Core Ops, SparseCore 1:
  165.5 25.6 all-gather.6
  192.9 23.8 all-gather.8
  405.0 36.4 reduce-scatter.20
  476.7 33.4 reduce-scatter.14
  513.9 34.9 reduce-scatter.12
  552.5 34.9 reduce-scatter.10
  591.3 42.2 reduce-scatter.16
  637.3 42.5 reduce-scatter.18
where the time goes:
time: 695 us; the launch traced here: 687 us
  waiting for transfers between devices  328 us (47%)
  blocking collectives  198 us (28%)
  matrix products  79.4 us (11%)
  other arithmetic  33.5 us (5%)
  local copies, waits for them, and re-layouts  28.8 us (4%)
  between operations  18.3 us (3%)
    psum x3, waiting for transfers between devices, head_total(): return lax.psum(partial_sum, 'head')  326 us
    unnamed x3, blocking collectives  113 us
    unnamed x103, local copies, waits for them, and re-layouts  20.7 us
    all_gather x1, blocking collectives, fetch_weights(): lax.all_gather(w_value, ('clip', 'seq'), axis=0, tiled=True)  16.6 us
    all_gather x1, blocking collectives, fetch_weights(): lax.all_gather(w_out, ('clip', 'seq'), axis=1, tiled=True)  16.3 us
    all_gather x1, blocking collectives, fetch_weights(): lax.all_gather(w_key, ('clip', 'seq'), axis=0, tiled=True)  15.9 us
    all_gather x1, blocking collectives, fetch_weights(): lax.all_gather(w_query, ('clip', 'seq'), axis=0, tiled=True)  15.6 us
  transfers between devices with their start and end apart: 11, of which 4 were waited for; matrix products, arithmetic and copies ran while one was open for 8% of the time, Pallas kernels for 0%

commit v1 on v0

--- a/solution.py
+++ b/solution.py
@@ -1,21 +1,477 @@
 from functools import partial
+import types
 
 import jax
 import jax.numpy as jnp
 from jax import lax
+from jax.experimental import pallas as pl
+from jax.experimental.pallas import tpu as pltpu
 from jax.sharding import PartitionSpec as P
 
 HEAD_DIM = 64
-
-
-eps = 1e-05
-
+EPS = 1e-05
+F32 = jnp.float32
+BF16 = jnp.bfloat16
+MESH = pl.DeviceIdType.MESH
+
+
+def flip(value, bit):
+    return value + bit * (1 - 2 * lax.rem(lax.div(value, bit), 2))
+
+
+def flips(value, mask, bits):
+    for bit in bits:
+        if mask & bit:
+            value = flip(value, bit)
+    return value
+
+
+def powers(size):
+    bits, bit = [], 1
+    while bit < size:
+        bits.append(bit)
+        bit *= 2
+    return bits
+
+
+class Cube:
+    def __init__(self, clips, seqs):
+        self.clips, self.seqs, self.size = clips, seqs, clips * seqs
+        self.seq_bits = [(bit, "seq", bit) for bit in powers(seqs)]
+        self.clip_bits = [(bit * seqs, "clip", bit) for bit in powers(clips)]
+        core, rest = self.clip_bits[:1], self.clip_bits[1:]
+        self.orders = (
+            self.seq_bits + rest + core,
+            rest[:1] + self.seq_bits + rest[1:] + core,
+        )
+        self.all_bits = [bit for bit, _, _ in self.seq_bits + self.clip_bits]
+
+    def rank(self):
+        return lax.axis_index("clip") * self.seqs + lax.axis_index("seq")
+
+    def block(self, mask):
+        return flips(self.rank(), mask, self.all_bits)
+
+    @staticmethod
+    def peer(step):
+        _, axis, bit = step
+        return {axis: flip(lax.axis_index(axis), bit)}
+
+
+class Sems:
+    def __init__(self, send, recv):
+        self.send, self.recv, self.used = send, recv, 0
+
+    def take(self):
+        self.used += 1
+        return self.send.at[self.used - 1], self.recv.at[self.used - 1]
+
+
+def remote(src, dst, sems, device):
+    return pltpu.make_async_remote_copy(
+        src_ref=src,
+        dst_ref=dst,
+        send_sem=sems[0],
+        recv_sem=sems[1],
+        device_id=device,
+        device_id_type=MESH,
+    )
+
+
+class Gather:
+    def __init__(self, cube, sems, view, colors):
+        self.cube, self.view, self.colors = cube, view, colors
+        self.steps = len(cube.orders[0])
+        self.copies = [[[] for _ in range(self.steps)] for _ in range(colors)]
+        for color in range(colors):
+            masks = [0]
+            for k, step in enumerate(cube.orders[color]):
+                for mask in masks:
+                    block = cube.block(mask)
+                    piece = view(block, color)
+                    self.copies[color][k].append(
+                        remote(piece, piece, sems.take(), cube.peer(step))
+                    )
+                masks = masks + [mask ^ step[0] for mask in masks]
+
+    def start(self, k):
+        for color in range(self.colors):
+            for copy in self.copies[color][k]:
+                copy.start()
+
+    def arrive(self, k):
+        for color in range(self.colors):
+            for copy in self.copies[color][k]:
+                copy.wait_recv()
+
+    def advance(self, k):
+        for color in range(self.colors):
+            for copy in self.copies[color][k]:
+                copy.wait_recv()
+            if k + 1 < self.steps:
+                for copy in self.copies[color][k + 1]:
+                    copy.start()
+
+    def drain(self):
+        for color in range(self.colors):
+            for step in self.copies[color]:
+                for copy in step:
+                    copy.wait_send()
+
+
+def normalize(rows):
+    mean = jnp.mean(rows, axis=-1, keepdims=True)
+    centered = rows - mean
+    spread = jnp.mean(centered * centered, axis=-1, keepdims=True)
+    inverse = lax.rsqrt(spread + EPS)
+    return centered * inverse, inverse
+
+
+def dot(a, b):
+    return jnp.dot(a, b, preferred_element_type=F32)
+
+
+def dot_nt(a, b):
+    return lax.dot_general(a, b, (((1,), (1,)), ((), ())), preferred_element_type=F32)
+
+
+def dot_tn(a, b):
+    return lax.dot_general(a, b, (((0,), (0,)), ((), ())), preferred_element_type=F32)
+
+
+NEG = -1e30
+
+
+def fill(shape, value, dtype=F32):
+    return jnp.full(shape, value, dtype)
+
+
+def lane(shape):
+    return lax.broadcasted_iota(jnp.int32, shape, len(shape) - 1)
+
+
+class Line:
+    def __init__(self, nodes, sems, view, parts):
+        self.n, self.z = nodes, lax.axis_index("head")
+        self.view = view
+        self.right = [[sems.take() for _ in range(parts)] for _ in range(nodes - 1)]
+        self.left = [[sems.take() for _ in range(parts)] for _ in range(nodes - 1)]
+
+    def moves(self, hop, part):
+        z, n = self.z, self.n
+
+        def copy(origin, sems, target):
+            piece = self.view(origin, part)
+            return remote(piece, piece, sems, {"head": target})
+
+        sends = (
+            (
+                (z >= hop) & (z < n - 1),
+                lambda: copy(z - hop, self.right[hop][part], z + 1),
+            ),
+            (
+                (n - 1 - z >= hop) & (z > 0),
+                lambda: copy(z + hop, self.left[hop][part], z - 1),
+            ),
+        )
+        arrivals = (
+            (z > hop, lambda: copy(z - 1 - hop, self.right[hop][part], z - 1)),
+            (n - 1 - z > hop, lambda: copy(z + 1 + hop, self.left[hop][part], z + 1)),
+        )
+        return sends, arrivals
+
+    def start(self, hop, part):
+        for condition, copy in self.moves(hop, part)[0]:
+            pl.when(condition)(lambda copy=copy: copy().start())
+
+    def arrive(self, hop, part):
+        for condition, copy in self.moves(hop, part)[1]:
+            pl.when(condition)(lambda copy=copy: copy().wait_recv())
+
+    def drain(self, part):
+        for hop in range(self.n - 1):
+            for condition, copy in self.moves(hop, part)[0]:
+                pl.when(condition)(lambda copy=copy: copy().wait_send())
+
+
+def entry_barrier(cube, heads):
+    barrier = pltpu.get_barrier_semaphore()
+    z = lax.axis_index("head")
+    peers = [cube.peer(step) for step in cube.orders[0]]
+    peers += [{"head": lax.rem(z + d, heads)} for d in range(1, heads)]
+    for peer in peers:
+        pl.semaphore_signal(barrier, inc=1, device_id=peer, device_id_type=MESH)
+    pl.semaphore_wait(barrier, len(peers))
+
+
+def stage_one(m, cube, nz, sems):
+    z = lax.axis_index("head")
+    r = cube.rank()
+    rows = m.wq.shape[0]
+    colors = m.gq.shape[1]
+    half = rows // colors
+    nh = m.q.shape[0]
+    frames = m.x.shape[0]
+    padded = m.xp.shape[0]
+    tile = 128
+    tiles = padded // tile
+    width = m.x.shape[1]
+
+    gq = Gather(cube, sems, lambda b, c: m.gq.at[b, c], colors)
+    gv = Gather(cube, sems, lambda b, c: m.gv.at[b], 1)
+    g1 = Gather(cube, sems, lambda b, c: m.g1.at[b, c], colors)
+    g2 = Gather(cube, sems, lambda b, c: m.g2.at[b, c], colors)
+    go = Gather(cube, sems, lambda b, c: m.go.at[:, b, c], colors)
+
+    m.gv[r] = m.vsh[...]
+    for c in range(colors):
+        part = pl.ds(c * half, half)
+        for h in range(nh):
+            cols = slice(h * HEAD_DIM, (h + 1) * HEAD_DIM)
+            m.gq[r, c, :, h * 128 : h * 128 + 64] = m.wk[part, cols]
+            m.gq[r, c, :, h * 128 + 64 : (h + 1) * 128] = m.wv[part, cols]
+        m.gq[r, c, :, nh * 128 : nh * 128 + nh * 64] = m.wq[part, :]
+        spare = m.gq.shape[3] - nh * 192
+        if spare:
+            m.gq[r, c, :, nh * 192 :] = fill((half, spare), 0, BF16)
+
+    entry_barrier(cube, nz)
+    gv.start(0)
+    gq.start(0)
+
+    wot = m.wo[...].T
+    w2t = m.w2[...].T
+    for c in range(colors):
+        part = slice(c * half, (c + 1) * half)
+        m.go[z, r, c] = wot[part]
+        m.g2[r, c] = w2t[part]
+        m.g1[r, c] = m.w1[part, :]
+    out_sems = [sems.take() for _ in range(nz - 1)]
+
+    def out_copies(arriving):
+        for d in range(1, nz):
+            origin = lax.rem(z + nz - d, nz) if arriving else z
+            target = lax.rem(z + d, nz)
+            piece = m.go.at[origin, r]
+            yield remote(piece, piece, out_sems[d - 1], {"head": target})
+
+    for copy in out_copies(False):
+        copy.start()
+
+    m.xp[0:frames] = m.x[...]
+    m.xp[frames:padded] = fill((padded - frames, width), 0, BF16)
+
+    def norm_tile(i, carry):
+        at = pl.ds(pl.multiple_of(i * tile, tile), tile)
+        xhat, inverse = normalize(m.xp[at].astype(F32))
+        m.xh1[at] = xhat
+        m.r1[at] = jnp.broadcast_to(inverse, (tile, 128))
+        return carry
+
+    third = tiles // cube_steps(gq)
+    for k in range(gq.steps):
+        top = tiles if k == gq.steps - 1 else third * (k + 1)
+        lax.fori_loop(third * k, top, norm_tile, 0)
+        gv.advance(k)
+        gq.advance(k)
+    for b in range(cube.size):
+        m.vec[:, b * rows : (b + 1) * rows] = m.gv[b, :, :rows]
+    g1.start(0)
+    g2.start(0)
+
+    gain, shift = m.vec[0:1, :], m.vec[1:2, :]
+    bias = m.bias[0:1, : m.gq.shape[3]]
+    scale = HEAD_DIM**-0.5
+
+    def project(i, carry):
+        at = pl.ds(pl.multiple_of(i * tile, tile), tile)
+        n1 = (m.xh1[at] * gain + shift).astype(BF16)
+        m.n1[at] = n1
+        packed = dot(n1, m.gq[...].reshape(cube.size * rows, m.gq.shape[3])) + bias
+        left = lane((tile, 128)) < 64
+        for h in range(nh):
+            m.kv[0, h, at] = packed[:, h * 128 : (h + 1) * 128].astype(BF16)
+            base = nh * 128 + (h // 2) * 128
+            pair = packed[:, base : base + 128]
+            if h % 2:
+                pair = pltpu.roll(pair, 64, 1)
+            pair = pair.astype(BF16).astype(F32) * scale
+            m.q[h, at] = jnp.where(left, pair, 0.0).astype(BF16)
+        return carry
+
+    lax.fori_loop(0, tiles, project, 0)
+
+    kv_sems = [sems.take() for _ in range(nh)]
+    other = {"seq": flip(lax.axis_index("seq"), 1)}
+    kv_copies = [
+        remote(m.kv.at[0, h], m.kv.at[1, h], kv_sems[h], other) for h in range(nh)
+    ]
+    for copy in kv_copies:
+        copy.start()
+    for copy in out_copies(True):
+        copy.wait_recv()
+    go.start(0)
+
+    left = lane((padded, 128)) < 64
+
+    def prepare(part, h):
+        block = m.kv[part, h]
+        m.kvt[part, h] = block.T
+        m.vo[part, h] = jnp.where(left, jnp.ones_like(block), block)
+
+    for h in range(nh):
+        prepare(0, h)
+
+    line = Line(nz, sems, lambda origin, part: m.attz.at[origin, part], nh)
+    block = 256
+    valid = frames - (padded - 128)
+
+    def attend(h):
+        def one(b, carry):
+            at = pl.ds(pl.multiple_of(b * block, block), block)
+            query = m.q[h, at]
+            keep = lane((block, 128)) < valid
+            parts = []
+            top = None
+            for part in range(2):
+                s = dot(query, m.kvt[part, h])
+                body, tail = s[:, : padded - 128], s[:, padded - 128 :]
+                tail = jnp.where(keep, tail, NEG)
+                parts += [body, tail]
+                high = jnp.maximum(jnp.max(body, axis=1, keepdims=True), jnp.max(tail, axis=1, keepdims=True))
+                top = high if top is None else jnp.maximum(top, high)
+            place = 0
+            for s in parts:
+                m.p[h, at, place : place + s.shape[1]] = jnp.exp(s - top).astype(BF16)
+                place += s.shape[1]
+            acc = dot(m.p[h, at, :padded], m.vo[0, h]) + dot(m.p[h, at, padded:], m.vo[1, h])
+            inverse = 1.0 / pltpu.roll(acc, 64, 1)
+            att = acc * inverse
+            right = lane((block, 128)) >= 64
+            m.il[h, at] = jnp.where(right, inverse, 0.0)
+            m.atto[h, at] = jnp.where(right, att, 0.0).astype(BF16)
+            turned = pltpu.roll(att, 64, 1)
+            packed = jnp.where(right[: block // 2], att[block // 2 :], turned[: block // 2])
+            to = pl.ds(pl.multiple_of(b * (block // 2), block // 2), block // 2)
+            m.attz[z, h, to] = packed.astype(BF16)
+            return carry
+
+        lax.fori_loop(0, padded // block, one, 0)
+
+    last = g1.steps - 1
+    for h in range(nh):
+        kv_copies[h].wait_recv()
+        prepare(1, h)
+        attend(h)
+        line.start(0, h)
+        if h < g1.steps:
+            for g in (g1, g2, go):
+                g.advance(h)
+        if h:
+            line.arrive(0, h - 1)
+            line.start(1, h - 1)
+        if h > 1:
+            line.arrive(1, h - 2)
+            line.start(2, h - 2)
+    for k in range(min(nh, g1.steps), g1.steps):
+        for g in (g1, g2, go):
+            g.advance(k)
+    for hop in range(nz - 1):
+        for h in range(nh):
+            done = nh - 1 - h
+            if hop >= done:
+                line.arrive(hop, h)
+                if hop + 1 < nz - 1:
+                    line.start(hop + 1, h)
+
+    for copy in kv_copies:
+        copy.wait_send()
+    for copy in out_copies(False):
+        copy.wait_send()
+    for g in (gv, gq, g1, g2, go):
+        g.drain()
+    for h in range(nh):
+        line.drain(h)
+
+
+def cube_steps(gather):
+    return gather.steps
+
+
+def front(inputs, vectors, biases, w_query, w_key, w_value, w_out, w_fc_one, w_fc_two, mesh_shape):
+    nz = mesh_shape["head"]
+    cube = Cube(mesh_shape["clip"], mesh_shape["seq"])
+    frames, width = inputs.shape
+    rows, local = w_query.shape
+    hidden = w_fc_one.shape[1]
+    nh = local // HEAD_DIM
+    padded = -(-frames // 256) * 256
+    colors = 2 if rows % 32 == 0 else 1
+    half = rows // colors
+    packed = -(-(nh * 192) // 128) * 128
+    outs = dict(
+        n1=((padded, width), BF16),
+        q=((nh, padded, 128), BF16),
+        kv=((2, nh, padded, 128), BF16),
+        atto=((nh, padded, 128), BF16),
+        attz=((nz, nh, padded // 2, 128), BF16),
+        gq=((cube.size, colors, half, packed), BF16),
+        go=((nz, cube.size, colors, half, local), BF16),
+        g1=((cube.size, colors, half, hidden), BF16),
+        g2=((cube.size, colors, half, hidden), BF16),
+        vec=((8, width), F32),
+    )
+    scratch = dict(
+        gv=((cube.size, 8, 128), F32),
+        xp=((padded, width), BF16),
+        xh1=((padded, width), F32),
+        r1=((padded, 128), F32),
+        kvt=((2, nh, 128, padded), BF16),
+        vo=((2, nh, padded, 128), BF16),
+        p=((nh, padded, 2 * padded), BF16),
+        il=((nh, padded, 128), F32),
+    )
+    ins = dict(x=inputs, vsh=vectors, bias=biases, wq=w_query, wk=w_key, wv=w_value, wo=w_out, w1=w_fc_one, w2=w_fc_two)
+    count = 200
+
+    def body(*refs):
+        names = list(ins) + list(outs) + list(scratch)
+        m = types.SimpleNamespace(**dict(zip(names, refs)))
+        sems = Sems(*refs[len(names):])
+        stage_one(m, cube, nz, sems)
+
+    res = pl.pallas_call(
+        body,
+        out_shape=[jax.ShapeDtypeStruct(*v) for v in outs.values()],
+        in_specs=[pl.BlockSpec(memory_space=pltpu.VMEM)] * len(ins),
+        out_specs=[pl.BlockSpec(memory_space=pltpu.VMEM)] * len(outs),
+        scratch_shapes=[pltpu.VMEM(*v) for v in scratch.values()] + [pltpu.SemaphoreType.DMA((count,))] * 2,
+        compiler_params=pltpu.CompilerParams(collective_id=0, has_side_effects=True, vmem_limit_bytes=60 * 2**20),
+        name="front",
+    )(*ins.values())
+    return types.SimpleNamespace(**dict(zip(outs, res)))
+
+
+def vector_pack(vectors):
+    stack = jnp.stack([v.astype(F32) for v in vectors])
+    return jnp.pad(stack, ((0, 8 - stack.shape[0]), (0, 128 - stack.shape[1])))
+
+
+def biases_pack(b_query, b_value, b_fc_one, heads):
+    zero = jnp.zeros((HEAD_DIM,), F32)
+    parts = []
+    for h in range(heads):
+        parts += [zero, b_value[h * HEAD_DIM : (h + 1) * HEAD_DIM].astype(F32)]
+    row = jnp.concatenate(parts + [b_query.astype(F32)])
+    width = b_fc_one.shape[0]
+    row = jnp.pad(row, (0, width - row.shape[0]))
+    return jnp.pad(jnp.stack([row, b_fc_one.astype(F32)]), ((0, 6), (0, 0)))
 
 def layer_norm_forward(values, norm_gain, norm_shift):
     row_mean = jnp.mean(values, axis=-1, keepdims=True)
     centered_values = values - row_mean
     spread = jnp.mean(centered_values * centered_values, axis=-1, keepdims=True)
-    inverse_deviation = lax.rsqrt(spread + eps)
+    inverse_deviation = lax.rsqrt(spread + EPS)
     standardized = centered_values * inverse_deviation
     return (standardized * norm_gain + norm_shift, standardized, inverse_deviation)
 
@@ -82,6 +538,7 @@
     w_fc_two,
     b_fc_two,
     cotangent,
+    mesh_shape=None,
 ):
     clips, frames, width = inputs.shape
     local = w_query.shape[1]
@@ -89,77 +546,38 @@
     scale = HEAD_DIM ** (-0.5)
     gathered_rows = jnp.float32
     count = clips * frames
-    rows, columns = fetch_weights(
-        gain_one,
-        shift_one,
-        w_query,
-        w_key,
-        w_value,
-        b_out,
-        gain_two,
-        shift_two,
-        w_fc_one,
-        b_fc_two,
-        w_out,
-        w_fc_two,
-    )
-    (
-        full_gain_one,
-        gathered_first_shift,
-        full_query,
-        full_key,
-        full_value,
-        full_b_out,
-        full_gain_two,
-        gathered_second_shift,
-        full_fc_one,
-        full_b_fc_two,
-    ) = rows
-    full_out, full_fc_two = columns
-    token_rows = inputs.astype(gathered_rows).reshape(count, width)
-    first_norm_gain = full_gain_one.astype(gathered_rows)
-    second_norm_gain = full_gain_two.astype(gathered_rows)
+    token_rows = inputs.astype(jnp.float32).reshape(count, width)
+    wide = biases_pack(b_query, b_value, b_fc_one, heads)
+    vectors = vector_pack((gain_one, shift_one, gain_two, shift_two, b_out, b_fc_two))
+    f = front(inputs.reshape(count, width), vectors, wide, w_query, w_key, w_value, w_out, w_fc_one, w_fc_two, mesh_shape)
+    gq = f.gq.reshape(width, -1)
+    full_key = jnp.concatenate([gq[:, i*128:i*128+64] for i in range(heads)], 1)
+    full_value = jnp.concatenate([gq[:, i*128+64:i*128+128] for i in range(heads)], 1)
+    full_query = gq[:, heads*128:heads*192]
+    z = lax.axis_index("head")
+    full_out = lax.dynamic_index_in_dim(f.go.reshape(4, width, local), z, 0, False).T
+    full_fc_one = f.g1.reshape(width, -1)
+    full_fc_two = f.g2.reshape(width, -1).T
+    v = f.vec
+    first_norm_gain, second_norm_gain = v[0], v[2]
+    gathered_first_shift, gathered_second_shift, full_b_out, full_b_fc_two = v[1], v[3], v[4], v[5]
     normalized_gathered, first_standardized, first_inverse_deviation = layer_norm_forward(
         token_rows, first_norm_gain, gathered_first_shift.astype(gathered_rows)
     )
-    normed_one = normalized_gathered.astype(jnp.bfloat16)
-    query = (
-        jnp.dot(normed_one, full_query, preferred_element_type=gathered_rows)
-        + b_query.astype(gathered_rows)
-    ).astype(jnp.bfloat16)
-    key = jnp.dot(normed_one, full_key, preferred_element_type=gathered_rows).astype(jnp.bfloat16)
-    value = (
-        jnp.dot(normed_one, full_value, preferred_element_type=gathered_rows)
-        + b_value.astype(gathered_rows)
-    ).astype(jnp.bfloat16)
+    normed_one = f.n1[:count]
+    query = jnp.concatenate([f.q[i, :count, :64] for i in range(heads)], 1) * 8
     query_clips = query.reshape(clips, frames, local)
-    key_all, value_all = (
-        lax.all_gather(key.reshape(clips, frames, local), "seq", axis=1, tiled=True),
-        lax.all_gather(value.reshape(clips, frames, local), "seq", axis=1, tiled=True),
-    )
-
-    def attend(block):
-        query_block, key_block, value_block = block
-        query_heads = query_block.reshape(frames, heads, HEAD_DIM)
-        key_heads = key_block.reshape(-1, heads, HEAD_DIM)
-        value_heads = value_block.reshape(-1, heads, HEAD_DIM)
-        scores = (
-            jnp.einsum("qhd,khd->hqk", query_heads, key_heads, preferred_element_type=gathered_rows)
-            * scale
-        )
-        top = jnp.max(scores, axis=-1, keepdims=True)
-        expo = jnp.exp(scores - top)
-        total = jnp.sum(expo, axis=-1, keepdims=True)
-        probs = (expo / total).astype(jnp.bfloat16)
-        result = jnp.einsum(
-            "hqk,khd->qhd", probs, value_heads, preferred_element_type=gathered_rows
-        )
-        return (result.reshape(frames, local).astype(jnp.bfloat16), (top + jnp.log(total))[..., 0])
-
-    attended_clips, log_totals = lax.map(attend, (query_clips, key_all, value_all))
-    attended = attended_clips.reshape(count, local)
+    sq = lax.axis_index("seq")
+    kvs = jnp.where(sq == 0, f.kv, f.kv[::-1])[:, :, :count]
+    key_all = jnp.concatenate([jnp.concatenate([kvs[p, i, :, :64] for i in range(heads)], 1) for p in range(2)], 0)[None]
+    value_all = jnp.concatenate([jnp.concatenate([kvs[p, i, :, 64:] for i in range(heads)], 1) for p in range(2)], 0)[None]
+    attended = jnp.concatenate([f.atto[i, :count, 64:] for i in range(heads)], 1)
+    log_totals = None
+    pk = f.attz.reshape(4, heads, 3, 128, 2, 64).transpose(2, 4, 3, 0, 1, 5).reshape(768, 768)[:count]
+    full_out_all = f.go.transpose(0, 4, 1, 2, 3).reshape(width, width)
+    attn_all = jnp.dot(pk, full_out_all, preferred_element_type=gathered_rows)
     attn_terms = jnp.dot(attended, full_out, preferred_element_type=gathered_rows)
-    middle_state = token_rows + head_total(attn_terms) + full_b_out.astype(gathered_rows)
+    middle_state = token_rows + attn_all + full_b_out.astype(gathered_rows)
     normalized_middle, second_standardized, second_inverse_deviation = layer_norm_forward(
         middle_state, second_norm_gain, gathered_second_shift.astype(gathered_rows)
     )
@@ -172,35 +590,6 @@
     outputs = (middle_state + head_total(ffn_terms) + full_b_fc_two.astype(gathered_rows)).astype(
         jnp.bfloat16
     )
-    rows, columns = fetch_weights(
-        gain_one,
-        shift_one,
-        w_query,
-        w_key,
-        w_value,
-        b_out,
-        gain_two,
-        shift_two,
-        w_fc_one,
-        b_fc_two,
-        w_out,
-        w_fc_two,
-    )
-    (
-        full_gain_one,
-        gathered_first_shift,
-        full_query,
-        full_key,
-        full_value,
-        full_b_out,
-        full_gain_two,
-        gathered_second_shift,
-        full_fc_one,
-        full_b_fc_two,
-    ) = rows
-    full_out, full_fc_two = columns
-    first_norm_gain = full_gain_one.astype(gathered_rows)
-    second_norm_gain = full_gain_two.astype(gathered_rows)
     upstream_gradient = cotangent.astype(gathered_rows).reshape(count, width)
     grad_b_fc_two = jnp.sum(upstream_gradient, axis=0)
     grad_top_low = upstream_gradient.astype(jnp.bfloat16)
@@ -233,7 +622,7 @@
     ).astype(jnp.bfloat16)
 
     def attend_back(block):
-        query_block, key_block, value_block, grad_block, log_block = block
+        query_block, key_block, value_block, grad_block = block
         query_heads = query_block.reshape(frames, heads, HEAD_DIM)
         key_heads = key_block.reshape(-1, heads, HEAD_DIM)
         value_heads = value_block.reshape(-1, heads, HEAD_DIM)
@@ -242,7 +631,7 @@
             jnp.einsum("qhd,khd->hqk", query_heads, key_heads, preferred_element_type=gathered_rows)
             * scale
         )
-        probs = jnp.exp(scores - log_block[..., None])
+        probs = jax.nn.softmax(scores, axis=-1)
         grad_values = jnp.einsum(
             "hqk,qhd->khd",
             probs.astype(jnp.bfloat16),
@@ -272,7 +661,7 @@
 
     grad_query_clips, grad_key_all, grad_value_all = lax.map(
         attend_back,
-        (query_clips, key_all, value_all, grad_attended.reshape(clips, frames, local), log_totals),
+        (query_clips, key_all, value_all, grad_attended.reshape(clips, frames, local)),
     )
     grad_key_own, grad_value_own = (
         lax.psum_scatter(grad_key_all, "seq", scatter_dimension=1, tiled=True),
@@ -345,7 +734,7 @@
 
 def solution(mesh):
     return jax.shard_map(
-        on_device,
+        partial(on_device, mesh_shape=dict(mesh.shape)),
         mesh=mesh,
         in_specs=(
             P("clip", "seq", None),

time: 695 us -> 698 us (level)
  blocking collectives: 198 us -> 86.9 us
  Pallas kernels: 0 us -> 69.8 us
  waiting for transfers between devices: 328 us -> 373 us
  local copies, waits for them, and re-layouts: 28.8 us -> 43.6 us
  matrix products: 79.4 us -> 67.4 us
    psum x3 -> x2, waiting for transfers between devices: 326 us -> 204 us  [head_total(): return lax.psum(partial_sum, 'head')]
    all_gather x6 -> x0, blocking collectives: 84.9 us -> none  [the longest x1 16.6 us: fetch_weights(): lax.all_gather(w_value, ('clip', 'seq'), axis=0, tiled=True)]
    pallas_call x0 -> x1, Pallas kernels: none -> 69.8 us  [front(): pl.pallas_call(body, out_shape=[jax.ShapeDtypeStruct(*v) for v in outs.va...]
    reduce_scatter x1, waiting for transfers between devices: 0.01 us -> 46.3 us  [on_device(): lax.psum_scatter(grad_w_fc_one, ('clip', 'seq'), scatter_dimension=0, til...]
    reduce_scatter x1, waiting for transfers between devices: 0.97 us -> 46.3 us  [on_device(): lax.psum_scatter(grad_w_fc_two, ('clip', 'seq'), scatter_dimension=1, til...]
    reduce_scatter x1, waiting for transfers between devices: 0.01 us -> 38.5 us  [on_device(): lax.psum_scatter(grad_w_query, ('clip', 'seq'), scatter_dimension=0, tile...]
    reduce_scatter x1, waiting for transfers between devices: 0.01 us -> 37.4 us  [on_device(): lax.psum_scatter(grad_w_key, ('clip', 'seq'), scatter_dimension=0, tiled=...]
    unnamed x3 -> x2, blocking collectives: 113 us -> 86.9 us
  transfers between devices with their start and end apart: 11 -> 8, of which waited for: 4 -> 6; matrix products, arithmetic and copies ran while one was open for 8% -> 11% of each run, Pallas kernels for 0% -> 0%
where the time goes in v1:
time: 698 us; the launch traced here: 688 us
  waiting for transfers between devices  373 us (53%)
  blocking collectives  86.9 us (12%)
  Pallas kernels  69.8 us (10%)
  matrix products  67.4 us (10%)
  local copies, waits for them, and re-layouts  43.6 us (6%)
  other arithmetic  31 us (4%)
  between operations  16.1 us (2%)
    psum x2, waiting for transfers between devices, head_total(): return lax.psum(partial_sum, 'head')  204 us
    unnamed x2, blocking collectives  86.9 us
    pallas_call x1, Pallas kernels, front(): pl.pallas_call(body, out_shape=[jax.ShapeDtypeStruct(*v) for v in outs.va...  69.8 us
    reduce_scatter x1, waiting for transfers between devices, on_device(): lax.psum_scatter(grad_w_fc_one, ('clip', 'seq'), scatter_dimension=0, til...  46.3 us
    reduce_scatter x1, waiting for transfers between devices, on_device(): lax.psum_scatter(grad_w_fc_two, ('clip', 'seq'), scatter_dimension=1, til...  46.3 us
    reduce_scatter x1, waiting for transfers between devices, on_device(): lax.psum_scatter(grad_w_query, ('clip', 'seq'), scatter_dimension=0, tile...  38.5 us
    reduce_scatter x1, waiting for transfers between devices, on_device(): lax.psum_scatter(grad_w_key, ('clip', 'seq'), scatter_dimension=0, tiled=...  37.4 us
    unnamed x63, local copies, waits for them, and re-layouts  14.3 us
  transfers between devices with their start and end apart: 8, of which 6 were waited for; matrix products, arithmetic and copies ran while one was open for 11% of the time, Pallas kernels for 0%

profile of v1, /device:TPU:0, one launch (start us, length us, event | category | flops | bytes accessed | tf_op | source)
XLA Modules:
  0.0 688.3 jit_solution(14435115338795864599)
XLA Ops:
  13.9 69.8 %front.1 = (bf16[768,768]{1,0:T(8,128)(2,1)}, bf16[3,768,128]{2,1,0:T(8,128)(2,1)}, bf16[2,3,768,128]{3,2,1,0:T(8,128)(2,1)}, bf16[3,768,128]{2,1,0:T(8,128)(2,1...) custom-call(bf16[750,768]{1,0:T(8,128)(2,1)} %bitcast.181, ...), custom_call_target="tpu_custom_call" | custom-call | tf_op jit(solution)/shard_map/front/pallas_call | solution.py:443
  91.7 2.8 copy.61
  94.5 3.9 reshape.168
  98.4 2.9 fusion.91
  102.5 7.1 %multiply_convert_fusion.1 = (bf16[750,768]{1,0:T(8,128)(2,1)}, f32[750,768]{1,0:T(8,128)S(1)}, f32[750,768]{1,0:T(8,128)S(1)}) fusion(f32[768]{0:T(1024)S(1)} %convert_element_type.106, bf16[768,768]{1,0:T(8,128)(2,1)S(1)} %bitcast.205, f32[750,768]{1,0:T(8,128)S(1)} %get-tuple-element.189, f32[768]{0:T(1024)S(1)} %get-tuple-element.139, ...), kind=kOutput, calls=%fused_computation.49 | convolution fusion | flops 925632000 | bytes 9258864 | tf_op jit(solution)/shard_map/dot_general | solution.py:585
  115.2 3.0 reverse_select_fusion
  136.4 10.3 %fusion.92 = (f32[3,750]{1,0:T(4,128)S(1)}, f32[3,750,1500]{2,1,0:T(8,128)}) fusion(bf16[1500,3,64]{0,2,1:T(8,128)(2,1)} %bitcast.188, bf16[750,1,64]{2,0,1:T(8,128)(2,1)} %get-tuple-element.183, bf16[750,1,64]{2,0,1:T(8,128)(2,1)} %get-tuple-element.184, bf16[750,1,64]{2,0,1:T(8,128)(2,1)} %get-tuple-element.182), kind=kOutput, calls=%fused_computation.163 | convolution fusion | flops 442558496 | bytes 14373000 | tf_op jit(solution)/shard_map/while/body/eval_jaxpr/sub | solution.py:634
  146.7 60.0 %all-reduce.18.cloned.1.call-done = f32[750,768]{1,0:T(8,128)} async-done(((f32[750,768]{1,0:T(8,128)}), f32[750,768]{1,0:T(8,128)}) %all-reduce.18.cloned.1.call-update) | async-done | bytes 2304016 | tf_op jit(solution)/shard_map/psum | solution.py:520
  209.6 3.3 fusion.86
  217.3 6.3 multiply_reduce_fusion
  223.7 6.3 multiply_convert_fusion
  232.5 2.8 convert_reduce_fusion.4
  237.1 62.3 %all-reduce.21 = (bf16[1,1500,192]{1,2,0:T(8,128)(2,1)}, bf16[1,1500,192]{1,2,0:T(8,128)(2,1)}) all-reduce(f32[1,1500,192]{1,2,0:T(8,128)} %bitcast.182, f32[1,1500,192]{1,2,0:T(8,128)} %bitcast.192), channel_id=2, replica_groups=mesh['clip'=4,'seq'=2,'head'=4] {'seq'}, use_global_device_ids=true, to_apply=%region_11.12.clone | all-reduce | flops 576000 | bytes 3456000
  309.4 3.1 fusion.47
  315.6 4.1 fusion.84
  319.8 4.1 fusion.42
  329.7 144.3 %all-reduce.20.cloned.1.call-done = (f32[750,768]{1,0:T(8,128)}, f32[750,768]{1,0:T(8,128)}) async-done(((f32[750,768]{1,0:T(8,128)}, f32[750,768]{1,0:T(8,128)}), (f32[750,768]{1,0:T(8,128)}, f32[750,768]{1,0:T(8,128)})) %all-reduce.20.cloned.1.call-update) | async-done | bytes 4608016 | tf_op jit(solution)/shard_map/psum | solution.py:520
  476.7 24.5 %all-reduce.11 = (f32[768]{0:T(1024)S(1)}, f32[768]{0:T(1024)S(1)}, f32[192]{0:T(256)}, f32[192]{0:T(256)}, f32[768]{0:T(1024)S(1)}, /*index=5*/f32[768]{0:T(102...) all-reduce(f32[768]{0:T(1024)S(1)} %get-tuple-element.131, ...), channel_id=4, replica_groups=mesh['clip'=4,'seq'=2,'head'=4] {'clip','seq'}, use_global_device_ids=true, to_apply=%region_17.18.clone | all-reduce | flops 5760 | bytes 46080
  504.8 2.8 fusion.22
  507.5 3.8 copy.68
  512.7 37.4 %reduce-scatter.13.cloned.1.call-done = f32[96,192]{1,0:T(8,128)} async-done(((f32[768,192]{1,0:T(8,128)}), f32[96,192]{1,0:T(8,128)}) %reduce-scatter.13.cloned.1.call-update) | async-done | bytes 73744 | tf_op jit(solution)/shard_map/reduce_scatter | solution.py:701
  550.1 38.5 %reduce-scatter.11.cloned.1.call-done = f32[96,192]{1,0:T(8,128)} async-done(((f32[768,192]{1,0:T(8,128)}), f32[96,192]{1,0:T(8,128)}) %reduce-scatter.11.cloned.1.call-update) | async-done | bytes 73744 | tf_op jit(solution)/shard_map/reduce_scatter | solution.py:700
  588.6 46.3 %reduce-scatter.17.cloned.1.call-done = f32[96,768]{1,0:T(8,128)} async-done(((f32[768,768]{1,0:T(8,128)}), f32[96,768]{1,0:T(8,128)}) %reduce-scatter.17.cloned.1.call-update) | async-done | bytes 294928 | tf_op jit(solution)/shard_map/reduce_scatter | solution.py:706
  635.0 46.3 %reduce-scatter.19.cloned.1.call-done = f32[768,96]{0,1:T(8,128)} async-done(((f32[768,768]{0,1:T(8,128)}), f32[768,96]{0,1:T(8,128)}) %reduce-scatter.19.cloned.1.call-update) | async-done | bytes 294928 | tf_op jit(solution)/shard_map/reduce_scatter | solution.py:711
  (130 shorter events, 75.9 us)
Async XLA Ops:
  7.2 199.6 %all-reduce.18.cloned.1.call-start = ((), (), s32[]{:S(2)}) async-start(), calls=%async_computation.6 | async-start | bytes 4620288 | tf_op jit(solution)/shard_map/psum | solution.py:520
  91.7 6.7 copy-start.1
  102.5 7.1 %copy-start.3 = (bf16[1,750,768]{2,1,0:T(8,128)(2,1)S(1)}, bf16[1,750,768]{2,1,0:T(8,128)(2,1)}, u32[]{:S(2)}) copy-start(bf16[1,750,768]{2,1,0:T(8,128)(2,1)} %param.33) | copy-start | bytes 3456004
  102.5 7.1 %copy-start.19 = (bf16[8,2,48,768]{3,2,1,0:T(8,128)(2,1)S(1)}, bf16[8,2,48,768]{3,2,1,0:T(8,128)(2,1)}, u32[]{:S(2)}) copy-start(bf16[8,2,48,768]{3,2,1,0:T(8,128)(2,1)} %get-tuple-element.55) | copy-start | bytes 3538948
  115.1 213.0 %reduce-scatter.21.cloned.1.call-start = ((), (), s32[]{:S(2)}) async-start(), calls=%async_computation.12 | async-start | bytes 884736
  122.7 4.5 copy-start.23
  128.4 4.3 copy-start.4
  128.4 5.5 copy-start.20
  128.4 5.5 copy-start.24
  206.8 8.0 %copy-start.2 = (f32[3,750,1500]{2,1,0:T(8,128)S(1)}, f32[3,750,1500]{2,1,0:T(8,128)}, u32[]{:S(2)}) copy-start(f32[3,750,1500]{2,1,0:T(8,128)} %get-tuple-element.192) | copy-start | bytes 40500004
  212.9 22.4 %copy-start = (f32[750,768]{1,0:T(8,128)}, f32[750,768]{1,0:T(8,128)S(1)}, u32[]{:S(2)}) copy-start(f32[750,768]{1,0:T(8,128)S(1)} %get-tuple-element.156) | copy-start | bytes 6912004
  223.7 6.3 copy-start.12
  223.7 6.3 copy-start.13
  223.7 6.4 copy-start.14
  237.0 237.0 %all-reduce.20.cloned.1.call-start = ((), (), s32[]{:S(2)}) async-start(), calls=%async_computation.13 | async-start | bytes 9240576 | tf_op jit(solution)/shard_map/psum | solution.py:520
  300.7 3.8 copy-start.8
  300.7 3.8 copy-start.9
  300.7 3.8 copy-start.10
  306.5 206.1 %reduce-scatter.15.cloned.1.call-start = ((), (), s32[]{:S(2)}) async-start(), calls=%async_computation.9 | async-start | bytes 884736 | tf_op jit(solution)/shard_map/reduce_scatter | solution.py:702
  309.3 240.8 %reduce-scatter.13.cloned.1.call-start = ((), (), s32[]{:S(2)}) async-start(), calls=%async_computation.8 | async-start | bytes 884736 | tf_op jit(solution)/shard_map/reduce_scatter | solution.py:701
  312.5 276.1 %reduce-scatter.11.cloned.1.call-start = ((), (), s32[]{:S(2)}) async-start(), calls=%async_computation.7 | async-start | bytes 884736 | tf_op jit(solution)/shard_map/reduce_scatter | solution.py:700
  315.3 319.6 %reduce-scatter.17.cloned.1.call-start = ((), (), s32[]{:S(2)}) async-start(), calls=%async_computation.10 | async-start | bytes 2654208 | tf_op jit(solution)/shard_map/reduce_scatter | solution.py:706
  319.7 361.5 %reduce-scatter.19.cloned.1.call-start = ((), (), s32[]{:S(2)}) async-start(), calls=%async_computation.11 | async-start | bytes 2654208 | tf_op jit(solution)/shard_map/reduce_scatter | solution.py:711
  507.5 3.8 copy-start.6
  (10 other events, 23.7 us)
Sparse Core Ops, SparseCore 0:
  115.2 91.5 all-reduce.17
  237.1 36.4 reduce-scatter.20
  306.7 167.2 all-reduce.19
  477.6 33.9 reduce-scatter.14
  515.1 34.9 reduce-scatter.12
  553.7 34.9 reduce-scatter.10
  592.6 42.3 reduce-scatter.16
  638.9 42.3 reduce-scatter.18

commit v2 on v1

v2 whole, which is shorter than its diff:
```python
from functools import partial
import types

import jax
import jax.numpy as jnp
from jax import lax
from jax.experimental import pallas as pl
from jax.experimental.pallas import tpu as pltpu
from jax.sharding import PartitionSpec as P

HEAD_DIM = 64
EPS = 1e-05
F32 = jnp.float32
BF16 = jnp.bfloat16
MESH = pl.DeviceIdType.MESH


def flip(value, bit):
    return value + bit * (1 - 2 * lax.rem(lax.div(value, bit), 2))


def flips(value, mask, bits):
    for bit in bits:
        if mask & bit:
            value = flip(value, bit)
    return value


def powers(size):
    bits, bit = [], 1
    while bit < size:
        bits.append(bit)
        bit *= 2
    return bits


class Cube:
    def __init__(self, clips, seqs):
        self.clips, self.seqs, self.size = clips, seqs, clips * seqs
        self.seq_bits = [(bit, "seq", bit) for bit in powers(seqs)]
        self.clip_bits = [(bit * seqs, "clip", bit) for bit in powers(clips)]
        core, rest = self.clip_bits[:1], self.clip_bits[1:]
        self.orders = (
            self.seq_bits + rest + core,
            rest[:1] + self.seq_bits + rest[1:] + core,
        )
        self.all_bits = [bit for bit, _, _ in self.seq_bits + self.clip_bits]

    def rank(self):
        return lax.axis_index("clip") * self.seqs + lax.axis_index("seq")

    def block(self, mask):
        return flips(self.rank(), mask, self.all_bits)

    @staticmethod
    def peer(step):
        _, axis, bit = step
        return {axis: flip(lax.axis_index(axis), bit)}


class Sems:
    def __init__(self, send, recv):
        self.send, self.recv, self.used = send, recv, 0

    def take(self):
        self.used += 1
        return self.send.at[self.used - 1], self.recv.at[self.used - 1]


def remote(src, dst, sems, device):
    return pltpu.make_async_remote_copy(
        src_ref=src,
        dst_ref=dst,
        send_sem=sems[0],
        recv_sem=sems[1],
        device_id=device,
        device_id_type=MESH,
    )


class Gather:
    def __init__(self, cube, sems, view, colors):
        self.cube, self.view, self.colors = cube, view, colors
        self.steps = len(cube.orders[0])
        self.copies = [[[] for _ in range(self.steps)] for _ in range(colors)]
        for color in range(colors):
            masks = [0]
            for k, step in enumerate(cube.orders[color]):
                for mask in masks:
                    block = cube.block(mask)
                    piece = view(block, color)
                    self.copies[color][k].append(
                        remote(piece, piece, sems.take(), cube.peer(step))
                    )
                masks = masks + [mask ^ step[0] for mask in masks]

    def start(self, k):
        for color in range(self.colors):
            for copy in self.copies[color][k]:
                copy.start()

    def arrive(self, k):
        for color in range(self.colors):
            for copy in self.copies[color][k]:
                copy.wait_recv()

    def advance(self, k):
        for color in range(self.colors):
            for copy in self.copies[color][k]:
                copy.wait_recv()
            if k + 1 < self.steps:
                for copy in self.copies[color][k + 1]:
                    copy.start()

    def drain(self):
        for color in range(self.colors):
            for step in self.copies[color]:
                for copy in step:
                    copy.wait_send()


def normalize(rows):
    mean = jnp.mean(rows, axis=-1, keepdims=True)
    centered = rows - mean
    spread = jnp.mean(centered * centered, axis=-1, keepdims=True)
    inverse = lax.rsqrt(spread + EPS)
    return centered * inverse, inverse


def dot(a, b):
    return jnp.dot(a, b, preferred_element_type=F32)


def dot_nt(a, b):
    return lax.dot_general(a, b, (((1,), (1,)), ((), ())), preferred_element_type=F32)


def dot_tn(a, b):
    return lax.dot_general(a, b, (((0,), (0,)), ((), ())), preferred_element_type=F32)


NEG = -1e30


def fill(shape, value, dtype=F32):
    return jnp.full(shape, value, dtype)


def lane(shape):
    return lax.broadcasted_iota(jnp.int32, shape, len(shape) - 1)


class Line:
    def __init__(self, nodes, sems, view, parts):
        self.n, self.z = nodes, lax.axis_index("head")
        self.view = view
        self.right = [[sems.take() for _ in range(parts)] for _ in range(nodes - 1)]
        self.left = [[sems.take() for _ in range(parts)] for _ in range(nodes - 1)]

    def moves(self, hop, part):
        z, n = self.z, self.n

        def copy(origin, sems, target):
            piece = self.view(origin, part)
            return remote(piece, piece, sems, {"head": target})

        sends = (
            (
                (z >= hop) & (z < n - 1),
                lambda: copy(z - hop, self.right[hop][part], z + 1),
            ),
            (
                (n - 1 - z >= hop) & (z > 0),
                lambda: copy(z + hop, self.left[hop][part], z - 1),
            ),
        )
        arrivals = (
            (z > hop, lambda: copy(z - 1 - hop, self.right[hop][part], z - 1)),
            (n - 1 - z > hop, lambda: copy(z + 1 + hop, self.left[hop][part], z + 1)),
        )
        return sends, arrivals

    def start(self, hop, part):
        for condition, copy in self.moves(hop, part)[0]:
            pl.when(condition)(lambda copy=copy: copy().start())

    def arrive(self, hop, part):
        for condition, copy in self.moves(hop, part)[1]:
            pl.when(condition)(lambda copy=copy: copy().wait_recv())

    def drain(self, part):
        for hop in range(self.n - 1):
            for condition, copy in self.moves(hop, part)[0]:
                pl.when(condition)(lambda copy=copy: copy().wait_send())


def entry_barrier(cube, heads):
    barrier = pltpu.get_barrier_semaphore()
    z = lax.axis_index("head")
    peers = [cube.peer(step) for step in cube.orders[0]]
    peers += [{"head": lax.rem(z + d, heads)} for d in range(1, heads)]
    for peer in peers:
        pl.semaphore_signal(barrier, inc=1, device_id=peer, device_id_type=MESH)
    pl.semaphore_wait(barrier, len(peers))


def stage_one(m, cube, nz, sems):
    z = lax.axis_index("head")
    r = cube.rank()
    rows = m.wq.shape[0]
    colors = m.gq.shape[1]
    half = rows // colors
    nh = m.q.shape[0]
    frames = m.x.shape[0]
    padded = m.xp.shape[0]
    tile = 128
    tiles = padded // tile
    width = m.x.shape[1]

    gq = Gather(cube, sems, lambda b, c: m.gq.at[b, c], colors)
    gv = Gather(cube, sems, lambda b, c: m.gv.at[b], 1)
    g1 = Gather(cube, sems, lambda b, c: m.g1.at[b, c], colors)
    g2 = Gather(cube, sems, lambda b, c: m.g2.at[b, c], colors)
    go = Gather(cube, sems, lambda b, c: m.go.at[:, b, c], colors)

    m.gv[r] = m.vsh[...]
    for c in range(colors):
        part = pl.ds(c * half, half)
        for h in range(nh):
            cols = slice(h * HEAD_DIM, (h + 1) * HEAD_DIM)
            m.gq[r, c, :, h * 128 : h * 128 + 64] = m.wk[part, cols]
            m.gq[r, c, :, h * 128 + 64 : (h + 1) * 128] = m.wv[part, cols]
        m.gq[r, c, :, nh * 128 : nh * 128 + nh * 64] = m.wq[part, :]
        spare = m.gq.shape[3] - nh * 192
        if spare:
            m.gq[r, c, :, nh * 192 :] = fill((half, spare), 0, BF16)

    entry_barrier(cube, nz)
    gv.start(0)
    gq.start(0)

    wot = m.wo[...].T
    w2t = m.w2[...].T
    for c in range(colors):
        part = slice(c * half, (c + 1) * half)
        m.go[z, r, c] = wot[part]
        m.g2[r, c] = w2t[part]
        m.g1[r, c] = m.w1[part, :]
    out_sems = [sems.take() for _ in range(nz - 1)]

    def out_copies(arriving):
        for d in range(1, nz):
            origin = lax.rem(z + nz - d, nz) if arriving else z
            target = lax.rem(z + d, nz)
            piece = m.go.at[origin, r]
            yield remote(piece, piece, out_sems[d - 1], {"head": target})

    for copy in out_copies(False):
        copy.start()

    m.xp[0:frames] = m.x[...]
    m.xp[frames:padded] = fill((padded - frames, width), 0, BF16)

    def norm_tile(i, carry):
        at = pl.ds(pl.multiple_of(i * tile, tile), tile)
        xhat, _ = normalize(m.xp[at].astype(F32))
        m.xh2[at] = xhat
        return carry

    third = tiles // gq.steps
    for k in range(gq.steps):
        top = tiles if k == gq.steps - 1 else third * (k + 1)
        lax.fori_loop(third * k, top, norm_tile, 0)
        gv.advance(k)
        gq.advance(k)
    for b in range(cube.size):
        m.vec[:, b * rows : (b + 1) * rows] = m.gv[b, :, :rows]
    g1.start(0)
    g2.start(0)

    gain, shift = m.vec[0:1, :], m.vec[1:2, :]
    bias = m.bias[0:1, : m.gq.shape[3]]
    scale = HEAD_DIM**-0.5

    def project(i, carry):
        at = pl.ds(pl.multiple_of(i * tile, tile), tile)
        n1 = (m.xh2[at] * gain + shift).astype(BF16)
        m.n1[at] = n1
        packed = dot(n1, m.gq[...].reshape(cube.size * rows, m.gq.shape[3])) + bias
        left = lane((tile, 128)) < 64
        for h in range(nh):
            m.kv[0, h, at] = packed[:, h * 128 : (h + 1) * 128].astype(BF16)
            base = nh * 128 + (h // 2) * 128
            pair = packed[:, base : base + 128]
            if h % 2:
                pair = pltpu.roll(pair, 64, 1)
            pair = pair.astype(BF16).astype(F32) * scale
            m.q[h, at] = jnp.where(left, pair, 0.0).astype(BF16)
        return carry

    lax.fori_loop(0, tiles, project, 0)

    kv_sems = [sems.take() for _ in range(nh)]
    other = {"seq": flip(lax.axis_index("seq"), 1)}
    kv_copies = [
        remote(m.kv.at[0, h], m.kv.at[1, h], kv_sems[h], other) for h in range(nh)
    ]
    for copy in kv_copies:
        copy.start()
    for copy in out_copies(True):
        copy.wait_recv()
    go.start(0)

    left = lane((padded, 128)) < 64

    def prepare(part, h):
        block = m.kv[part, h]
        m.kvt[part, h] = block.T
        m.vo[part, h] = jnp.where(left, jnp.ones_like(block), block)

    for h in range(nh):
        prepare(0, h)

    line = Line(nz, sems, lambda origin, part: m.attz.at[origin, part], nh)
    block = 256
    valid = frames - (padded - 128)

    def attend(h):
        def one(b, carry):
            at = pl.ds(pl.multiple_of(b * block, block), block)
            query = m.q[h, at]
            keep = lane((block, 128)) < valid
            parts = []
            top = None
            for part in range(2):
                s = dot(query, m.kvt[part, h])
                body, tail = s[:, : padded - 128], s[:, padded - 128 :]
                tail = jnp.where(keep, tail, NEG)
                parts += [body, tail]
                high = jnp.maximum(jnp.max(body, axis=1, keepdims=True), jnp.max(tail, axis=1, keepdims=True))
                top = high if top is None else jnp.maximum(top, high)
            place = 0
            for s in parts:
                m.p[h, at, place : place + s.shape[1]] = jnp.exp(s - top).astype(BF16)
                place += s.shape[1]
            acc = dot(m.p[h, at, :padded], m.vo[0, h]) + dot(m.p[h, at, padded:], m.vo[1, h])
            inverse = 1.0 / pltpu.roll(acc, 64, 1)
            att = acc * inverse
            right = lane((block, 128)) >= 64
            m.il[h, at] = jnp.where(right, inverse, 0.0)
            m.atto[h, at] = jnp.where(right, att, 0.0).astype(BF16)
            turned = pltpu.roll(att, 64, 1)
            packed = jnp.where(right[: block // 2], att[block // 2 :], turned[: block // 2])
            to = pl.ds(pl.multiple_of(b * (block // 2), block // 2), block // 2)
            m.attz[z, h, to] = packed.astype(BF16)
            return carry

        lax.fori_loop(0, padded // block, one, 0)

    for h in range(nh):
        kv_copies[h].wait_recv()
        prepare(1, h)
        attend(h)
        line.start(0, h)
        if h < g1.steps:
            for g in (g1, g2, go):
                g.advance(h)
        if h:
            line.arrive(0, h - 1)
            line.start(1, h - 1)
        if h > 1:
            line.arrive(1, h - 2)
            line.start(2, h - 2)
    for k in range(min(nh, g1.steps), g1.steps):
        for g in (g1, g2, go):
            g.advance(k)
    for hop in range(nz - 1):
        for h in range(nh):
            done = nh - 1 - h
            if hop >= done:
                line.arrive(hop, h)
                if hop + 1 < nz - 1:
                    line.start(hop + 1, h)

    for copy in kv_copies:
        copy.wait_send()
    for copy in out_copies(False):
        copy.wait_send()
    for g in (gv, gq, g1, g2, go):
        g.drain()
    for h in range(nh):
        line.drain(h)


class Scatter:
    def __init__(self, cube, sems, buffer, landing, rows, colors):
        self.cube, self.buffer, self.landing = cube, buffer, landing
        self.rows, self.colors, self.half = rows, colors, rows // colors
        self.steps = len(cube.orders[0])
        self.plan = [[[] for _ in range(self.steps)] for _ in range(colors)]
        for color in range(colors):
            masks, slot = [0], 0
            for k, step in enumerate(cube.orders[color]):
                for mask in masks:
                    copy = remote(
                        self.view(cube.block(mask ^ step[0]), color),
                        landing.at[color, slot],
                        sems.take(),
                        cube.peer(step),
                    )
                    self.plan[color][k].append((mask, slot, copy))
                    slot += 1
                masks = masks + [mask ^ step[0] for mask in masks]

    def view(self, block, color):
        start = block * self.rows + color * self.half
        return self.buffer.at[pl.ds(pl.multiple_of(start, 8), self.half)]

    def start(self):
        self.left = self.steps - 1
        self.send(self.left)

    def step(self):
        if self.left > 0:
            self.advance(self.left)
            self.left -= 1

    def send(self, k):
        for color in range(self.colors):
            for _, _, copy in self.plan[color][k]:
                copy.start()

    def advance(self, k):
        for color in range(self.colors):
            for mask, slot, copy in self.plan[color][k]:
                copy.wait_recv()
                view = self.view(self.cube.block(mask), color)
                total = view[...].astype(F32) + self.landing[color, slot].astype(F32)
                view[...] = total.astype(BF16)
            for _, _, copy in self.plan[color][k - 1]:
                copy.start()

    def finish(self):
        while self.left > 0:
            self.step()
        parts = []
        for color in range(self.colors):
            ((_, slot, copy),) = self.plan[color][0]
            copy.wait_recv()
            view = self.view(self.cube.block(0), color)
            parts.append(view[...].astype(F32) + self.landing[color, slot].astype(F32))
        return parts[0] if len(parts) == 1 else jnp.concatenate(parts, axis=0)

    def drain(self):
        for color in range(self.colors):
            for step in self.plan[color]:
                for _, _, copy in step:
                    copy.wait_send()


class LineSum:
    def __init__(self, nz, send, recv, base, chunks, rows, part, landed, crossed, total):
        z = lax.axis_index("head")
        self.inner = (z > 0) & (z < nz - 1)
        self.mate, self.cross = {"head": flip(z, 1)}, {"head": nz - 1 - z}
        self.send_sem, self.recv_sem, self.base = send, recv, base
        self.chunks, self.rows = chunks, rows
        self.part, self.landed, self.crossed, self.total = part, landed, crossed, total

    def at(self, ref, i):
        return ref.at[pl.ds(pl.multiple_of(i * self.rows, self.rows), self.rows)]

    def sems(self, kind, i):
        place = self.base + kind * self.chunks + i
        return self.send_sem.at[place], self.recv_sem.at[place]

    def first(self, i):
        return remote(self.at(self.part, i), self.at(self.landed, i), self.sems(0, i), self.mate)

    def second(self, i):
        return remote(self.at(self.part, i), self.at(self.crossed, i), self.sems(1, i), self.cross)

    def third(self, i):
        piece = self.at(self.total, i)
        return remote(piece, piece, self.sems(2, i), self.mate)

    def offer(self, i):
        @pl.when(jnp.logical_not(self.inner))
        def _():
            self.first(i).start()

    def relay(self, i):
        @pl.when(self.inner)
        def _():
            self.first(i).wait_recv()
            view = self.at(self.part, i)
            total = view[...].astype(F32) + self.at(self.landed, i)[...].astype(F32)
            view[...] = total.astype(BF16)
            self.second(i).start()

    def ready(self, i):
        self.close(i)
        self.accept(i)

    def close(self, i):
        @pl.when(self.inner)
        def _():
            self.second(i).wait_recv()
            total = self.at(self.part, i)[...].astype(F32) + self.at(self.crossed, i)[...].astype(F32)
            self.at(self.total, i)[...] = total.astype(BF16)
            self.third(i).start()

    def accept(self, i):
        @pl.when(jnp.logical_not(self.inner))
        def _():
            self.third(i).wait_recv()

    def drain(self, i):
        @pl.when(self.inner)
        def _():
            self.second(i).wait_send()
            self.third(i).wait_send()

        @pl.when(jnp.logical_not(self.inner))
        def _():
            self.first(i).wait_send()


def loop(start, stop, step):
    lax.fori_loop(start, stop, lambda i, carry: (step(i), carry)[1], 0)


def rows_of(i, size):
    return pl.ds(pl.multiple_of(i * size, size), size)


def add_rows(m, row, values):
    count, width = values.shape
    m.acc[row, :, :width] += jnp.sum(values.reshape(count // 8, 8, width), axis=0)


B_FC_TWO, GAIN_TWO, SHIFT_TWO, B_OUT, GAIN_ONE, SHIFT_ONE, B_QKV, B_FC_ONE = range(8)
BLOCK = 256
CHUNK = 64


def stage_two(m, cube, nz, sum_two):
    padded, width = m.xp.shape
    rows = m.wq.shape[0]
    nh = m.q.shape[0]
    frames = m.cot.shape[0]
    hidden = m.w1.shape[1]
    m.gp[0:frames] = m.cot[...]
    m.gp[frames:padded] = fill((padded - frames, width), 0, BF16)
    m.acc[...] = fill(m.acc.shape, 0)
    gain, shift, b_out = m.vec[2:3, :], m.vec[3:4, :], m.vec[4:5, :]
    b_one = m.bias[1:2, :]
    per = BLOCK // CHUNK
    w_one = lambda: m.g1[...].reshape(cube.size * rows, hidden)
    w_two = lambda: m.g2[...].reshape(cube.size * rows, hidden)

    def block(b):
        at = rows_of(b, BLOCK)
        small = rows_of(b, BLOCK // 2)
        mid = m.xp[at].astype(F32) + b_out
        for zz in range(nz):
            pieces = [m.attz[zz, h, small] for h in range(nh)]
            top = jnp.concatenate([p[:, :64] for p in pieces], axis=1)
            low = jnp.concatenate([p[:, 64:] for p in pieces], axis=1)
            att = jnp.concatenate([top, low], axis=0)
            mid = mid + dot_nt(att, m.go[zz].reshape(cube.size * rows, nh * HEAD_DIM))
        xhat, inverse = normalize(mid)
        m.igrad[at] = mid
        m.xh2[at] = xhat
        m.r2[at] = jnp.broadcast_to(inverse, (BLOCK, 128))
        n2 = (xhat * gain + shift).astype(BF16)
        m.n2[at] = n2
        pre = dot(n2, w_one()) + b_one
        cdf = 0.5 + 0.5 * lax.erf(pre * 0.7071067811865476)
        act = (pre * cdf).astype(BF16)
        m.act[at] = act
        slope = cdf + pre * jnp.exp(pre * pre * -0.5) * 0.3989422804014327
        g = m.gp[at]
        add_rows(m, B_FC_TWO, g.astype(F32))
        gpre = (dot(g, w_two()) * slope).astype(BF16)
        m.gpre[at] = gpre
        add_rows(m, B_FC_ONE, gpre.astype(F32))
        back = dot_nt(gpre, w_one())
        add_rows(m, GAIN_TWO, back * m.xh2[at])
        add_rows(m, SHIFT_TWO, back)
        m.part[at] = back.astype(BF16)
        loop(0, per, lambda j: sum_two.offer(b * per + j))

        @pl.when(b > 0)
        def _():
            loop(0, per, lambda j: sum_two.relay((b - 1) * per + j))

        m.opart[at] = dot_nt(m.act[at], w_two()).astype(BF16)

    loop(0, padded // BLOCK, block)


def stage_three(m, cube, nz, sems, sum_two, sum_out, sum_one):
    z = lax.axis_index("head")
    padded, width = m.xp.shape
    rows = m.wq.shape[0]
    nh = m.q.shape[0]
    local = nh * HEAD_DIM
    colors = m.gq.shape[1]
    chunks = padded // CHUNK
    blocks = padded // BLOCK
    per = BLOCK // CHUNK
    scale = HEAD_DIM**-0.5
    packed = m.gq.shape[3]
    s1 = Scatter(cube, sems, m.dw1, m.dl1, rows, colors)
    s2 = Scatter(cube, sems, m.dw2, m.dl2, rows, colors)
    so = Scatter(cube, sems, m.dwo, m.dlo, rows, colors)
    sq = Scatter(cube, sems, m.dwq, m.dlq, rows, colors)
    tile = 128
    tiles = width // tile

    def product(left, right, into, columns):
        def one(i):
            cols = pl.ds(pl.multiple_of(i * tile, tile), tile)
            into[rows_of(i, tile)] = dot_tn(left[:, cols], right())[:, :columns].astype(BF16)

        return one

    one = product(m.n2, lambda: m.gpre[...], m.dw1, m.dw1.shape[1])

    def first(i):
        one(i)

        @pl.when(i < per)
        def _():
            sum_two.relay(chunks - per + i)

    loop(0, tiles, first)
    s1.start()
    loop(0, tiles, product(m.gp, lambda: m.act[...], m.dw2, m.dw2.shape[1]))
    s2.start()

    gain_two = m.vec[2:3, :]

    def middle(i):
        sum_two.ready(i)
        at = rows_of(i, CHUNK)
        n = m.total[at].astype(F32)
        e = n * gain_two
        xhat = m.xh2[at]
        r = m.r2[at][:, :1]
        mean = jnp.mean(e, axis=-1, keepdims=True)
        along = jnp.mean(e * xhat, axis=-1, keepdims=True)
        grad = m.gp[at].astype(F32) + r * (e - mean - xhat * along)
        m.xh2[at] = grad
        add_rows(m, B_OUT, grad)
        low = grad.astype(BF16)
        m.n2[at] = low
        da = dot(low, m.go[z].reshape(cube.size * rows, local)).astype(BF16).astype(F32)
        right = lane((CHUNK, 128)) >= 64
        for h in range(nh):
            base = (h // 2) * 128
            wide = da[:, base : min(base + 128, local)]
            if wide.shape[1] < 128:
                wide = jnp.concatenate([wide, jnp.zeros((CHUNK, 128 - wide.shape[1]), F32)], axis=1)
            if h % 2 == 0:
                wide = pltpu.roll(wide, 64, 1)
            m.act[at, h * 128 : (h + 1) * 128] = jnp.where(right, wide * m.il[h, at], 0.0).astype(BF16)
            m.at[at, h * 64 : (h + 1) * 64] = m.atto[h, at][:, 64:]

    third = chunks // 3
    loop(0, third, middle)
    s1.step()
    s2.step()
    loop(third, 2 * third, middle)
    s1.step()
    s2.step()
    loop(2 * third, chunks, middle)
    loop(0, tiles, product(m.n2, lambda: m.at[...], m.dwo, local))
    so.start()

    for h in range(nh):
        m.qt[h] = m.q[h].T
        m.dat[h] = m.act[:, h * 128 : (h + 1) * 128].T
    big = padded // sum_out.rows
    loop(0, big, sum_out.offer)
    kv_sems = [sems.take() for _ in range(nh)]
    other = {"seq": flip(lax.axis_index("seq"), 1)}
    kv_copies = [remote(m.kvs.at[h], m.kvr.at[h], kv_sems[h], other) for h in range(nh)]
    for h in range(nh):
        m.dkv[0, h] = fill((128, padded), 0)
        m.dkv[1, h] = fill((128, padded), 0)

        def back(b, h=h):
            at = rows_of(b, BLOCK)
            da = m.act[at, h * 128 : (h + 1) * 128]
            inner = jnp.sum(da.astype(F32) * m.atto[h, at].astype(F32), axis=1, keepdims=True)
            for part in (1, 0):
                keys = slice(part * padded, (part + 1) * padded)
                dp = dot(da, m.kvt[part, h])
                p = m.p[h, at, keys]
                ds = (p.astype(F32) * (dp - inner)).astype(BF16)
                m.ds[:, keys] = ds
                m.dkv[part, h] += dot(m.qt[h, :, at], m.ds[:, keys]) + dot(m.dat[h, :, at], p)
            dq = dot(m.ds[:, :padded], m.kv[0, h]) + dot(m.ds[:, padded:], m.kv[1, h])
            dq = (dq * scale)[:, :64].astype(BF16)
            m.gpre[at, nh * 128 + h * 64 : nh * 128 + (h + 1) * 64] = dq
            point = h * blocks + b

            @pl.when((point >= 2) & (point < 2 + big))
            def _():
                sum_out.relay(point - 2)

            @pl.when((point >= 5) & (point < 5 + big))
            def _():
                sum_out.close(point - 5)

        loop(0, blocks, back)
        m.kvs[h] = m.dkv[1, h].astype(BF16)
        kv_copies[h].start()
        if h == 0:
            so.step()
        if h == 1:
            so.step()
    points = nh * blocks
    for i in range(max(0, points - 2), big):
        sum_out.relay(i)
    for i in range(max(0, points - 5), big):
        sum_out.close(i)
    spare = packed - nh * 192
    if spare:
        m.gpre[:, nh * 192 : packed] = fill((padded, spare), 0, BF16)
    for h in range(nh):
        kv_copies[h].wait_recv()
        total = m.dkv[0, h] + m.kvr[h].astype(F32)
        m.gpre[:, h * 128 : (h + 1) * 128] = total.T.astype(BF16)

    def last(b):
        at = rows_of(b, BLOCK)
        grads = m.gpre[at, :packed]
        add_rows(m, B_QKV, grads.astype(F32))
        back = dot_nt(grads, m.gq[...].reshape(cube.size * rows, packed))
        xhat, _ = normalize(m.xp[at].astype(F32))
        add_rows(m, GAIN_ONE, back * xhat)
        add_rows(m, SHIFT_ONE, back)
        m.part[at] = back.astype(BF16)
        loop(0, per, lambda j: sum_one.offer(b * per + j))

        @pl.when(b > 0)
        def _():
            loop(0, per, lambda j: sum_one.relay((b - 1) * per + j))

    loop(0, chunks, sum_two.drain)
    loop(0, blocks, last)
    one_q = product(m.n1, lambda: m.gpre[:, :packed], m.dwq, packed)

    def qkv(i):
        one_q(i)

        @pl.when(i < per)
        def _():
            sum_one.relay(chunks - per + i)

    loop(0, tiles, qkv)
    sq.start()

    for row in range(8):
        m.vs[row : row + 1, :] = jnp.sum(m.acc[row], axis=0, keepdims=True)
    vec_steps = [(cube.peer(step), False) for step in cube.orders[0]]
    vec_steps += [({"head": flip(z, bit)}, True) for bit in powers(nz)]
    row_id = lax.broadcasted_iota(jnp.int32, m.vs.shape, 0)
    partial_rows = (row_id == GAIN_TWO) | (row_id == SHIFT_TWO) | (row_id == GAIN_ONE) | (row_id == SHIFT_ONE)
    vec_copies = []

    def vec_send(k):
        if k < len(vec_steps):
            m.vo_[k] = m.vs[...]
            copy = remote(m.vo_.at[k], m.vr.at[k], sems.take(), vec_steps[k][0])
            copy.start()
            vec_copies.append(copy)

    def vec_take(k):
        if k < len(vec_steps):
            vec_copies[k].wait_recv()
            arrived = m.vr[k]
            if vec_steps[k][1]:
                arrived = jnp.where(partial_rows, arrived, 0.0)
            m.vs[...] += arrived
            vec_send(k + 1)

    vec_send(0)
    b_two = m.vec[5:6, :]

    def output(i):
        sum_out.accept(i)
        at = rows_of(i, sum_out.rows)
        m.ototal[at] = (m.igrad[at] + m.ototal[at].astype(F32) + b_two).astype(BF16)

    gain_one = m.vec[0:1, :]

    def final(i):
        sum_one.ready(i)
        at = rows_of(i, CHUNK)
        e = m.total[at].astype(F32) * gain_one
        xhat, r = normalize(m.xp[at].astype(F32))
        mean = jnp.mean(e, axis=-1, keepdims=True)
        along = jnp.mean(e * xhat, axis=-1, keepdims=True)
        m.igrad[at] = m.xh2[at] + r * (e - mean - xhat * along)

    loop(0, big, sum_out.drain)
    loop(0, big, output)
    m.ow1[...] = s1.finish()
    m.ow2[...] = s2.finish().T
    m.owo[...] = so.finish().T
    vec_take(0)
    sq.step()
    loop(0, third, final)
    vec_take(1)
    sq.step()
    vec_take(2)
    loop(third, 2 * third, final)
    vec_take(3)
    got = sq.finish()
    for h in range(nh):
        cols = slice(h * HEAD_DIM, (h + 1) * HEAD_DIM)
        m.owk[:, cols] = got[:, h * 128 : h * 128 + 64]
        m.owv[:, cols] = got[:, h * 128 + 64 : (h + 1) * 128]
    m.owq[...] = got[:, nh * 128 : nh * 128 + local]
    vec_take(4)
    for k in range(5, len(vec_steps)):
        vec_take(k)
    m.ovec[...] = m.vs[...]
    loop(2 * third, chunks, final)

    for copy in kv_copies + vec_copies:
        copy.wait_send()
    for s in (s1, s2, so, sq):
        s.drain()
    loop(0, chunks, sum_one.drain)


def layer(inputs, cotangent, vectors, biases, w_query, w_key, w_value, w_out, w_fc_one, w_fc_two, mesh_shape):
    nz = mesh_shape["head"]
    cube = Cube(mesh_shape["clip"], mesh_shape["seq"])
    frames, width = inputs.shape
    rows, local = w_query.shape
    hidden = w_fc_one.shape[1]
    nh = local // HEAD_DIM
    padded = -(-frames // BLOCK) * BLOCK
    colors = 2 if rows % 32 == 0 else 1
    half = rows // colors
    packed = -(-(nh * 192) // 128) * 128
    nb = cube.size
    steps = len(cube.all_bits) + len(powers(nz))
    ins = dict(
        x=inputs,
        cot=cotangent,
        vsh=vectors,
        bias=biases,
        wq=w_query,
        wk=w_key,
        wv=w_value,
        wo=w_out,
        w1=w_fc_one,
        w2=w_fc_two,
    )
    outs = dict(
        ototal=((padded, width), BF16),
        igrad=((padded, width), F32),
        ovec=((8, width), F32),
        owq=((rows, local), F32),
        owk=((rows, local), F32),
        owv=((rows, local), F32),
        owo=((local, rows), F32),
        ow1=((rows, hidden), F32),
        ow2=((hidden, rows), F32),
    )
    flat = (padded, width)
    scratch = dict(
        gq=((nb, colors, half, packed), BF16),
        go=((nz, nb, colors, half, local), BF16),
        g1=((nb, colors, half, hidden), BF16),
        g2=((nb, colors, half, hidden), BF16),
        gv=((nb, 8, 128), F32),
        vec=((8, width), F32),
        n1=(flat, BF16),
        q=((nh, padded, 128), BF16),
        kv=((2, nh, padded, 128), BF16),
        kvt=((2, nh, 128, padded), BF16),
        vo=((2, nh, padded, 128), BF16),
        p=((nh, padded, 2 * padded), BF16),
        il=((nh, padded, 128), F32),
        atto=((nh, padded, 128), BF16),
        attz=((nz, nh, padded // 2, 128), BF16),
        xp=(flat, BF16),
        gp=(flat, BF16),
        xh2=(flat, F32),
        r2=((padded, 128), F32),
        n2=(flat, BF16),
        act=((padded, hidden), BF16),
        gpre=((padded, hidden), BF16),
        acc=((8, 8, width), F32),
        vs=((8, width), F32),
        vo_=((steps, 8, width), F32),
        vr=((steps, 8, width), F32),
        part=(flat, BF16),
        landed=(flat, BF16),
        crossed=(flat, BF16),
        crossed_one=(flat, BF16),
        total=(flat, BF16),
        opart=(flat, BF16),
        olanded=(flat, BF16),
        ocrossed=(flat, BF16),
        at=((padded, local), BF16),
        qt=((nh, 128, padded), BF16),
        dat=((nh, 128, padded), BF16),
        dkv=((2, nh, 128, padded), F32),
        kvs=((nh, 128, padded), BF16),
        kvr=((nh, 128, padded), BF16),
        ds=((BLOCK, 2 * padded), BF16),
        dw1=((width, hidden), BF16),
        dl1=((colors, nb - 1, half, hidden), BF16),
        dw2=((width, hidden), BF16),
        dl2=((colors, nb - 1, half, hidden), BF16),
        dwo=((width, local), BF16),
        dlo=((colors, nb - 1, half, local), BF16),
        dwq=((width, packed), BF16),
        dlq=((colors, nb - 1, half, packed), BF16),
    )
    small, large = padded // CHUNK, padded // 128
    lines = 3 * (2 * small + large)
    count = lines + 9 * colors * (nb - 1) + 60

    def body(*refs):
        names = list(ins) + list(outs) + list(scratch)
        m = types.SimpleNamespace(**dict(zip(names, refs)))
        send, recv = refs[len(names) :]
        sems = Sems(send, recv)
        sems.used = lines
        sum_two = LineSum(nz, send, recv, 0, small, CHUNK, m.part, m.landed, m.crossed, m.total)
        sum_one = LineSum(nz, send, recv, 3 * small, small, CHUNK, m.part, m.landed, m.crossed_one, m.total)
        sum_out = LineSum(nz, send, recv, 6 * small, large, 128, m.opart, m.olanded, m.ocrossed, m.ototal)
        stage_one(m, cube, nz, sems)
        stage_two(m, cube, nz, sum_two)
        stage_three(m, cube, nz, sems, sum_two, sum_out, sum_one)
        assert sems.used <= count, (sems.used, count)

    res = pl.pallas_call(
        body,
        out_shape=[jax.ShapeDtypeStruct(*v) for v in outs.values()],
        in_specs=[pl.BlockSpec(memory_space=pltpu.VMEM)] * len(ins),
        out_specs=[pl.BlockSpec(memory_space=pltpu.VMEM)] * len(outs),
        scratch_shapes=[pltpu.VMEM(*v) for v in scratch.values()] + [pltpu.SemaphoreType.DMA((count,))] * 2,
        compiler_params=pltpu.CompilerParams(
            collective_id=0, has_side_effects=True, vmem_limit_bytes=67_043_328
        ),
        name="layer",
    )(*ins.values())
    return types.SimpleNamespace(**dict(zip(outs, res)))


def vector_pack(vectors):
    stack = jnp.stack([v.astype(F32) for v in vectors])
    return jnp.pad(stack, ((0, 8 - stack.shape[0]), (0, 128 - stack.shape[1])))


def biases_pack(b_query, b_value, b_fc_one, heads):
    zero = jnp.zeros((HEAD_DIM,), F32)
    parts = []
    for h in range(heads):
        parts += [zero, b_value[h * HEAD_DIM : (h + 1) * HEAD_DIM].astype(F32)]
    row = jnp.concatenate(parts + [b_query.astype(F32)])
    width = b_fc_one.shape[0]
    row = jnp.pad(row, (0, width - row.shape[0]))
    return jnp.pad(jnp.stack([row, b_fc_one.astype(F32)]), ((0, 6), (0, 0)))


def on_device(
    inputs,
    gain_one,
    shift_one,
    w_query,
    b_query,
    w_key,
    w_value,
    b_value,
    w_out,
    b_out,
    gain_two,
    shift_two,
    w_fc_one,
    b_fc_one,
    w_fc_two,
    b_fc_two,
    cotangent,
    mesh_shape,
):
    clips, frames, width = inputs.shape
    count = clips * frames
    local = w_query.shape[1]
    heads = local // HEAD_DIM
    share = gain_one.shape[0]
    vectors = vector_pack((gain_one, shift_one, gain_two, shift_two, b_out, b_fc_two))
    biases = biases_pack(b_query, b_value, b_fc_one, heads)
    res = layer(
        inputs.reshape(count, width),
        cotangent.reshape(count, width),
        vectors,
        biases,
        w_query,
        w_key,
        w_value,
        w_out,
        w_fc_one,
        w_fc_two,
        mesh_shape,
    )
    rank = lax.axis_index("clip") * mesh_shape["seq"] + lax.axis_index("seq")
    owned = lax.dynamic_slice_in_dim(res.ovec, rank * share, share, axis=1)
    qkv = res.ovec[B_QKV]
    b_values = jnp.concatenate([qkv[h * 128 + 64 : (h + 1) * 128] for h in range(heads)])
    return (
        res.ototal[:count].reshape(clips, frames, width),
        res.igrad[:count].reshape(clips, frames, width),
        owned[GAIN_ONE],
        owned[SHIFT_ONE],
        res.owq,
        qkv[heads * 128 : heads * 128 + local],
        res.owk,
        res.owv,
        b_values,
        res.owo,
        owned[B_OUT],
        owned[GAIN_TWO],
        owned[SHIFT_TWO],
        res.ow1,
        res.ovec[B_FC_ONE],
        res.ow2,
        owned[B_FC_TWO],
    )


def solution(mesh):
    group = ("clip", "seq")
    rows, columns, own, heads = P(group, "head"), P("head", group), P(group), P("head")
    tokens = P("clip", "seq", None)
    return jax.shard_map(
        partial(on_device, mesh_shape=dict(mesh.shape)),
        mesh=mesh,
        in_specs=(
            tokens, own, own, rows, heads, rows, rows, heads, columns,
            own, own, own, rows, heads, columns, own, tokens,
        ),
        out_specs=(
            tokens, tokens, own, own, rows, heads, rows, rows, heads,
            columns, own, own, own, rows, heads, columns, own,
        ),
        check_vma=False,
    )
```

time: 698 us -> 239 us (0.34); the launches traced: 688 us -> 239 us
  waiting for transfers between devices: 373 us -> 0 us
  Pallas kernels: 69.8 us -> 215 us
  blocking collectives: 86.9 us -> 0 us
  matrix products: 67.4 us -> 0 us
  other arithmetic: 31 us -> 2.7 us
  local copies, waits for them, and re-layouts: 43.6 us -> 20.2 us
  between operations: 16.1 us -> 0.74 us
    psum x2 -> x0, waiting for transfers between devices: 204 us -> none  [head_total(): return lax.psum(partial_sum, 'head')]
    reduce_scatter x5 -> x0, waiting for transfers between devices: 169 us -> none  [the longest x1 46.3 us: on_device(): lax.psum_scatter(grad_w_fc_one, ('clip', 'seq'), scatter_dimension=0, til...]
    pallas_call x1, Pallas kernels: 69.8 us -> 215 us  [layer(): pl.pallas_call(body, out_shape=[jax.ShapeDtypeStruct(*v) for v in outs.va...]
    unnamed x2 -> x0, blocking collectives: 86.9 us -> none
    dot_general x18 -> x0, matrix products: 55.4 us -> none  [the longest x1 7.11 us: on_device(): jnp.dot(normed_two, full_fc_one, preferred_element_type=gathered_rows)]
    reduce_sum x8 -> x0, other arithmetic: 12.7 us -> none  [the longest x1 3.34 us: on_device(): grad_b_out = jnp.sum(middle_gradient, axis=0)]
    sub x1 -> x0, matrix products: 10.3 us -> none  [attend_back(): probs = jax.nn.softmax(scores, axis=-1)]
    convert_element_type x2 -> x0, other arithmetic: 7 us -> none  [the longest x1 6.32 us: attend_back(): grad_scores = (probs * (grad_probs - inner)).astype(jnp.bfloat16)]
  transfers between devices with their start and end apart: 8 -> 0, of which waited for: 6 -> 0; matrix products, arithmetic and copies ran while one was open for 11% -> 0% of each run, Pallas kernels for 0% -> 0%
where the time goes in v2:
time: 239 us
  Pallas kernels  215 us (90%)
  local copies, waits for them, and re-layouts  20.2 us (8%)
  other arithmetic  2.7 us (1%)
    pallas_call x1, Pallas kernels, layer(): pl.pallas_call(body, out_shape=[jax.ShapeDtypeStruct(*v) for v in outs.va...  215 us
    unnamed x20, local copies, waits for them, and re-layouts  10.6 us

profile of v2, /device:TPU:0, one launch (start us, length us, event | category | flops | bytes accessed | tf_op | source)
XLA Modules:
  0.0 239.0 jit_solution(6152555650647425122)
XLA Ops:
  0.7 0.8 slice_convert_fusion
  1.5 0.7 concatenate.6
  2.3 0.8 stack.46
  3.0 0.6 pad_convert_fusion.refs_2_
  3.6 0.7 reshape.54
  4.3 0.6 select_maximum_fusion.refs_3_
  4.9 1.7 copy.34.refs_9_
  6.6 215.4 %layer.1 = (bf16[768,768]{1,0:T(8,128)(2,1)}, f32[768,768]{1,0:T(8,128)}, f32[8,768]{1,0:T(8,128)}, f32[96,192]{1,0:T(8,128)}, f32[96,192]{1,0:T(8,128)}, /*inde...) custom-call(bf16[750,768]{1,0:T(8,128)(2,1)} %bitcast.31, bf16[750,768]{1,0:T(8,128)(2,1)} %bitcast.32, ...), custom_call_target="tpu_custom_call" | custom-call | tf_op jit(solution)/shard_map/layer/pallas_call | solution.py:948
  222.1 2.5 %slice_bitcast_fusion.1 = bf16[1,750,768]{2,1,0:T(8,128)(2,1)} fusion(bf16[768,768]{1,0:T(8,128)(2,1)} %get-tuple-element.26), kind=kLoop, calls=%fused_computation.1 | loop fusion | bytes 2304000 | tf_op jit(solution)/shard_map/reshape | solution.py:1023
  224.6 1.3 slice.72
  225.9 0.8 slice_bitcast_fusion.8
  226.6 0.6 pad_maximum_fusion
  227.3 0.8 constant_dynamic-slice_fusion
  228.0 1.3 slice_reduce_fusion
  229.4 0.5 slice_bitcast_fusion.2
  229.9 1.9 copy.36
  231.8 0.1 slice_bitcast_fusion
  231.9 0.0 copy-start.5
  232.0 3.8 %copy.35 = f32[1,750,768]{2,0,1:T(1,128)} copy(f32[1,750,768]{2,1,0:T(8,128)S(1)} %slice_bitcast_fusion) | data formatting | bytes 4608000
  235.7 0.6 copy.42
  236.4 0.6 copy.43
  237.0 0.6 copy.44
  237.7 0.6 copy.45
  238.3 0.7 copy.46
  (14 shorter events, 0.0 us)
Async XLA Ops:
  222.1 9.7 %copy-start = (f32[768,768]{1,0:T(8,128)S(1)}, f32[768,768]{1,0:T(8,128)}, u32[]{:S(2)}) copy-start(f32[768,768]{1,0:T(8,128)} %get-tuple-element.27) | copy-start | bytes 7077892
  231.9 3.8 %copy-start.5 = (f32[96,192]{1,0:T(8,128)S(1)}, f32[96,192]{1,0:T(8,128)}, u32[]{:S(2)}) copy-start(f32[96,192]{1,0:T(8,128)} %get-tuple-element.85) | copy-start | bytes 221188
  231.9 4.4 %copy-start.4 = (f32[96,192]{1,0:T(8,128)S(1)}, f32[96,192]{1,0:T(8,128)}, u32[]{:S(2)}) copy-start(f32[96,192]{1,0:T(8,128)} %get-tuple-element.87) | copy-start | bytes 221188
  232.0 5.1 %copy-start.3 = (f32[96,192]{1,0:T(8,128)S(1)}, f32[96,192]{1,0:T(8,128)}, u32[]{:S(2)}) copy-start(f32[96,192]{1,0:T(8,128)} %get-tuple-element.88) | copy-start | bytes 221188
  232.0 5.7 %copy-start.2 = (f32[192,96]{1,0:T(8,128)S(1)}, f32[192,96]{1,0:T(8,128)}, u32[]{:S(2)}) copy-start(f32[192,96]{1,0:T(8,128)} %get-tuple-element.90) | copy-start | bytes 221188
  232.0 6.3 %copy-start.1 = (f32[96,768]{1,0:T(8,128)S(1)}, f32[96,768]{1,0:T(8,128)}, u32[]{:S(2)}) copy-start(f32[96,768]{1,0:T(8,128)} %get-tuple-element.94) | copy-start | bytes 884740

commit v3 on v2

--- a/solution.py
+++ b/solution.py
@@ -94,23 +94,15 @@
                     )
                 masks = masks + [mask ^ step[0] for mask in masks]
 
-    def start(self, k):
-        for color in range(self.colors):
-            for copy in self.copies[color][k]:
-                copy.start()
-
-    def arrive(self, k):
-        for color in range(self.colors):
-            for copy in self.copies[color][k]:
-                copy.wait_recv()
-
-    def advance(self, k):
-        for color in range(self.colors):
-            for copy in self.copies[color][k]:
-                copy.wait_recv()
-            if k + 1 < self.steps:
-                for copy in self.copies[color][k + 1]:
-                    copy.start()
+    def start(self, k, color):
+        for copy in self.copies[color][k]:
+            copy.start()
+
+    def advance(self, k, color):
+        for copy in self.copies[color][k]:
+            copy.wait_recv()
+        if k + 1 < self.steps:
+            self.start(k + 1, color)
 
     def drain(self):
         for color in range(self.colors):
@@ -223,7 +215,10 @@
     g2 = Gather(cube, sems, lambda b, c: m.g2.at[b, c], colors)
     go = Gather(cube, sems, lambda b, c: m.go.at[:, b, c], colors)
 
-    m.gv[r] = m.vsh[...]
+    m.vec[...] = fill(m.vec.shape, 0)
+    for row, ref in enumerate(m.shares):
+        m.vec[row : row + 1, :rows] = ref[...].astype(F32)
+    m.gv[r] = m.vec[:, :128]
     for c in range(colors):
         part = pl.ds(c * half, half)
         for h in range(nh):
@@ -234,18 +229,17 @@
         spare = m.gq.shape[3] - nh * 192
         if spare:
             m.gq[r, c, :, nh * 192 :] = fill((half, spare), 0, BF16)
+        m.g2[r, c] = m.w2[part, :]
+        m.g1[r, c] = m.w1[part, :]
 
     entry_barrier(cube, nz)
-    gv.start(0)
-    gq.start(0)
+    gv.start(0, 0)
+    for c in range(colors):
+        gq.start(0, c)
 
     wot = m.wo[...].T
-    w2t = m.w2[...].T
     for c in range(colors):
-        part = slice(c * half, (c + 1) * half)
-        m.go[z, r, c] = wot[part]
-        m.g2[r, c] = w2t[part]
-        m.g1[r, c] = m.w1[part, :]
+        m.go[z, r, c] = wot[c * half : (c + 1) * half]
     out_sems = [sems.take() for _ in range(nz - 1)]
 
     def out_copies(arriving):
@@ -257,6 +251,9 @@
 
     for copy in out_copies(False):
         copy.start()
+    for c in range(1, colors):
+        g1.start(0, c)
+        g2.start(0, c)
 
     m.xp[0:frames] = m.x[...]
     m.xp[frames:padded] = fill((padded - frames, width), 0, BF16)
@@ -271,15 +268,18 @@
     for k in range(gq.steps):
         top = tiles if k == gq.steps - 1 else third * (k + 1)
         lax.fori_loop(third * k, top, norm_tile, 0)
-        gv.advance(k)
-        gq.advance(k)
+        gv.advance(k, 0)
+        for c in range(colors):
+            gq.advance(k, c)
     for b in range(cube.size):
         m.vec[:, b * rows : (b + 1) * rows] = m.gv[b, :, :rows]
-    g1.start(0)
-    g2.start(0)
-
     gain, shift = m.vec[0:1, :], m.vec[1:2, :]
-    bias = m.bias[0:1, : m.gq.shape[3]]
+    m.bias[...] = fill(m.bias.shape, 0)
+    bv = m.bv[...].astype(F32)[None, :]
+    for h in range(nh):
+        m.bias[0:1, h * 128 + 64 : (h + 1) * 128] = bv[:, h * HEAD_DIM : (h + 1) * HEAD_DIM]
+    m.bias[0:1, nh * 128 : nh * 192] = m.bq[...].astype(F32)[None, :]
+    bias = m.bias[0:1, :]
     scale = HEAD_DIM**-0.5
 
     def project(i, carry):
@@ -305,11 +305,15 @@
     kv_copies = [
         remote(m.kv.at[0, h], m.kv.at[1, h], kv_sems[h], other) for h in range(nh)
     ]
-    for copy in kv_copies:
-        copy.start()
     for copy in out_copies(True):
         copy.wait_recv()
-    go.start(0)
+    for c in range(1, colors):
+        go.start(0, c)
+    kv_copies[0].start()
+    for g in (g1, g2, go):
+        g.start(0, 0)
+    for copy in kv_copies[1:]:
+        copy.start()
 
     left = lane((padded, 128)) < 64
 
@@ -357,30 +361,39 @@
 
         lax.fori_loop(0, padded // block, one, 0)
 
+    def weights(k, c):
+        if c < colors and k < g1.steps:
+            for g in (g1, g2, go):
+                g.advance(k, c)
+
     for h in range(nh):
         kv_copies[h].wait_recv()
         prepare(1, h)
         attend(h)
         line.start(0, h)
-        if h < g1.steps:
-            for g in (g1, g2, go):
-                g.advance(h)
-        if h:
+        if h == 0:
+            weights(0, 1)
+        if h >= 1:
             line.arrive(0, h - 1)
             line.start(1, h - 1)
-        if h > 1:
+        if h == 1:
+            weights(0, 0)
+        if h >= 2:
             line.arrive(1, h - 2)
             line.start(2, h - 2)
-    for k in range(min(nh, g1.steps), g1.steps):
-        for g in (g1, g2, go):
-            g.advance(k)
     for hop in range(nz - 1):
         for h in range(nh):
             done = nh - 1 - h
             if hop >= done:
+                if hop == nz - 2 and h == 1:
+                    weights(1, 0)
+                    weights(1, 1)
                 line.arrive(hop, h)
                 if hop + 1 < nz - 1:
                     line.start(hop + 1, h)
+    for k in range(2, g1.steps):
+        for c in range(colors):
+            weights(k, c)
 
     for copy in kv_copies:
         copy.wait_send()
@@ -498,9 +511,14 @@
             view[...] = total.astype(BF16)
             self.second(i).start()
 
-    def ready(self, i):
-        self.close(i)
-        self.accept(i)
+    def pump(self, i):
+        @pl.when(i < self.chunks)
+        def _():
+            self.relay(i)
+
+        @pl.when(i >= LAG)
+        def _():
+            self.close(i - LAG)
 
     def close(self, i):
         @pl.when(self.inner)
@@ -541,10 +559,11 @@
 
 B_FC_TWO, GAIN_TWO, SHIFT_TWO, B_OUT, GAIN_ONE, SHIFT_ONE, B_QKV, B_FC_ONE = range(8)
 BLOCK = 256
-CHUNK = 64
-
-
-def stage_two(m, cube, nz, sum_two):
+CHUNK = 32
+LAG = 4
+
+
+def stage_two(m, cube, nz, sum_two, sum_out):
     padded, width = m.xp.shape
     rows = m.wq.shape[0]
     nh = m.q.shape[0]
@@ -554,7 +573,7 @@
     m.gp[frames:padded] = fill((padded - frames, width), 0, BF16)
     m.acc[...] = fill(m.acc.shape, 0)
     gain, shift, b_out = m.vec[2:3, :], m.vec[3:4, :], m.vec[4:5, :]
-    b_one = m.bias[1:2, :]
+    b_one = m.bf1[...].astype(F32)[None, :]
     per = BLOCK // CHUNK
     w_one = lambda: m.g1[...].reshape(cube.size * rows, hidden)
     w_two = lambda: m.g2[...].reshape(cube.size * rows, hidden)
@@ -570,7 +589,7 @@
             att = jnp.concatenate([top, low], axis=0)
             mid = mid + dot_nt(att, m.go[zz].reshape(cube.size * rows, nh * HEAD_DIM))
         xhat, inverse = normalize(mid)
-        m.igrad[at] = mid
+        m.mid[at] = mid
         m.xh2[at] = xhat
         m.r2[at] = jnp.broadcast_to(inverse, (BLOCK, 128))
         n2 = (xhat * gain + shift).astype(BF16)
@@ -590,14 +609,10 @@
         add_rows(m, SHIFT_TWO, back)
         m.part[at] = back.astype(BF16)
         loop(0, per, lambda j: sum_two.offer(b * per + j))
-
-        @pl.when(b > 0)
-        def _():
-            loop(0, per, lambda j: sum_two.relay((b - 1) * per + j))
-
         m.opart[at] = dot_nt(m.act[at], w_two()).astype(BF16)
 
     loop(0, padded // BLOCK, block)
+    loop(0, sum_out.chunks, sum_out.offer)
 
 
 def stage_three(m, cube, nz, sems, sum_two, sum_out, sum_one):
@@ -627,23 +642,24 @@
         return one
 
     one = product(m.n2, lambda: m.gpre[...], m.dw1, m.dw1.shape[1])
+    two = product(m.gp, lambda: m.act[...], m.dw2, m.dw2.shape[1])
 
     def first(i):
         one(i)
-
-        @pl.when(i < per)
-        def _():
-            sum_two.relay(chunks - per + i)
+        sum_two.pump(i)
+
+    def second(i):
+        two(i)
+        sum_two.pump(tiles + i)
 
     loop(0, tiles, first)
     s1.start()
-    loop(0, tiles, product(m.gp, lambda: m.act[...], m.dw2, m.dw2.shape[1]))
+    loop(0, tiles, second)
     s2.start()
-
     gain_two = m.vec[2:3, :]
 
     def middle(i):
-        sum_two.ready(i)
+        sum_two.accept(i)
         at = rows_of(i, CHUNK)
         n = m.total[at].astype(F32)
         e = n * gain_two
@@ -668,22 +684,28 @@
             m.act[at, h * 128 : (h + 1) * 128] = jnp.where(right, wide * m.il[h, at], 0.0).astype(BF16)
             m.at[at, h * 64 : (h + 1) * 64] = m.atto[h, at][:, 64:]
 
-    third = chunks // 3
-    loop(0, third, middle)
+    ahead = 2 * tiles
+
+    def pumped(i):
+        sum_two.pump(i + ahead)
+        middle(i)
+
+    stop = chunks + LAG - ahead
     s1.step()
-    s2.step()
-    loop(third, 2 * third, middle)
-    s1.step()
-    s2.step()
-    loop(2 * third, chunks, middle)
+    fourth = stop // 4
+    for part in range(4):
+        loop(part * fourth, stop if part == 3 else (part + 1) * fourth, pumped)
+        (s2, s1)[part % 2].step()
+    loop(stop, chunks, middle)
+
     loop(0, tiles, product(m.n2, lambda: m.at[...], m.dwo, local))
     so.start()
 
     for h in range(nh):
         m.qt[h] = m.q[h].T
         m.dat[h] = m.act[:, h * 128 : (h + 1) * 128].T
-    big = padded // sum_out.rows
-    loop(0, big, sum_out.offer)
+    big = sum_out.chunks
+    sum_out.relay(0)
     kv_sems = [sems.take() for _ in range(nh)]
     other = {"seq": flip(lax.axis_index("seq"), 1)}
     kv_copies = [remote(m.kvs.at[h], m.kvr.at[h], kv_sems[h], other) for h in range(nh)]
@@ -707,30 +729,26 @@
             m.gpre[at, nh * 128 + h * 64 : nh * 128 + (h + 1) * 64] = dq
             point = h * blocks + b
 
-            @pl.when((point >= 2) & (point < 2 + big))
-            def _():
-                sum_out.relay(point - 2)
-
-            @pl.when((point >= 5) & (point < 5 + big))
-            def _():
-                sum_out.close(point - 5)
+            for i, (when, done) in enumerate(((2, None), (5, 0), (8, 1))):
+
+                @pl.when(point == when)
+                def _(i=i, done=done):
+                    sum_out.relay(i + 1)
+                    if done is not None:
+                        sum_out.close(done)
 
         loop(0, blocks, back)
         m.kvs[h] = m.dkv[1, h].astype(BF16)
         kv_copies[h].start()
-        if h == 0:
+        if h < nh - 1:
             so.step()
-        if h == 1:
-            so.step()
-    points = nh * blocks
-    for i in range(max(0, points - 2), big):
-        sum_out.relay(i)
-    for i in range(max(0, points - 5), big):
-        sum_out.close(i)
     spare = packed - nh * 192
     if spare:
         m.gpre[:, nh * 192 : packed] = fill((padded, spare), 0, BF16)
     for h in range(nh):
+        if h == nh - 1:
+            sum_out.relay(4)
+            sum_out.close(2)
         kv_copies[h].wait_recv()
         total = m.dkv[0, h] + m.kvr[h].astype(F32)
         m.gpre[:, h * 128 : (h + 1) * 128] = total.T.astype(BF16)
@@ -746,23 +764,20 @@
         m.part[at] = back.astype(BF16)
         loop(0, per, lambda j: sum_one.offer(b * per + j))
 
-        @pl.when(b > 0)
-        def _():
-            loop(0, per, lambda j: sum_one.relay((b - 1) * per + j))
-
     loop(0, chunks, sum_two.drain)
     loop(0, blocks, last)
     one_q = product(m.n1, lambda: m.gpre[:, :packed], m.dwq, packed)
 
     def qkv(i):
         one_q(i)
-
-        @pl.when(i < per)
-        def _():
-            sum_one.relay(chunks - per + i)
-
+        sum_one.pump(i)
+
+    sum_out.relay(5)
+    sum_out.close(3)
     loop(0, tiles, qkv)
     sq.start()
+    sum_out.close(4)
+    sum_out.close(5)
 
     for row in range(8):
         m.vs[row : row + 1, :] = jnp.sum(m.acc[row], axis=0, keepdims=True)
@@ -794,12 +809,12 @@
     def output(i):
         sum_out.accept(i)
         at = rows_of(i, sum_out.rows)
-        m.ototal[at] = (m.igrad[at] + m.ototal[at].astype(F32) + b_two).astype(BF16)
+        m.ototal[at] = (m.mid[at] + m.ototal[at].astype(F32) + b_two).astype(BF16)
 
     gain_one = m.vec[0:1, :]
 
     def final(i):
-        sum_one.ready(i)
+        sum_one.accept(i)
         at = rows_of(i, CHUNK)
         e = m.total[at].astype(F32) * gain_one
         xhat, r = normalize(m.xp[at].astype(F32))
@@ -807,30 +822,57 @@
         along = jnp.mean(e * xhat, axis=-1, keepdims=True)
         m.igrad[at] = m.xh2[at] + r * (e - mean - xhat * along)
 
-    loop(0, big, sum_out.drain)
-    loop(0, big, output)
-    m.ow1[...] = s1.finish()
-    m.ow2[...] = s2.finish().T
-    m.owo[...] = so.finish().T
+    def tail(i):
+        sum_one.pump(i + tiles)
+        final(i)
+
+    def unpack():
+        got = sq.finish()
+        for h in range(nh):
+            cols = slice(h * HEAD_DIM, (h + 1) * HEAD_DIM)
+            m.owk[:, cols] = got[:, h * 128 : h * 128 + 64]
+            m.owv[:, cols] = got[:, h * 128 + 64 : (h + 1) * 128]
+        m.owq[...] = got[:, nh * 128 : nh * 128 + local]
+
+    def vectors():
+        for k in range(len(vec_steps) - 2, len(vec_steps)):
+            vec_take(k)
+        m.ovec[...] = fill(m.ovec.shape, 0)
+        names = (GAIN_ONE, SHIFT_ONE, B_OUT, GAIN_TWO, SHIFT_TWO, B_FC_TWO)
+        for b in range(cube.size):
+
+            @pl.when(cube.rank() == b)
+            def _(b=b):
+                for place, row in enumerate(names):
+                    m.ovec[place : place + 1, :rows] = m.vs[row : row + 1, b * rows : (b + 1) * rows]
+
+        m.ovec[6:7, :local] = m.vs[B_QKV : B_QKV + 1, nh * 128 : nh * 192]
+        for h in range(nh):
+            m.ovec[7:8, h * 64 : (h + 1) * 64] = m.vs[B_QKV : B_QKV + 1, h * 128 + 64 : (h + 1) * 128]
+        m.ovec[8:9, :] = m.vs[B_FC_ONE : B_FC_ONE + 1, :]
+
+    def outputs():
+        loop(0, big, sum_out.drain)
+        loop(0, big, output)
+
+    def early():
+        m.ow1[...] = s1.finish()
+        m.ow2[...] = s2.finish()
+        m.owo[...] = so.finish().T
+
+    def cubed():
+        for k in range(1, len(vec_steps) - 2):
+            vec_take(k)
+
     vec_take(0)
-    sq.step()
-    loop(0, third, final)
-    vec_take(1)
-    sq.step()
-    vec_take(2)
-    loop(third, 2 * third, final)
-    vec_take(3)
-    got = sq.finish()
-    for h in range(nh):
-        cols = slice(h * HEAD_DIM, (h + 1) * HEAD_DIM)
-        m.owk[:, cols] = got[:, h * 128 : h * 128 + 64]
-        m.owv[:, cols] = got[:, h * 128 + 64 : (h + 1) * 128]
-    m.owq[...] = got[:, nh * 128 : nh * 128 + local]
-    vec_take(4)
-    for k in range(5, len(vec_steps)):
-        vec_take(k)
-    m.ovec[...] = m.vs[...]
-    loop(2 * third, chunks, final)
+    stop = chunks + LAG - tiles
+    jobs = (early, sq.step, cubed, sq.step, outputs, unpack, vectors)
+    share = stop // len(jobs)
+    for part, job in enumerate(jobs):
+        loop(part * share, (part + 1) * share, tail)
+        job()
+    loop(len(jobs) * share, stop, tail)
+    loop(stop, chunks, final)
 
     for copy in kv_copies + vec_copies:
         copy.wait_send()
@@ -839,12 +881,12 @@
     loop(0, chunks, sum_one.drain)
 
 
-def layer(inputs, cotangent, vectors, biases, w_query, w_key, w_value, w_out, w_fc_one, w_fc_two, mesh_shape):
+def layer(tokens, shares, biases, weights, mesh_shape):
     nz = mesh_shape["head"]
     cube = Cube(mesh_shape["clip"], mesh_shape["seq"])
-    frames, width = inputs.shape
-    rows, local = w_query.shape
-    hidden = w_fc_one.shape[1]
+    frames, width = tokens[0].shape
+    rows, local = weights[0].shape
+    hidden = weights[4].shape[1]
     nh = local // HEAD_DIM
     padded = -(-frames // BLOCK) * BLOCK
     colors = 2 if rows % 32 == 0 else 1
@@ -852,28 +894,21 @@
     packed = -(-(nh * 192) // 128) * 128
     nb = cube.size
     steps = len(cube.all_bits) + len(powers(nz))
-    ins = dict(
-        x=inputs,
-        cot=cotangent,
-        vsh=vectors,
-        bias=biases,
-        wq=w_query,
-        wk=w_key,
-        wv=w_value,
-        wo=w_out,
-        w1=w_fc_one,
-        w2=w_fc_two,
-    )
+    token_names, bias_names = ("x", "cot"), ("bq", "bv", "bf1")
+    weight_names = ("wq", "wk", "wv", "wo", "w1", "w2")
+    share_names = tuple(f"share{i}" for i in range(len(shares)))
+    names = token_names + share_names + bias_names + weight_names
+    ins = dict(zip(names, (*tokens, *shares, *biases, *weights)))
     outs = dict(
         ototal=((padded, width), BF16),
         igrad=((padded, width), F32),
-        ovec=((8, width), F32),
+        ovec=((16, width), F32),
         owq=((rows, local), F32),
         owk=((rows, local), F32),
         owv=((rows, local), F32),
         owo=((local, rows), F32),
         ow1=((rows, hidden), F32),
-        ow2=((hidden, rows), F32),
+        ow2=((rows, hidden), F32),
     )
     flat = (padded, width)
     scratch = dict(
@@ -883,6 +918,8 @@
         g2=((nb, colors, half, hidden), BF16),
         gv=((nb, 8, 128), F32),
         vec=((8, width), F32),
+        bias=((8, packed), F32),
+        mid=(flat, F32),
         n1=(flat, BF16),
         q=((nh, padded, 128), BF16),
         kv=((2, nh, padded, 128), BF16),
@@ -927,7 +964,7 @@
         dwq=((width, packed), BF16),
         dlq=((colors, nb - 1, half, packed), BF16),
     )
-    small, large = padded // CHUNK, padded // 128
+    small, large = padded // CHUNK, 6
     lines = 3 * (2 * small + large)
     count = lines + 9 * colors * (nb - 1) + 60
 
@@ -935,13 +972,14 @@
         names = list(ins) + list(outs) + list(scratch)
         m = types.SimpleNamespace(**dict(zip(names, refs)))
         send, recv = refs[len(names) :]
+        m.shares = [getattr(m, name) for name in share_names]
         sems = Sems(send, recv)
         sems.used = lines
         sum_two = LineSum(nz, send, recv, 0, small, CHUNK, m.part, m.landed, m.crossed, m.total)
         sum_one = LineSum(nz, send, recv, 3 * small, small, CHUNK, m.part, m.landed, m.crossed_one, m.total)
-        sum_out = LineSum(nz, send, recv, 6 * small, large, 128, m.opart, m.olanded, m.ocrossed, m.ototal)
+        sum_out = LineSum(nz, send, recv, 6 * small, large, padded // large, m.opart, m.olanded, m.ocrossed, m.ototal)
         stage_one(m, cube, nz, sems)
-        stage_two(m, cube, nz, sum_two)
+        stage_two(m, cube, nz, sum_two, sum_out)
         stage_three(m, cube, nz, sems, sum_two, sum_out, sum_one)
         assert sems.used <= count, (sems.used, count)
 
@@ -959,20 +997,51 @@
     return types.SimpleNamespace(**dict(zip(outs, res)))
 
 
-def vector_pack(vectors):
-    stack = jnp.stack([v.astype(F32) for v in vectors])
-    return jnp.pad(stack, ((0, 8 - stack.shape[0]), (0, 128 - stack.shape[1])))
-
-
-def biases_pack(b_query, b_value, b_fc_one, heads):
-    zero = jnp.zeros((HEAD_DIM,), F32)
-    parts = []
-    for h in range(heads):
-        parts += [zero, b_value[h * HEAD_DIM : (h + 1) * HEAD_DIM].astype(F32)]
-    row = jnp.concatenate(parts + [b_query.astype(F32)])
-    width = b_fc_one.shape[0]
-    row = jnp.pad(row, (0, width - row.shape[0]))
-    return jnp.pad(jnp.stack([row, b_fc_one.astype(F32)]), ((0, 6), (0, 0)))
+def finish(res, frames):
+    padded, width = res.ototal.shape
+    rows, local = res.owq.shape
+    hidden = res.ow1.shape[1]
+    tile = 256
+    whole = lambda shape: pl.BlockSpec(shape, lambda i: (0,) * len(shape))
+    sizes = [rows] * 6 + [local] * 2 + [hidden]
+    passed = (res.owq, res.owk, res.owv, res.owo, res.ow1, res.ow2)
+
+    def body(out_ref, grad_ref, vec_ref, *refs):
+        ins, (to_out, to_grad, *rest) = refs[: len(passed)], refs[len(passed) :]
+        to_out[...] = out_ref[...]
+        to_grad[:, 0, :] = grad_ref[...]
+
+        @pl.when(pl.program_id(0) == 0)
+        def _():
+            for source, target in zip(ins, rest):
+                target[...] = source[...]
+            *vectors, last = rest[len(passed) :]
+            for i, target in enumerate(vectors):
+                target[...] = vec_ref[i : i + 1, : sizes[i]]
+            for i in range(hidden // 128):
+                last[i : i + 1, :] = vec_ref[len(vectors) : len(vectors) + 1, i * 128 : (i + 1) * 128]
+
+    row_tile = pl.BlockSpec((tile, width), lambda i: (i, 0))
+    vectors = [jax.ShapeDtypeStruct((1, size), F32) for size in sizes[:-1]]
+    vectors.append(jax.ShapeDtypeStruct((hidden // 128, 128), F32))
+    kept = [jax.ShapeDtypeStruct(a.shape, a.dtype) for a in passed]
+    return pl.pallas_call(
+        body,
+        grid=(padded // tile,),
+        out_shape=[
+            jax.ShapeDtypeStruct((frames, width), BF16),
+            jax.ShapeDtypeStruct((frames, 1, width), F32),
+            *kept,
+            *vectors,
+        ],
+        in_specs=[row_tile, row_tile, whole(res.ovec.shape)] + [whole(a.shape) for a in passed],
+        out_specs=[
+            row_tile,
+            pl.BlockSpec((tile, 1, width), lambda i: (i, 0, 0)),
+            *[whole(a.shape) for a in kept + vectors],
+        ],
+        name="finish",
+    )(res.ototal, res.igrad, res.ovec, *passed)
 
 
 def on_device(
@@ -997,46 +1066,34 @@
 ):
     clips, frames, width = inputs.shape
     count = clips * frames
-    local = w_query.shape[1]
-    heads = local // HEAD_DIM
-    share = gain_one.shape[0]
-    vectors = vector_pack((gain_one, shift_one, gain_two, shift_two, b_out, b_fc_two))
-    biases = biases_pack(b_query, b_value, b_fc_one, heads)
+    row = lambda v: v.reshape(1, -1)
     res = layer(
-        inputs.reshape(count, width),
-        cotangent.reshape(count, width),
-        vectors,
-        biases,
-        w_query,
-        w_key,
-        w_value,
-        w_out,
-        w_fc_one,
-        w_fc_two,
+        (inputs.reshape(count, width), cotangent.reshape(count, width)),
+        tuple(row(v) for v in (gain_one, shift_one, gain_two, shift_two, b_out, b_fc_two)),
+        (b_query, b_value, b_fc_one),
+        (w_query, w_key, w_value, w_out, w_fc_one, w_fc_two.T),
         mesh_shape,
     )
-    rank = lax.axis_index("clip") * mesh_shape["seq"] + lax.axis_index("seq")
-    owned = lax.dynamic_slice_in_dim(res.ovec, rank * share, share, axis=1)
-    qkv = res.ovec[B_QKV]
-    b_values = jnp.concatenate([qkv[h * 128 + 64 : (h + 1) * 128] for h in range(heads)])
+    outputs, grad, g_query, g_key, g_value, g_out, g_one, g_two, *vectors = finish(res, count)
+    g1, s1, b_o, g2, s2, b_two, b_q, b_v, b_one = (v.reshape(-1) for v in vectors)
     return (
-        res.ototal[:count].reshape(clips, frames, width),
-        res.igrad[:count].reshape(clips, frames, width),
-        owned[GAIN_ONE],
-        owned[SHIFT_ONE],
-        res.owq,
-        qkv[heads * 128 : heads * 128 + local],
-        res.owk,
-        res.owv,
-        b_values,
-        res.owo,
-        owned[B_OUT],
-        owned[GAIN_TWO],
-        owned[SHIFT_TWO],
-        res.ow1,
-        res.ovec[B_FC_ONE],
-        res.ow2,
-        owned[B_FC_TWO],
+        outputs.reshape(clips, frames, width),
+        grad.transpose(1, 0, 2).reshape(clips, frames, width),
+        g1,
+        s1,
+        g_query,
+        b_q,
+        g_key,
+        g_value,
+        b_v,
+        g_out,
+        b_o,
+        g2,
+        s2,
+        g_one,
+        b_one,
+        g_two.T,
+        b_two,
     )
 
 

time: 239 us -> 181 us (0.76)
  Pallas kernels: 215 us -> 180 us
  local copies, waits for them, and re-layouts: 20.2 us -> 0 us
  other arithmetic: 2.7 us -> 0 us
    pallas_call x1, Pallas kernels: 215 us -> 175 us  [layer(): pl.pallas_call(body, out_shape=[jax.ShapeDtypeStruct(*v) for v in outs.va...]
    unnamed x20 -> x0, local copies, waits for them, and re-layouts: 10.6 us -> none
    pallas_call x0 -> x1, Pallas kernels: none -> 5.53 us  [finish(): pl.pallas_call(body, grid=(padded // tile,), out_shape=[jax.ShapeDtypeStr...]
    slice x3 -> x0, local copies, waits for them, and re-layouts: 3.36 us -> none  [the longest x1 1.34 us: on_device(): res.ovec[B_FC_ONE]]
    reshape x2 -> x0, local copies, waits for them, and re-layouts: 2.64 us -> none  [the longest x1 2.49 us: on_device(): res.ototal[:count].reshape(clips, frames, width)]
where the time goes in v3:
time: 181 us
  Pallas kernels  180 us (99%)
    pallas_call x1, Pallas kernels, layer(): pl.pallas_call(body, out_shape=[jax.ShapeDtypeStruct(*v) for v in outs.va...  175 us
    pallas_call x1, Pallas kernels, finish(): pl.pallas_call(body, grid=(padded // tile,), out_shape=[jax.ShapeDtypeStr...  5.53 us

profile of v3, /device:TPU:0, one launch (start us, length us, event | category | flops | bytes accessed | tf_op | source)
XLA Modules:
  0.0 180.9 jit_solution(7257571494480278946)
XLA Ops:
  0.7 174.6 %layer.1 = (bf16[768,768]{1,0:T(8,128)(2,1)}, f32[768,768]{1,0:T(8,128)}, f32[16,768]{1,0:T(8,128)}, f32[96,192]{1,0:T(8,128)}, f32[96,192]{1,0:T(8,128)}, /*ind...) custom-call(bf16[750,768]{1,0:T(8,128)(2,1)} %bitcast.21, ...), custom_call_target="tpu_custom_call" | custom-call | tf_op jit(solution)/shard_map/layer/pallas_call | solution.py:986
  175.2 5.5 %finish.1 = (bf16[750,768]{1,0:T(8,128)(2,1)}, f32[750,1,768]{2,1,0:T(1,128)}, f32[96,192]{1,0:T(8,128)}, f32[96,192]{1,0:T(8,128)}, f32[96,192]{1,0:T(8,128)}, ...) custom-call(bf16[768,768]{1,0:T(8,128)(2,1)} %get-tuple-element.43.o, ...), custom_call_target="tpu_custom_call" | custom-call | tf_op jit(solution)/shard_map/finish/pallas_call | solution.py:1028

commit v4 on v3

--- a/solution.py
+++ b/solution.py
@@ -132,6 +132,7 @@
 
 
 NEG = -1e30
+LINE_LAG = 3
 
 
 def fill(shape, value, dtype=F32):
@@ -143,32 +144,31 @@
 
 
 class Line:
-    def __init__(self, nodes, sems, view, parts):
+    def __init__(self, nodes, send, recv, base, view, parts):
         self.n, self.z = nodes, lax.axis_index("head")
-        self.view = view
-        self.right = [[sems.take() for _ in range(parts)] for _ in range(nodes - 1)]
-        self.left = [[sems.take() for _ in range(parts)] for _ in range(nodes - 1)]
+        self.send_sem, self.recv_sem, self.base = send, recv, base
+        self.view, self.parts = view, parts
+
+    @staticmethod
+    def count(nodes, parts):
+        return 2 * (nodes - 1) * parts
 
     def moves(self, hop, part):
         z, n = self.z, self.n
 
-        def copy(origin, sems, target):
+        def copy(origin, way, target):
             piece = self.view(origin, part)
+            place = self.base + (way * (n - 1) + hop) * self.parts + part
+            sems = self.send_sem.at[place], self.recv_sem.at[place]
             return remote(piece, piece, sems, {"head": target})
 
         sends = (
-            (
-                (z >= hop) & (z < n - 1),
-                lambda: copy(z - hop, self.right[hop][part], z + 1),
-            ),
-            (
-                (n - 1 - z >= hop) & (z > 0),
-                lambda: copy(z + hop, self.left[hop][part], z - 1),
-            ),
+            ((z >= hop) & (z < n - 1), lambda: copy(z - hop, 0, z + 1)),
+            ((n - 1 - z >= hop) & (z > 0), lambda: copy(z + hop, 1, z - 1)),
         )
         arrivals = (
-            (z > hop, lambda: copy(z - 1 - hop, self.right[hop][part], z - 1)),
-            (n - 1 - z > hop, lambda: copy(z + 1 + hop, self.left[hop][part], z + 1)),
+            (z > hop, lambda: copy(z - 1 - hop, 0, z - 1)),
+            (n - 1 - z > hop, lambda: copy(z + 1 + hop, 1, z + 1)),
         )
         return sends, arrivals
 
@@ -179,6 +179,20 @@
     def arrive(self, hop, part):
         for condition, copy in self.moves(hop, part)[1]:
             pl.when(condition)(lambda copy=copy: copy().wait_recv())
+
+    def pump(self, step):
+        @pl.when(step < self.parts)
+        def _():
+            self.start(0, step)
+
+        for hop in range(self.n - 1):
+            part = step - LINE_LAG * (hop + 1)
+
+            @pl.when((part >= 0) & (part < self.parts))
+            def _(hop=hop, part=part):
+                self.arrive(hop, part)
+                if hop + 1 < self.n - 1:
+                    self.start(hop + 1, part)
 
     def drain(self, part):
         for hop in range(self.n - 1):
@@ -186,17 +200,18 @@
                 pl.when(condition)(lambda copy=copy: copy().wait_send())
 
 
-def entry_barrier(cube, heads):
-    barrier = pltpu.get_barrier_semaphore()
+def entry_peers(cube, heads):
     z = lax.axis_index("head")
     peers = [cube.peer(step) for step in cube.orders[0]]
-    peers += [{"head": lax.rem(z + d, heads)} for d in range(1, heads)]
+    return peers + [{"head": lax.rem(z + d, heads)} for d in range(1, heads)]
+
+
+def greet(peers):
     for peer in peers:
-        pl.semaphore_signal(barrier, inc=1, device_id=peer, device_id_type=MESH)
-    pl.semaphore_wait(barrier, len(peers))
-
-
-def stage_one(m, cube, nz, sems):
+        pl.semaphore_signal(pltpu.get_barrier_semaphore(), inc=1, device_id=peer, device_id_type=MESH)
+
+
+def stage_one(m, cube, nz, sems, line):
     z = lax.axis_index("head")
     r = cube.rank()
     rows = m.wq.shape[0]
@@ -209,6 +224,9 @@
     tiles = padded // tile
     width = m.x.shape[1]
 
+    peers = entry_peers(cube, nz)
+    greet(peers)
+    gk = Gather(cube, sems, lambda b, c: m.gk.at[b, c], colors)
     gq = Gather(cube, sems, lambda b, c: m.gq.at[b, c], colors)
     gv = Gather(cube, sems, lambda b, c: m.gv.at[b], 1)
     g1 = Gather(cube, sems, lambda b, c: m.g1.at[b, c], colors)
@@ -216,6 +234,8 @@
     go = Gather(cube, sems, lambda b, c: m.go.at[:, b, c], colors)
 
     m.vec[...] = fill(m.vec.shape, 0)
+    for name in m.first_loads:
+        m.load[name].wait()
     for row, ref in enumerate(m.shares):
         m.vec[row : row + 1, :rows] = ref[...].astype(F32)
     m.gv[r] = m.vec[:, :128]
@@ -223,23 +243,27 @@
         part = pl.ds(c * half, half)
         for h in range(nh):
             cols = slice(h * HEAD_DIM, (h + 1) * HEAD_DIM)
-            m.gq[r, c, :, h * 128 : h * 128 + 64] = m.wk[part, cols]
-            m.gq[r, c, :, h * 128 + 64 : (h + 1) * 128] = m.wv[part, cols]
-        m.gq[r, c, :, nh * 128 : nh * 128 + nh * 64] = m.wq[part, :]
-        spare = m.gq.shape[3] - nh * 192
+            m.gk[r, c, :, h * 128 : h * 128 + 64] = m.wk[part, cols]
+            m.gk[r, c, :, h * 128 + 64 : (h + 1) * 128] = m.wv[part, cols]
+        m.gq[r, c, :, : nh * 64] = m.wq[part, :]
+        spare = m.gq.shape[3] - nh * 64
         if spare:
-            m.gq[r, c, :, nh * 192 :] = fill((half, spare), 0, BF16)
+            m.gq[r, c, :, nh * 64 :] = fill((half, spare), 0, BF16)
+
+    pl.semaphore_wait(pltpu.get_barrier_semaphore(), len(peers))
+    gv.start(0, 0)
+    for g in (gk, gq):
+        for c in range(colors):
+            g.start(0, c)
+
+    for name in m.next_loads:
+        m.load[name].wait()
+    wot = m.wo[...].T
+    for c in range(colors):
+        part = slice(c * half, (c + 1) * half)
+        m.go[z, r, c] = wot[part]
         m.g2[r, c] = m.w2[part, :]
         m.g1[r, c] = m.w1[part, :]
-
-    entry_barrier(cube, nz)
-    gv.start(0, 0)
-    for c in range(colors):
-        gq.start(0, c)
-
-    wot = m.wo[...].T
-    for c in range(colors):
-        m.go[z, r, c] = wot[c * half : (c + 1) * half]
     out_sems = [sems.take() for _ in range(nz - 1)]
 
     def out_copies(arriving):
@@ -251,10 +275,6 @@
 
     for copy in out_copies(False):
         copy.start()
-    for c in range(1, colors):
-        g1.start(0, c)
-        g2.start(0, c)
-
     m.xp[0:frames] = m.x[...]
     m.xp[frames:padded] = fill((padded - frames, width), 0, BF16)
 
@@ -270,7 +290,14 @@
         lax.fori_loop(third * k, top, norm_tile, 0)
         gv.advance(k, 0)
         for c in range(colors):
-            gq.advance(k, c)
+            gk.advance(k, c)
+        if k < gq.steps - 1:
+            for c in range(colors):
+                gq.advance(k, c)
+        if k == 0:
+            for g in (g1, g2):
+                for c in range(colors):
+                    g.start(0, c)
     for b in range(cube.size):
         m.vec[:, b * rows : (b + 1) * rows] = m.gv[b, :, :rows]
     gain, shift = m.vec[0:1, :], m.vec[1:2, :]
@@ -278,42 +305,49 @@
     bv = m.bv[...].astype(F32)[None, :]
     for h in range(nh):
         m.bias[0:1, h * 128 + 64 : (h + 1) * 128] = bv[:, h * HEAD_DIM : (h + 1) * HEAD_DIM]
-    m.bias[0:1, nh * 128 : nh * 192] = m.bq[...].astype(F32)[None, :]
-    bias = m.bias[0:1, :]
+    m.bias[1:2, : nh * 64] = m.bq[...].astype(F32)[None, :]
     scale = HEAD_DIM**-0.5
 
     def project(i, carry):
         at = pl.ds(pl.multiple_of(i * tile, tile), tile)
         n1 = (m.xh2[at] * gain + shift).astype(BF16)
         m.n1[at] = n1
-        packed = dot(n1, m.gq[...].reshape(cube.size * rows, m.gq.shape[3])) + bias
+        packed = dot(n1, m.gk[...].reshape(cube.size * rows, nh * 128)) + m.bias[0:1, : nh * 128]
+        for h in range(nh):
+            m.kv[0, h, at] = packed[:, h * 128 : (h + 1) * 128].astype(BF16)
+        return carry
+
+    lax.fori_loop(0, tiles, project, 0)
+
+    kv_sems = [sems.take() for _ in range(nh)]
+    other = {"seq": flip(lax.axis_index("seq"), 1)}
+    kv_copies = [
+        remote(m.kv.at[0, h], m.kv.at[1, h], kv_sems[h], other) for h in range(nh)
+    ]
+    kv_copies[0].start()
+    for copy in out_copies(True):
+        copy.wait_recv()
+    for c in range(colors):
+        go.start(0, c)
+    for copy in kv_copies[1:]:
+        copy.start()
+    for c in range(colors):
+        gq.advance(gq.steps - 1, c)
+
+    def project_query(i, carry):
+        at = pl.ds(pl.multiple_of(i * tile, tile), tile)
+        wide = m.gq.shape[3]
+        packed = dot(m.n1[at], m.gq[...].reshape(cube.size * rows, wide)) + m.bias[1:2, :wide]
         left = lane((tile, 128)) < 64
         for h in range(nh):
-            m.kv[0, h, at] = packed[:, h * 128 : (h + 1) * 128].astype(BF16)
-            base = nh * 128 + (h // 2) * 128
-            pair = packed[:, base : base + 128]
+            pair = packed[:, (h // 2) * 128 : (h // 2) * 128 + 128]
             if h % 2:
                 pair = pltpu.roll(pair, 64, 1)
             pair = pair.astype(BF16).astype(F32) * scale
             m.q[h, at] = jnp.where(left, pair, 0.0).astype(BF16)
         return carry
 
-    lax.fori_loop(0, tiles, project, 0)
-
-    kv_sems = [sems.take() for _ in range(nh)]
-    other = {"seq": flip(lax.axis_index("seq"), 1)}
-    kv_copies = [
-        remote(m.kv.at[0, h], m.kv.at[1, h], kv_sems[h], other) for h in range(nh)
-    ]
-    for copy in out_copies(True):
-        copy.wait_recv()
-    for c in range(1, colors):
-        go.start(0, c)
-    kv_copies[0].start()
-    for g in (g1, g2, go):
-        g.start(0, 0)
-    for copy in kv_copies[1:]:
-        copy.start()
+    lax.fori_loop(0, tiles, project_query, 0)
 
     left = lane((padded, 128)) < 64
 
@@ -325,7 +359,6 @@
     for h in range(nh):
         prepare(0, h)
 
-    line = Line(nz, sems, lambda origin, part: m.attz.at[origin, part], nh)
     block = 256
     valid = frames - (padded - 128)
 
@@ -354,55 +387,51 @@
             m.il[h, at] = jnp.where(right, inverse, 0.0)
             m.atto[h, at] = jnp.where(right, att, 0.0).astype(BF16)
             turned = pltpu.roll(att, 64, 1)
-            packed = jnp.where(right[: block // 2], att[block // 2 :], turned[: block // 2])
-            to = pl.ds(pl.multiple_of(b * (block // 2), block // 2), block // 2)
-            m.attz[z, h, to] = packed.astype(BF16)
+            pieces = [
+                jnp.where(right[:64], att[g + 64 : g + 128], turned[g : g + 64])
+                for g in range(0, block, 128)
+            ]
+            part = h * (padded // block) + b
+            m.attz[z, part] = jnp.concatenate(pieces, axis=0).astype(BF16)
+            line.pump(part)
             return carry
 
         lax.fori_loop(0, padded // block, one, 0)
 
-    def weights(k, c):
-        if c < colors and k < g1.steps:
-            for g in (g1, g2, go):
+    def weights(gathers, k, c):
+        if c < colors and k < g1.steps - 1:
+            for g in gathers:
                 g.advance(k, c)
 
+    feed = (g1, g2)
+    plan = {0: ((feed, 0, 0), (feed, 0, 1)), 1: (((go,), 0, 0), ((go,), 0, 1))}
+    plan[nh - 1] = ((feed, 1, 0),)
     for h in range(nh):
         kv_copies[h].wait_recv()
         prepare(1, h)
         attend(h)
-        line.start(0, h)
-        if h == 0:
-            weights(0, 1)
-        if h >= 1:
-            line.arrive(0, h - 1)
-            line.start(1, h - 1)
-        if h == 1:
-            weights(0, 0)
-        if h >= 2:
-            line.arrive(1, h - 2)
-            line.start(2, h - 2)
-    for hop in range(nz - 1):
-        for h in range(nh):
-            done = nh - 1 - h
-            if hop >= done:
-                if hop == nz - 2 and h == 1:
-                    weights(1, 0)
-                    weights(1, 1)
-                line.arrive(hop, h)
-                if hop + 1 < nz - 1:
-                    line.start(hop + 1, h)
+        for job in plan.get(h, ()):
+            weights(*job)
+    parts = line.parts
+    stop = parts + LINE_LAG * (nz - 1)
+    loop(parts, parts + 3, line.pump)
+    weights((go,), 1, 0)
+    weights(feed, 1, 1)
+    loop(parts + 3, stop - 2, line.pump)
+    weights((go,), 1, 1)
+    loop(stop - 2, stop, line.pump)
     for k in range(2, g1.steps):
-        for c in range(colors):
-            weights(k, c)
+        for g in (go, g1, g2):
+            for c in range(colors):
+                g.advance(k, c)
 
     for copy in kv_copies:
         copy.wait_send()
     for copy in out_copies(False):
         copy.wait_send()
-    for g in (gv, gq, g1, g2, go):
+    for g in (gv, gk, gq, g1, g2, go):
         g.drain()
-    for h in range(nh):
-        line.drain(h)
+    loop(0, line.parts, line.drain)
 
 
 class Scatter:
@@ -472,11 +501,11 @@
 
 
 class LineSum:
-    def __init__(self, nz, send, recv, base, chunks, rows, part, landed, crossed, total):
+    def __init__(self, nz, send, recv, ends, middle, chunks, rows, part, landed, crossed, total):
         z = lax.axis_index("head")
         self.inner = (z > 0) & (z < nz - 1)
         self.mate, self.cross = {"head": flip(z, 1)}, {"head": nz - 1 - z}
-        self.send_sem, self.recv_sem, self.base = send, recv, base
+        self.send_sem, self.recv_sem, self.bases = send, recv, (ends, middle, ends)
         self.chunks, self.rows = chunks, rows
         self.part, self.landed, self.crossed, self.total = part, landed, crossed, total
 
@@ -484,7 +513,7 @@
         return ref.at[pl.ds(pl.multiple_of(i * self.rows, self.rows), self.rows)]
 
     def sems(self, kind, i):
-        place = self.base + kind * self.chunks + i
+        place = self.bases[kind] + i
         return self.send_sem.at[place], self.recv_sem.at[place]
 
     def first(self, i):
@@ -559,6 +588,7 @@
 
 B_FC_TWO, GAIN_TWO, SHIFT_TWO, B_OUT, GAIN_ONE, SHIFT_ONE, B_QKV, B_FC_ONE = range(8)
 BLOCK = 256
+STEP = 128
 CHUNK = 32
 LAG = 4
 
@@ -569,21 +599,22 @@
     nh = m.q.shape[0]
     frames = m.cot.shape[0]
     hidden = m.w1.shape[1]
+    m.load["cot"].wait()
     m.gp[0:frames] = m.cot[...]
     m.gp[frames:padded] = fill((padded - frames, width), 0, BF16)
     m.acc[...] = fill(m.acc.shape, 0)
     gain, shift, b_out = m.vec[2:3, :], m.vec[3:4, :], m.vec[4:5, :]
     b_one = m.bf1[...].astype(F32)[None, :]
-    per = BLOCK // CHUNK
+    per = STEP // CHUNK
     w_one = lambda: m.g1[...].reshape(cube.size * rows, hidden)
     w_two = lambda: m.g2[...].reshape(cube.size * rows, hidden)
 
     def block(b):
-        at = rows_of(b, BLOCK)
-        small = rows_of(b, BLOCK // 2)
+        at = rows_of(b, STEP)
+        packed = rows_of(lax.rem(b, 2), STEP // 2)
         mid = m.xp[at].astype(F32) + b_out
         for zz in range(nz):
-            pieces = [m.attz[zz, h, small] for h in range(nh)]
+            pieces = [m.attz[zz, h * (padded // BLOCK) + lax.div(b, 2), packed] for h in range(nh)]
             top = jnp.concatenate([p[:, :64] for p in pieces], axis=1)
             low = jnp.concatenate([p[:, 64:] for p in pieces], axis=1)
             att = jnp.concatenate([top, low], axis=0)
@@ -591,7 +622,7 @@
         xhat, inverse = normalize(mid)
         m.mid[at] = mid
         m.xh2[at] = xhat
-        m.r2[at] = jnp.broadcast_to(inverse, (BLOCK, 128))
+        m.r2[at] = jnp.broadcast_to(inverse, (STEP, 128))
         n2 = (xhat * gain + shift).astype(BF16)
         m.n2[at] = n2
         pre = dot(n2, w_one()) + b_one
@@ -609,9 +640,15 @@
         add_rows(m, SHIFT_TWO, back)
         m.part[at] = back.astype(BF16)
         loop(0, per, lambda j: sum_two.offer(b * per + j))
+
+        @pl.when(b >= 2)
+        def _():
+            sum_two.pump(2 * b - 4)
+            sum_two.pump(2 * b - 3)
+
         m.opart[at] = dot_nt(m.act[at], w_two()).astype(BF16)
 
-    loop(0, padded // BLOCK, block)
+    loop(0, padded // STEP, block)
     loop(0, sum_out.chunks, sum_out.offer)
 
 
@@ -624,9 +661,9 @@
     colors = m.gq.shape[1]
     chunks = padded // CHUNK
     blocks = padded // BLOCK
-    per = BLOCK // CHUNK
+    per = STEP // CHUNK
     scale = HEAD_DIM**-0.5
-    packed = m.gq.shape[3]
+    packed = m.gk.shape[3] + m.gq.shape[3]
     s1 = Scatter(cube, sems, m.dw1, m.dl1, rows, colors)
     s2 = Scatter(cube, sems, m.dw2, m.dl2, rows, colors)
     so = Scatter(cube, sems, m.dwo, m.dlo, rows, colors)
@@ -646,11 +683,13 @@
 
     def first(i):
         one(i)
-        sum_two.pump(i)
+        sum_two.pump(early + i)
 
     def second(i):
         two(i)
-        sum_two.pump(tiles + i)
+        sum_two.pump(early + tiles + i)
+
+    early = 2 * (padded // STEP - 2)
 
     loop(0, tiles, first)
     s1.start()
@@ -684,19 +723,20 @@
             m.act[at, h * 128 : (h + 1) * 128] = jnp.where(right, wide * m.il[h, at], 0.0).astype(BF16)
             m.at[at, h * 64 : (h + 1) * 64] = m.atto[h, at][:, 64:]
 
-    ahead = 2 * tiles
+    ahead = early + 2 * tiles
+    stop = chunks + LAG - ahead
+    each = chunks // stop
 
     def pumped(i):
         sum_two.pump(i + ahead)
-        middle(i)
-
-    stop = chunks + LAG - ahead
+        loop(i * each, (i + 1) * each, middle)
+
     s1.step()
     fourth = stop // 4
     for part in range(4):
         loop(part * fourth, stop if part == 3 else (part + 1) * fourth, pumped)
         (s2, s1)[part % 2].step()
-    loop(stop, chunks, middle)
+    loop(stop * each, chunks, middle)
 
     loop(0, tiles, product(m.n2, lambda: m.at[...], m.dwo, local))
     so.start()
@@ -754,10 +794,12 @@
         m.gpre[:, h * 128 : (h + 1) * 128] = total.T.astype(BF16)
 
     def last(b):
-        at = rows_of(b, BLOCK)
+        at = rows_of(b, STEP)
         grads = m.gpre[at, :packed]
         add_rows(m, B_QKV, grads.astype(F32))
-        back = dot_nt(grads, m.gq[...].reshape(cube.size * rows, packed))
+        keys = nh * 128
+        back = dot_nt(grads[:, :keys], m.gk[...].reshape(cube.size * rows, keys))
+        back = back + dot_nt(grads[:, keys:], m.gq[...].reshape(cube.size * rows, packed - keys))
         xhat, _ = normalize(m.xp[at].astype(F32))
         add_rows(m, GAIN_ONE, back * xhat)
         add_rows(m, SHIFT_ONE, back)
@@ -765,7 +807,7 @@
         loop(0, per, lambda j: sum_one.offer(b * per + j))
 
     loop(0, chunks, sum_two.drain)
-    loop(0, blocks, last)
+    loop(0, padded // STEP, last)
     one_q = product(m.n1, lambda: m.gpre[:, :packed], m.dwq, packed)
 
     def qkv(i):
@@ -833,6 +875,8 @@
             m.owk[:, cols] = got[:, h * 128 : h * 128 + 64]
             m.owv[:, cols] = got[:, h * 128 + 64 : (h + 1) * 128]
         m.owq[...] = got[:, nh * 128 : nh * 128 + local]
+        for name in ("owk", "owv", "owq"):
+            m.save[name].start()
 
     def vectors():
         for k in range(len(vec_steps) - 2, len(vec_steps)):
@@ -850,15 +894,20 @@
         for h in range(nh):
             m.ovec[7:8, h * 64 : (h + 1) * 64] = m.vs[B_QKV : B_QKV + 1, h * 128 + 64 : (h + 1) * 128]
         m.ovec[8:9, :] = m.vs[B_FC_ONE : B_FC_ONE + 1, :]
+        m.save["ovec"].start()
 
     def outputs():
         loop(0, big, sum_out.drain)
         loop(0, big, output)
+        m.save["ototal"].start()
 
     def early():
         m.ow1[...] = s1.finish()
+        m.save["ow1"].start()
         m.ow2[...] = s2.finish()
+        m.save["ow2"].start()
         m.owo[...] = so.finish().T
+        m.save["owo"].start()
 
     def cubed():
         for k in range(1, len(vec_steps) - 2):
@@ -873,6 +922,7 @@
         job()
     loop(len(jobs) * share, stop, tail)
     loop(stop, chunks, final)
+    m.save["igrad"].start()
 
     for copy in kv_copies + vec_copies:
         copy.wait_send()
@@ -898,6 +948,7 @@
     weight_names = ("wq", "wk", "wv", "wo", "w1", "w2")
     share_names = tuple(f"share{i}" for i in range(len(shares)))
     names = token_names + share_names + bias_names + weight_names
+    parts = nh * (padded // BLOCK)
     ins = dict(zip(names, (*tokens, *shares, *biases, *weights)))
     outs = dict(
         ototal=((padded, width), BF16),
@@ -912,7 +963,8 @@
     )
     flat = (padded, width)
     scratch = dict(
-        gq=((nb, colors, half, packed), BF16),
+        gk=((nb, colors, half, nh * 128), BF16),
+        gq=((nb, colors, half, packed - nh * 128), BF16),
         go=((nz, nb, colors, half, local), BF16),
         g1=((nb, colors, half, hidden), BF16),
         g2=((nb, colors, half, hidden), BF16),
@@ -928,7 +980,7 @@
         p=((nh, padded, 2 * padded), BF16),
         il=((nh, padded, 128), F32),
         atto=((nh, padded, 128), BF16),
-        attz=((nz, nh, padded // 2, 128), BF16),
+        attz=((nz, parts, BLOCK // 2, 128), BF16),
         xp=(flat, BF16),
         gp=(flat, BF16),
         xh2=(flat, F32),
@@ -965,30 +1017,53 @@
         dlq=((colors, nb - 1, half, packed), BF16),
     )
     small, large = padded // CHUNK, 6
-    lines = 3 * (2 * small + large)
-    count = lines + 9 * colors * (nb - 1) + 60
+    sums = 3 * small + 2 * large
+    lines = sums + Line.count(nz, parts)
+    count = lines + (9 * colors + 1) * (nb - 1) + (nz - 1) + 2 * nh + steps
 
     def body(*refs):
+        far_in, far_out = refs[: len(ins)], refs[len(ins) : len(ins) + len(outs)]
         names = list(ins) + list(outs) + list(scratch)
+        refs = refs[len(ins) + len(outs) :]
         m = types.SimpleNamespace(**dict(zip(names, refs)))
-        send, recv = refs[len(names) :]
+        send, recv, move = refs[len(names) :]
+        m.load = {
+            name: pltpu.make_async_copy(far, getattr(m, name), move.at[i])
+            for i, (name, far) in enumerate(zip(ins, far_in))
+        }
+        m.save = {
+            name: pltpu.make_async_copy(getattr(m, name), far, move.at[len(ins) + i])
+            for i, (name, far) in enumerate(zip(outs, far_out))
+        }
+        m.first_loads = share_names + ("wk", "wv", "wq")
+        m.next_loads = ("wo", "w1", "w2", "x", *bias_names)
+        for name in (*m.first_loads, *m.next_loads, "cot"):
+            m.load[name].start()
         m.shares = [getattr(m, name) for name in share_names]
         sems = Sems(send, recv)
         sems.used = lines
-        sum_two = LineSum(nz, send, recv, 0, small, CHUNK, m.part, m.landed, m.crossed, m.total)
-        sum_one = LineSum(nz, send, recv, 3 * small, small, CHUNK, m.part, m.landed, m.crossed_one, m.total)
-        sum_out = LineSum(nz, send, recv, 6 * small, large, padded // large, m.opart, m.olanded, m.ocrossed, m.ototal)
-        stage_one(m, cube, nz, sems)
+        sum_two = LineSum(nz, send, recv, 0, small, small, CHUNK, m.part, m.landed, m.crossed, m.total)
+        sum_one = LineSum(nz, send, recv, 0, 2 * small, small, CHUNK, m.part, m.landed, m.crossed_one, m.total)
+        sum_out = LineSum(
+            nz, send, recv, 3 * small, 3 * small + large, large, padded // large, m.opart, m.olanded, m.ocrossed, m.ototal
+        )
+        line = Line(nz, send, recv, sums, lambda origin, part: m.attz.at[origin, part], parts)
+        stage_one(m, cube, nz, sems, line)
         stage_two(m, cube, nz, sum_two, sum_out)
         stage_three(m, cube, nz, sems, sum_two, sum_out, sum_one)
-        assert sems.used <= count, (sems.used, count)
+        assert sems.used == count, (sems.used, count)
+        for copy in m.save.values():
+            copy.wait()
 
     res = pl.pallas_call(
         body,
         out_shape=[jax.ShapeDtypeStruct(*v) for v in outs.values()],
-        in_specs=[pl.BlockSpec(memory_space=pltpu.VMEM)] * len(ins),
-        out_specs=[pl.BlockSpec(memory_space=pltpu.VMEM)] * len(outs),
-        scratch_shapes=[pltpu.VMEM(*v) for v in scratch.values()] + [pltpu.SemaphoreType.DMA((count,))] * 2,
+        in_specs=[pl.BlockSpec(memory_space=pl.ANY)] * len(ins),
+        out_specs=[pl.BlockSpec(memory_space=pl.ANY)] * len(outs),
+        scratch_shapes=[pltpu.VMEM(a.shape, a.dtype) for a in ins.values()]
+        + [pltpu.VMEM(*v) for v in (outs | scratch).values()]
+        + [pltpu.SemaphoreType.DMA((count,))] * 2
+        + [pltpu.SemaphoreType.DMA((len(ins) + len(outs),))],
         compiler_params=pltpu.CompilerParams(
             collective_id=0, has_side_effects=True, vmem_limit_bytes=67_043_328
         ),
@@ -1002,46 +1077,68 @@
     rows, local = res.owq.shape
     hidden = res.ow1.shape[1]
     tile = 256
-    whole = lambda shape: pl.BlockSpec(shape, lambda i: (0,) * len(shape))
-    sizes = [rows] * 6 + [local] * 2 + [hidden]
+    sizes = [rows] * 6 + [local] * 2
     passed = (res.owq, res.owk, res.owv, res.owo, res.ow1, res.ow2)
-
-    def body(out_ref, grad_ref, vec_ref, *refs):
-        ins, (to_out, to_grad, *rest) = refs[: len(passed)], refs[len(passed) :]
-        to_out[...] = out_ref[...]
-        to_grad[:, 0, :] = grad_ref[...]
-
-        @pl.when(pl.program_id(0) == 0)
-        def _():
-            for source, target in zip(ins, rest):
-                target[...] = source[...]
-            *vectors, last = rest[len(passed) :]
-            for i, target in enumerate(vectors):
-                target[...] = vec_ref[i : i + 1, : sizes[i]]
-            for i in range(hidden // 128):
-                last[i : i + 1, :] = vec_ref[len(vectors) : len(vectors) + 1, i * 128 : (i + 1) * 128]
-
-    row_tile = pl.BlockSpec((tile, width), lambda i: (i, 0))
-    vectors = [jax.ShapeDtypeStruct((1, size), F32) for size in sizes[:-1]]
+    n = len(passed)
+
+    def body(out_far, grad_far, vec_far, *refs):
+        far, (to_out, to_grad, *to) = refs[:n], refs[n : 2 * n + 2 + 9]
+        out_near, grad_near, vec_near, *near = refs[2 * n + 11 : 3 * n + 14]
+        grad_flat, *flat = refs[3 * n + 14 : -1]
+        sem = refs[-1]
+        copy = lambda i, a, b: pltpu.make_async_copy(a, b, sem.at[i])
+        pieces = [(t, min(tile, padded - t)) for t in range(0, padded, tile)]
+        loads = [
+            copy(i, grad_far.at[pl.ds(t, size)], grad_near.at[pl.ds(t, size)]) for i, (t, size) in enumerate(pieces)
+        ]
+        k = len(pieces)
+        others = [copy(k + i, a, b) for i, (a, b) in enumerate(zip((vec_far, out_far, *far), (vec_near, out_near, *near)))]
+        for c in loads + others:
+            c.start()
+        k += len(others)
+        saves = []
+
+        def save(a, b):
+            saves.append(copy(k + len(saves), a, b))
+            saves[-1].start()
+
+        for c, (t, size) in zip(loads, pieces):
+            c.wait()
+            size = min(size, frames - t)
+            grad_flat[t : t + size, 0, :] = grad_near[t : t + size]
+            save(grad_flat.at[pl.ds(t, size)], to_grad.at[pl.ds(t, size)])
+        others[0].wait()
+        for i in range(8):
+            flat[i][...] = vec_near[i : i + 1, : sizes[i]]
+        for i in range(hidden // 128):
+            flat[8][i : i + 1, :] = vec_near[8:9, i * 128 : (i + 1) * 128]
+        others[1].wait()
+        flat[9][...] = out_near[0:frames]
+        save(flat[9], to_out)
+        for i in range(9):
+            save(flat[i], to[n + i])
+        for c, a, b in zip(others[2:], near, to):
+            c.wait()
+            save(a, b)
+        for c in saves:
+            c.wait()
+
+    vectors = [jax.ShapeDtypeStruct((1, size), F32) for size in sizes]
     vectors.append(jax.ShapeDtypeStruct((hidden // 128, 128), F32))
     kept = [jax.ShapeDtypeStruct(a.shape, a.dtype) for a in passed]
+    final = jax.ShapeDtypeStruct((frames, width), BF16)
+    grads = jax.ShapeDtypeStruct((frames, 1, width), F32)
+    given = (res.ototal, res.igrad, res.ovec, *passed)
+    near = [*given, grads, *vectors, final]
     return pl.pallas_call(
         body,
-        grid=(padded // tile,),
-        out_shape=[
-            jax.ShapeDtypeStruct((frames, width), BF16),
-            jax.ShapeDtypeStruct((frames, 1, width), F32),
-            *kept,
-            *vectors,
-        ],
-        in_specs=[row_tile, row_tile, whole(res.ovec.shape)] + [whole(a.shape) for a in passed],
-        out_specs=[
-            row_tile,
-            pl.BlockSpec((tile, 1, width), lambda i: (i, 0, 0)),
-            *[whole(a.shape) for a in kept + vectors],
-        ],
+        out_shape=[final, grads, *kept, *vectors],
+        in_specs=[pl.BlockSpec(memory_space=pl.ANY)] * len(given),
+        out_specs=[pl.BlockSpec(memory_space=pl.ANY)] * (2 + n + 9),
+        scratch_shapes=[pltpu.VMEM(a.shape, a.dtype) for a in near] + [pltpu.SemaphoreType.DMA((-(-padded // tile) * 2 + 2 * n + 12,))],
+        compiler_params=pltpu.CompilerParams(vmem_limit_bytes=67_043_328),
         name="finish",
-    )(res.ototal, res.igrad, res.ovec, *passed)
+    )(*given)
 
 
 def on_device(

time: 181 us -> 168 us (0.928)
  Pallas kernels: 180 us -> 167 us
    pallas_call x1, Pallas kernels: 175 us -> 163 us  [layer(): pl.pallas_call(body, out_shape=[jax.ShapeDtypeStruct(*v) for v in outs.va...]
    pallas_call x1, Pallas kernels: 5.53 us -> 3.71 us  [finish(): pl.pallas_call(body, out_shape=[final, grads, *kept, *vectors], in_specs=...]
where the time goes in v4:
time: 168 us
  Pallas kernels  167 us (99%)
    pallas_call x1, Pallas kernels, layer(): pl.pallas_call(body, out_shape=[jax.ShapeDtypeStruct(*v) for v in outs.va...  163 us
    pallas_call x1, Pallas kernels, finish(): pl.pallas_call(body, out_shape=[final, grads, *kept, *vectors], in_specs=...  3.71 us

profile of v4, /device:TPU:0, one launch (start us, length us, event | category | flops | bytes accessed | tf_op | source)
XLA Modules:
  0.0 167.9 jit_solution(6335539198228982280)
XLA Ops:
  0.7 163.4 %layer.1 = (bf16[768,768]{1,0:T(8,128)(2,1)}, f32[768,768]{1,0:T(8,128)}, f32[16,768]{1,0:T(8,128)}, f32[96,192]{1,0:T(8,128)}, f32[96,192]{1,0:T(8,128)}, /*ind...) custom-call(bf16[750,768]{1,0:T(8,128)(2,1)} %bitcast.21, ...), custom_call_target="tpu_custom_call" | custom-call | tf_op jit(solution)/shard_map/layer/pallas_call | solution.py:1058
  164.1 3.7 %finish.1 = (bf16[750,768]{1,0:T(8,128)(2,1)}, f32[750,1,768]{2,1,0:T(1,128)}, f32[96,192]{1,0:T(8,128)}, f32[96,192]{1,0:T(8,128)}, f32[96,192]{1,0:T(8,128)}, ...) custom-call(bf16[768,768]{1,0:T(8,128)(2,1)} %get-tuple-element.43.o, ...), custom_call_target="tpu_custom_call" | custom-call | tf_op jit(solution)/shard_map/finish/pallas_call | solution.py:1133

commit v5 on v4

--- a/solution.py
+++ b/solution.py
@@ -549,6 +549,12 @@
         def _():
             self.close(i - LAG)
 
+    def step(self, i, lag):
+        if i < self.chunks:
+            self.relay(i)
+        if i >= lag:
+            self.close(i - lag)
+
     def close(self, i):
         @pl.when(self.inner)
         def _():
@@ -591,6 +597,7 @@
 STEP = 128
 CHUNK = 32
 LAG = 4
+OUT_LAG = 3
 
 
 def stage_two(m, cube, nz, sum_two, sum_out):
@@ -695,6 +702,8 @@
     s1.start()
     loop(0, tiles, second)
     s2.start()
+    for h in range(nh):
+        m.qt[h] = m.q[h].T
     gain_two = m.vec[2:3, :]
 
     def middle(i):
@@ -736,22 +745,25 @@
     for part in range(4):
         loop(part * fourth, stop if part == 3 else (part + 1) * fourth, pumped)
         (s2, s1)[part % 2].step()
+    taken = []
+
+    def out_step():
+        if len(taken) < sum_out.chunks + OUT_LAG:
+            sum_out.step(len(taken), OUT_LAG)
+            taken.append(None)
+
+    out_step()
     loop(stop * each, chunks, middle)
-
-    loop(0, tiles, product(m.n2, lambda: m.at[...], m.dwo, local))
-    so.start()
+    out_step()
 
     for h in range(nh):
-        m.qt[h] = m.q[h].T
         m.dat[h] = m.act[:, h * 128 : (h + 1) * 128].T
     big = sum_out.chunks
-    sum_out.relay(0)
+    out_step()
     kv_sems = [sems.take() for _ in range(nh)]
     other = {"seq": flip(lax.axis_index("seq"), 1)}
     kv_copies = [remote(m.kvs.at[h], m.kvr.at[h], kv_sems[h], other) for h in range(nh)]
     for h in range(nh):
-        m.dkv[0, h] = fill((128, padded), 0)
-        m.dkv[1, h] = fill((128, padded), 0)
 
         def back(b, h=h):
             at = rows_of(b, BLOCK)
@@ -760,39 +772,27 @@
             for part in (1, 0):
                 keys = slice(part * padded, (part + 1) * padded)
                 dp = dot(da, m.kvt[part, h])
-                p = m.p[h, at, keys]
-                ds = (p.astype(F32) * (dp - inner)).astype(BF16)
-                m.ds[:, keys] = ds
-                m.dkv[part, h] += dot(m.qt[h, :, at], m.ds[:, keys]) + dot(m.dat[h, :, at], p)
-            dq = dot(m.ds[:, :padded], m.kv[0, h]) + dot(m.ds[:, padded:], m.kv[1, h])
+                m.ds[at, keys] = (m.p[h, at, keys].astype(F32) * (dp - inner)).astype(BF16)
+            dq = dot(m.ds[at, :padded], m.kv[0, h]) + dot(m.ds[at, padded:], m.kv[1, h])
             dq = (dq * scale)[:, :64].astype(BF16)
             m.gpre[at, nh * 128 + h * 64 : nh * 128 + (h + 1) * 64] = dq
-            point = h * blocks + b
-
-            for i, (when, done) in enumerate(((2, None), (5, 0), (8, 1))):
-
-                @pl.when(point == when)
-                def _(i=i, done=done):
-                    sum_out.relay(i + 1)
-                    if done is not None:
-                        sum_out.close(done)
 
         loop(0, blocks, back)
-        m.kvs[h] = m.dkv[1, h].astype(BF16)
+        out_step()
+        far, own = slice(padded, 2 * padded), slice(0, padded)
+        m.kvs[h] = (dot(m.qt[h], m.ds[:, far]) + dot(m.dat[h], m.p[h, :, far])).astype(BF16)
         kv_copies[h].start()
-        if h < nh - 1:
-            so.step()
+        m.dkv[h] = dot(m.qt[h], m.ds[:, own]) + dot(m.dat[h], m.p[h, :, own])
+        out_step()
     spare = packed - nh * 192
     if spare:
         m.gpre[:, nh * 192 : packed] = fill((padded, spare), 0, BF16)
     for h in range(nh):
-        if h == nh - 1:
-            sum_out.relay(4)
-            sum_out.close(2)
         kv_copies[h].wait_recv()
-        total = m.dkv[0, h] + m.kvr[h].astype(F32)
+        total = m.dkv[h] + m.kvr[h].astype(F32)
         m.gpre[:, h * 128 : (h + 1) * 128] = total.T.astype(BF16)
 
+    out_step()
     def last(b):
         at = rows_of(b, STEP)
         grads = m.gpre[at, :packed]
@@ -808,44 +808,57 @@
 
     loop(0, chunks, sum_two.drain)
     loop(0, padded // STEP, last)
+    out_step()
+    for row in range(8):
+        m.vs[row : row + 1, :] = jnp.sum(m.acc[row], axis=0, keepdims=True)
+    cube_peers = [cube.peer(step) for step in cube.orders[0]]
+    vec_copies = []
+
+    def vec_send(k):
+        if k < len(cube_peers):
+            m.vo_[k] = m.vs[...]
+            vec_copies.append(remote(m.vo_.at[k], m.vr.at[k], sems.take(), cube_peers[k]))
+            vec_copies[-1].start()
+            return
+        m.vo_[k] = m.vs[...]
+        for d in range(1, nz):
+            target = {"head": lax.rem(z + d, nz)}
+            vec_copies.append(remote(m.vo_.at[k], m.vr.at[k + d - 1], sems.take(), target))
+            vec_copies[-1].start()
+
+    def vec_take(k):
+        if k < len(cube_peers):
+            vec_copies[k].wait_recv()
+            m.vs[...] += m.vr[k]
+            vec_send(k + 1)
+
+    vec_send(0)
     one_q = product(m.n1, lambda: m.gpre[:, :packed], m.dwq, packed)
+    one_o = product(m.n2, lambda: m.at[...], m.dwo, local)
 
     def qkv(i):
         one_q(i)
         sum_one.pump(i)
 
-    sum_out.relay(5)
-    sum_out.close(3)
-    loop(0, tiles, qkv)
+    def out(i):
+        one_o(i)
+        sum_one.pump(tiles + i)
+
+    half = tiles // 2
+    loop(0, half, qkv)
+    out_step()
+    loop(half, tiles, qkv)
     sq.start()
-    sum_out.close(4)
-    sum_out.close(5)
-
-    for row in range(8):
-        m.vs[row : row + 1, :] = jnp.sum(m.acc[row], axis=0, keepdims=True)
-    vec_steps = [(cube.peer(step), False) for step in cube.orders[0]]
-    vec_steps += [({"head": flip(z, bit)}, True) for bit in powers(nz)]
-    row_id = lax.broadcasted_iota(jnp.int32, m.vs.shape, 0)
-    partial_rows = (row_id == GAIN_TWO) | (row_id == SHIFT_TWO) | (row_id == GAIN_ONE) | (row_id == SHIFT_ONE)
-    vec_copies = []
-
-    def vec_send(k):
-        if k < len(vec_steps):
-            m.vo_[k] = m.vs[...]
-            copy = remote(m.vo_.at[k], m.vr.at[k], sems.take(), vec_steps[k][0])
-            copy.start()
-            vec_copies.append(copy)
-
-    def vec_take(k):
-        if k < len(vec_steps):
-            vec_copies[k].wait_recv()
-            arrived = m.vr[k]
-            if vec_steps[k][1]:
-                arrived = jnp.where(partial_rows, arrived, 0.0)
-            m.vs[...] += arrived
-            vec_send(k + 1)
-
-    vec_send(0)
+    out_step()
+    vec_take(0)
+    loop(0, half, out)
+    out_step()
+    loop(half, tiles, out)
+    so.start()
+    while len(taken) < sum_out.chunks + OUT_LAG:
+        out_step()
+    vec_take(1)
+
     b_two = m.vec[5:6, :]
 
     def output(i):
@@ -864,9 +877,18 @@
         along = jnp.mean(e * xhat, axis=-1, keepdims=True)
         m.igrad[at] = m.xh2[at] + r * (e - mean - xhat * along)
 
+    ahead = 2 * tiles
+    stop = chunks + LAG - ahead
+    turn = 2 * stop - chunks
+
     def tail(i):
-        sum_one.pump(i + tiles)
+        sum_one.pump(i + ahead)
         final(i)
+
+    def faster(i):
+        sum_one.pump(i + ahead)
+        final(2 * i - turn)
+        final(2 * i - turn + 1)
 
     def unpack():
         got = sq.finish()
@@ -879,8 +901,13 @@
             m.save[name].start()
 
     def vectors():
-        for k in range(len(vec_steps) - 2, len(vec_steps)):
-            vec_take(k)
+        row_id = lax.broadcasted_iota(jnp.int32, m.vs.shape, 0)
+        summed = (row_id == GAIN_TWO) | (row_id == SHIFT_TWO) | (row_id == GAIN_ONE) | (row_id == SHIFT_ONE)
+        base = len(cube_peers)
+        for d in range(1, nz):
+            vec_copies[base + d - 1].wait_recv()
+        rest = sum(m.vr[base + d - 1] for d in range(1, nz))
+        m.vs[...] += jnp.where(summed, rest, 0.0)
         m.ovec[...] = fill(m.ovec.shape, 0)
         names = (GAIN_ONE, SHIFT_ONE, B_OUT, GAIN_TWO, SHIFT_TWO, B_FC_TWO)
         for b in range(cube.size):
@@ -906,23 +933,44 @@
         m.save["ow1"].start()
         m.ow2[...] = s2.finish()
         m.save["ow2"].start()
+
+    def first_job():
+        sq.step()
+
+    def second_job():
+        for k in range(2, len(cube_peers)):
+            vec_take(k)
+
+    def third_job():
+        sq.step()
+        so.step()
+
+    def sixth_job():
+        unpack()
         m.owo[...] = so.finish().T
         m.save["owo"].start()
 
-    def cubed():
-        for k in range(1, len(vec_steps) - 2):
-            vec_take(k)
-
-    vec_take(0)
-    stop = chunks + LAG - tiles
-    jobs = (early, sq.step, cubed, sq.step, outputs, unpack, vectors)
-    share = stop // len(jobs)
-    for part, job in enumerate(jobs):
-        loop(part * share, (part + 1) * share, tail)
-        job()
-    loop(len(jobs) * share, stop, tail)
-    loop(stop, chunks, final)
-    m.save["igrad"].start()
+    def fourth_job():
+        outputs()
+        so.step()
+
+    jobs = (first_job, second_job, third_job, fourth_job, early, sixth_job)
+    near = turn // 3
+    ends = [near, 2 * near, turn]
+    far = (stop - turn) // 4
+    ends += [turn + far, turn + 2 * far, turn + 3 * far, stop]
+    begin = 0
+    saved = 0
+    for place, end in enumerate(ends):
+        loop(begin, end, tail if end <= turn else faster)
+        begin = end
+        done = (end if end <= turn else 2 * end - turn) * CHUNK
+        m.save_rows(saved, done - saved).start()
+        saved = done
+        if place < len(jobs):
+            jobs[place]()
+    assert saved == padded
+    vectors()
 
     for copy in kv_copies + vec_copies:
         copy.wait_send()
@@ -943,7 +991,7 @@
     half = rows // colors
     packed = -(-(nh * 192) // 128) * 128
     nb = cube.size
-    steps = len(cube.all_bits) + len(powers(nz))
+    steps = len(cube.all_bits) + nz - 1
     token_names, bias_names = ("x", "cot"), ("bq", "bv", "bf1")
     weight_names = ("wq", "wk", "wv", "wo", "w1", "w2")
     share_names = tuple(f"share{i}" for i in range(len(shares)))
@@ -1003,10 +1051,10 @@
         at=((padded, local), BF16),
         qt=((nh, 128, padded), BF16),
         dat=((nh, 128, padded), BF16),
-        dkv=((2, nh, 128, padded), F32),
+        dkv=((nh, 128, padded), F32),
         kvs=((nh, 128, padded), BF16),
         kvr=((nh, 128, padded), BF16),
-        ds=((BLOCK, 2 * padded), BF16),
+        ds=((padded, 2 * padded), BF16),
         dw1=((width, hidden), BF16),
         dl1=((colors, nb - 1, half, hidden), BF16),
         dw2=((width, hidden), BF16),
@@ -1016,7 +1064,7 @@
         dwq=((width, packed), BF16),
         dlq=((colors, nb - 1, half, packed), BF16),
     )
-    small, large = padded // CHUNK, 6
+    small, large = padded // CHUNK, 12
     sums = 3 * small + 2 * large
     lines = sums + Line.count(nz, parts)
     count = lines + (9 * colors + 1) * (nb - 1) + (nz - 1) + 2 * nh + steps
@@ -1034,7 +1082,17 @@
         m.save = {
             name: pltpu.make_async_copy(getattr(m, name), far, move.at[len(ins) + i])
             for i, (name, far) in enumerate(zip(outs, far_out))
+            if name != "igrad"
         }
+        rows_far = far_out[list(outs).index("igrad")]
+
+        def save_rows(start, size):
+            part = pl.ds(start, size)
+            at = len(ins) + len(outs) + len(m.saved)
+            m.saved.append(pltpu.make_async_copy(m.igrad.at[part], rows_far.at[part], move.at[at]))
+            return m.saved[-1]
+
+        m.saved, m.save_rows = [], save_rows
         m.first_loads = share_names + ("wk", "wv", "wq")
         m.next_loads = ("wo", "w1", "w2", "x", *bias_names)
         for name in (*m.first_loads, *m.next_loads, "cot"):
@@ -1052,7 +1110,7 @@
         stage_two(m, cube, nz, sum_two, sum_out)
         stage_three(m, cube, nz, sems, sum_two, sum_out, sum_one)
         assert sems.used == count, (sems.used, count)
-        for copy in m.save.values():
+        for copy in (*m.save.values(), *m.saved):
             copy.wait()
 
     res = pl.pallas_call(
@@ -1063,7 +1121,7 @@
         scratch_shapes=[pltpu.VMEM(a.shape, a.dtype) for a in ins.values()]
         + [pltpu.VMEM(*v) for v in (outs | scratch).values()]
         + [pltpu.SemaphoreType.DMA((count,))] * 2
-        + [pltpu.SemaphoreType.DMA((len(ins) + len(outs),))],
+        + [pltpu.SemaphoreType.DMA((len(ins) + len(outs) + 7,))],
         compiler_params=pltpu.CompilerParams(
             collective_id=0, has_side_effects=True, vmem_limit_bytes=67_043_328
         ),

time: 168 us -> 159 us (0.946)
  Pallas kernels: 167 us -> 158 us
    pallas_call x1, Pallas kernels: 163 us -> 154 us  [layer(): pl.pallas_call(body, out_shape=[jax.ShapeDtypeStruct(*v) for v in outs.va...]
where the time goes in v5:
time: 159 us
  Pallas kernels  158 us (99%)
    pallas_call x1, Pallas kernels, layer(): pl.pallas_call(body, out_shape=[jax.ShapeDtypeStruct(*v) for v in outs.va...  154 us
    pallas_call x1, Pallas kernels, finish(): pl.pallas_call(body, out_shape=[final, grads, *kept, *vectors], in_specs=...  3.71 us

profile of v5, /device:TPU:0, one launch (start us, length us, event | category | flops | bytes accessed | tf_op | source)
XLA Modules:
  0.0 158.8 jit_solution(1413129479043980061)
XLA Ops:
  0.7 154.3 %layer.1 = (bf16[768,768]{1,0:T(8,128)(2,1)}, f32[768,768]{1,0:T(8,128)}, f32[16,768]{1,0:T(8,128)}, f32[96,192]{1,0:T(8,128)}, f32[96,192]{1,0:T(8,128)}, /*ind...) custom-call(bf16[750,768]{1,0:T(8,128)(2,1)} %bitcast.21, ...), custom_call_target="tpu_custom_call" | custom-call | tf_op jit(solution)/shard_map/layer/pallas_call | solution.py:1116
  155.0 3.7 %finish.1 = (bf16[750,768]{1,0:T(8,128)(2,1)}, f32[750,1,768]{2,1,0:T(1,128)}, f32[96,192]{1,0:T(8,128)}, f32[96,192]{1,0:T(8,128)}, f32[96,192]{1,0:T(8,128)}, ...) custom-call(bf16[768,768]{1,0:T(8,128)(2,1)} %get-tuple-element.43.o, ...), custom_call_target="tpu_custom_call" | custom-call | tf_op jit(solution)/shard_map/finish/pallas_call | solution.py:1191

commit v6 on v5

--- a/solution.py
+++ b/solution.py
@@ -132,7 +132,7 @@
 
 
 NEG = -1e30
-LINE_LAG = 3
+LINE_LAG = 2
 
 
 def fill(shape, value, dtype=F32):
@@ -358,6 +358,10 @@
 
     for h in range(nh):
         prepare(0, h)
+    m.load["cot"].wait()
+    m.gp[0:frames] = m.cot[...]
+    m.gp[frames:padded] = fill((padded - frames, width), 0, BF16)
+    m.acc[...] = fill(m.acc.shape, 0)
 
     block = 256
     valid = frames - (padded - 128)
@@ -425,13 +429,16 @@
             for c in range(colors):
                 g.advance(k, c)
 
-    for copy in kv_copies:
-        copy.wait_send()
-    for copy in out_copies(False):
-        copy.wait_send()
-    for g in (gv, gk, gq, g1, g2, go):
-        g.drain()
-    loop(0, line.parts, line.drain)
+    def drain():
+        for copy in kv_copies:
+            copy.wait_send()
+        for copy in out_copies(False):
+            copy.wait_send()
+        for g in (gv, gk, gq, g1, g2, go):
+            g.drain()
+        loop(0, line.parts, line.drain)
+
+    return drain
 
 
 class Scatter:
@@ -597,7 +604,7 @@
 STEP = 128
 CHUNK = 32
 LAG = 4
-OUT_LAG = 3
+OUT_LAG = 2
 
 
 def stage_two(m, cube, nz, sum_two, sum_out):
@@ -606,10 +613,6 @@
     nh = m.q.shape[0]
     frames = m.cot.shape[0]
     hidden = m.w1.shape[1]
-    m.load["cot"].wait()
-    m.gp[0:frames] = m.cot[...]
-    m.gp[frames:padded] = fill((padded - frames, width), 0, BF16)
-    m.acc[...] = fill(m.acc.shape, 0)
     gain, shift, b_out = m.vec[2:3, :], m.vec[3:4, :], m.vec[4:5, :]
     b_one = m.bf1[...].astype(F32)[None, :]
     per = STEP // CHUNK
@@ -643,10 +646,10 @@
         m.gpre[at] = gpre
         add_rows(m, B_FC_ONE, gpre.astype(F32))
         back = dot_nt(gpre, w_one())
+        m.part[at] = back.astype(BF16)
+        loop(0, per, lambda j: sum_two.offer(b * per + j))
         add_rows(m, GAIN_TWO, back * m.xh2[at])
         add_rows(m, SHIFT_TWO, back)
-        m.part[at] = back.astype(BF16)
-        loop(0, per, lambda j: sum_two.offer(b * per + j))
 
         @pl.when(b >= 2)
         def _():
@@ -659,7 +662,7 @@
     loop(0, sum_out.chunks, sum_out.offer)
 
 
-def stage_three(m, cube, nz, sems, sum_two, sum_out, sum_one):
+def stage_three(m, cube, nz, sems, sum_two, sum_out, sum_one, drain):
     z = lax.axis_index("head")
     padded, width = m.xp.shape
     rows = m.wq.shape[0]
@@ -740,19 +743,20 @@
         sum_two.pump(i + ahead)
         loop(i * each, (i + 1) * each, middle)
 
+    taken = []
+
+    def out_step():
+        if len(taken) < sum_out.chunks + OUT_LAG:
+            sum_out.step(len(taken), OUT_LAG)
+            taken.append(None)
+
     s1.step()
     fourth = stop // 4
     for part in range(4):
         loop(part * fourth, stop if part == 3 else (part + 1) * fourth, pumped)
         (s2, s1)[part % 2].step()
-    taken = []
-
-    def out_step():
-        if len(taken) < sum_out.chunks + OUT_LAG:
-            sum_out.step(len(taken), OUT_LAG)
-            taken.append(None)
-
-    out_step()
+        if part >= 2:
+            out_step()
     loop(stop * each, chunks, middle)
     out_step()
 
@@ -800,11 +804,11 @@
         keys = nh * 128
         back = dot_nt(grads[:, :keys], m.gk[...].reshape(cube.size * rows, keys))
         back = back + dot_nt(grads[:, keys:], m.gq[...].reshape(cube.size * rows, packed - keys))
+        m.part[at] = back.astype(BF16)
+        loop(0, per, lambda j: sum_one.offer(b * per + j))
         xhat, _ = normalize(m.xp[at].astype(F32))
         add_rows(m, GAIN_ONE, back * xhat)
         add_rows(m, SHIFT_ONE, back)
-        m.part[at] = back.astype(BF16)
-        loop(0, per, lambda j: sum_one.offer(b * per + j))
 
     loop(0, chunks, sum_two.drain)
     loop(0, padded // STEP, last)
@@ -942,6 +946,7 @@
             vec_take(k)
 
     def third_job():
+        drain()
         sq.step()
         so.step()
 
@@ -949,6 +954,8 @@
         unpack()
         m.owo[...] = so.finish().T
         m.save["owo"].start()
+        for scatter in (s1, s2, so, sq):
+            scatter.drain()
 
     def fourth_job():
         outputs()
@@ -974,8 +981,6 @@
 
     for copy in kv_copies + vec_copies:
         copy.wait_send()
-    for s in (s1, s2, so, sq):
-        s.drain()
     loop(0, chunks, sum_one.drain)
 
 
@@ -1106,9 +1111,9 @@
             nz, send, recv, 3 * small, 3 * small + large, large, padded // large, m.opart, m.olanded, m.ocrossed, m.ototal
         )
         line = Line(nz, send, recv, sums, lambda origin, part: m.attz.at[origin, part], parts)
-        stage_one(m, cube, nz, sems, line)
+        drain = stage_one(m, cube, nz, sems, line)
         stage_two(m, cube, nz, sum_two, sum_out)
-        stage_three(m, cube, nz, sems, sum_two, sum_out, sum_one)
+        stage_three(m, cube, nz, sems, sum_two, sum_out, sum_one, drain)
         assert sems.used == count, (sems.used, count)
         for copy in (*m.save.values(), *m.saved):
             copy.wait()

time: 159 us -> 157 us (0.987)
  Pallas kernels: 158 us -> 156 us
    pallas_call x1, Pallas kernels: 154 us -> 152 us  [layer(): pl.pallas_call(body, out_shape=[jax.ShapeDtypeStruct(*v) for v in outs.va...]
where the time goes in v6:
time: 157 us
  Pallas kernels  156 us (99%)
    pallas_call x1, Pallas kernels, layer(): pl.pallas_call(body, out_shape=[jax.ShapeDtypeStruct(*v) for v in outs.va...  152 us
    pallas_call x1, Pallas kernels, finish(): pl.pallas_call(body, out_shape=[final, grads, *kept, *vectors], in_specs=...  3.71 us

profile of v6, /device:TPU:0, one launch (start us, length us, event | category | flops | bytes accessed | tf_op | source)
XLA Modules:
  0.0 156.7 jit_solution(8559097913838814704)
XLA Ops:
  0.7 152.2 %layer.1 = (bf16[768,768]{1,0:T(8,128)(2,1)}, f32[768,768]{1,0:T(8,128)}, f32[16,768]{1,0:T(8,128)}, f32[96,192]{1,0:T(8,128)}, f32[96,192]{1,0:T(8,128)}, /*ind...) custom-call(bf16[750,768]{1,0:T(8,128)(2,1)} %bitcast.21, ...), custom_call_target="tpu_custom_call" | custom-call | tf_op jit(solution)/shard_map/layer/pallas_call | solution.py:1121
  152.9 3.7 %finish.1 = (bf16[750,768]{1,0:T(8,128)(2,1)}, f32[750,1,768]{2,1,0:T(1,128)}, f32[96,192]{1,0:T(8,128)}, f32[96,192]{1,0:T(8,128)}, f32[96,192]{1,0:T(8,128)}, ...) custom-call(bf16[768,768]{1,0:T(8,128)(2,1)} %get-tuple-element.43.o, ...), custom_call_target="tpu_custom_call" | custom-call | tf_op jit(solution)/shard_map/finish/pallas_call | solution.py:1196
